TPU v7x, 128 devices: a whole 4x4x4 slice. The times are simulated.
128 devices in a mesh: lat: 8 (over z, core), lon: 16 (over y, x).
Axes of the slice: x: 4, y: 4, z: 4, core: 2. Of those that a mesh axis runs over, the one named last changes fastest.
Arguments:
- tracers: float32 [16, 8, 128, 2048], P(None, None, 'lat', 'lon'), may hold values from -6 to 6
- winds: float32 [3, 8, 128, 2048], P(None, None, 'lat', 'lon'), may hold values from -4 to 4
- depart_first: int32 [3, 8, 128, 2048], P(None, None, 'lat', 'lon'), may hold values from -3 to 2, as said below
- depart_second: int32 [3, 8, 128, 2048], P(None, None, 'lat', 'lon'), may hold values from -2 to 1, as said below
- fluxes: bfloat16 [6144, 128, 256], P(('lat', 'lon')), may hold values from 0.049804688 to 5
- remap_weights: bfloat16 [6144, 4, 256, 128], P(('lat', 'lon')), may hold values from 0.00019931793 to 0.019897461
- target_device: int32 [6144, 4], P(('lat', 'lon')), may hold values from 0 to 127, all different within a row; in each aligned block of 48 rows (0 to 47, 48 to 95, ...) at most 2 rows name the same one
- target_block: int32 [6144, 4], P(('lat', 'lon')), may hold values from 0 to 15
Outputs:
- advected: float32 [16, 8, 128, 2048], P(None, None, 'lat', 'lon')
Inputs may be any that keep to these rules, and one draw needn't show every extreme that they name: `depart_first`: component 0 (levels) is -1 or 0; components 1 and 2 are row and column offsets. `depart_second`: component 0 (levels) is -1 or 0; components 1 and 2 are row and column offsets. `target_device`: device g is the one at lat index g // 16 and lon index g % 16. Each row names 4 different devices; among the rows of one device no device is named more than 2 times.
All inputs are finite; a program needn't handle non-finite values.
Results may differ from a plain program's by a relative error of at most 0.00088.
Values may be sent and summed in bfloat16 or wider, within the bound.
No kernel may reach another device: no remote copies, remote signals or barrier semaphores. Data moves between devices by JAX's collectives and lax.ppermute only.
A program may use at most 192 MiB of HBM per device.

v0:
```python
import jax
import jax.numpy as jnp
from jax import lax
from jax.sharding import PartitionSpec as P

NTR = 16
CAP = 2
BLK_DEV = 16
HMAX = 3


def padded_2(block, sides, width, periodic):
    for axis, dim in sides:
        count = lax.axis_size(axis)
        forward = [(i, i + 1) for i in range(count - 1)]
        if periodic:
            forward.append((count - 1, 0))
        backward = [(target, source) for source, target in forward]
        low = lax.ppermute(
            lax.slice_in_dim(block, block.shape[dim] - width, None, axis=dim), axis, forward
        )
        high = lax.ppermute(lax.slice_in_dim(block, 0, width, axis=dim), axis, backward)
        block = jnp.concatenate([low, block, high], axis=dim)
    return block


def in_blocks(value, dim, peers):
    dims = value.shape
    pieces = value.reshape(*dims[:dim], peers, dims[dim] // peers, *dims[dim + 1 :])
    return jnp.moveaxis(pieces, dim, 0)


def joined_along(pieces, dim):
    dims = list(pieces.shape[1:])
    dims[dim] *= pieces.shape[0]
    return jnp.moveaxis(pieces, 0, dim).reshape(dims)


def joined_exchange(value, axis, axes, splits, concats):
    sizes = [lax.axis_size(a) for a in axes]
    pieces = in_blocks(value, splits[0], sizes[0])
    pieces = jnp.moveaxis(in_blocks(pieces, splits[1] + 1, sizes[1]), 0, 1)
    inside = pieces.shape[2:]
    pieces = pieces.reshape(-1, *inside)
    pieces = lax.all_to_all(pieces, axis, split_axis=0, concat_axis=0, tiled=True)
    pieces = joined_along(pieces.reshape(*sizes, *inside), concats[0] + 1)
    return joined_along(pieces, concats[1])


def cubic_weights(frac):
    first = -frac * (frac - 1.0) * (frac - 2.0) / 6.0
    second = (frac + 1.0) * (frac - 1.0) * (frac - 2.0) / 2.0
    third = -(frac + 1.0) * frac * (frac - 2.0) / 2.0
    fourth = (frac + 1.0) * frac * (frac - 1.0) / 6.0
    return (first, second, third, fourth)


def offset_weights(offset, frac, reach):
    stencil = cubic_weights(frac)
    spread = []
    for target in range(-reach, reach + 1):
        weight = jnp.zeros(frac.shape, jnp.float32)
        for step in range(4):
            weight = weight + jnp.where(offset + step - 1 == target, stencil[step], 0.0)
        spread.append(weight)
    return spread


def tricubic(padded, depart, frac, margin):
    chans, levels, rows_wide, cols_wide = padded.shape
    rows = rows_wide - 2 * margin
    cols = cols_wide - 2 * margin
    lowest = padded[:, :1]
    highest = padded[:, -1:]
    stacked = jnp.concatenate([lowest, lowest, padded, highest, highest], axis=1)
    level_w = offset_weights(depart[0], frac[0], 2)
    row_w = offset_weights(depart[1], frac[1], margin)
    col_w = offset_weights(depart[2], frac[2], margin)
    total = jnp.zeros((chans, levels, rows, cols), jnp.float32)
    for above in range(5):
        for across in range(2 * margin + 1):
            inner = jnp.zeros((chans, levels, rows, cols), jnp.float32)
            for sideways in range(2 * margin + 1):
                piece = stacked[
                    :, above : above + levels, across : across + rows, sideways : sideways + cols
                ]
                inner = inner + col_w[sideways][None] * piece
            total = total + (level_w[above] * row_w[across])[None] * inner
    return total


def body(
    tracers, winds, depart_first, depart_second, fluxes, remap_weights, target_device, target_block
):
    wide = HMAX + 1
    narrow = max((HMAX + 1) // 2 + 1, HMAX // 2 + 2)
    wind_side = padded_2(winds, (("lon", 3),), wide, True)
    wind_wide = padded_2(wind_side, (("lat", 2),), wide, False)
    tracer_side = padded_2(tracers, (("lon", 3),), narrow, True)
    tracer_wide = padded_2(tracer_side, (("lat", 2),), narrow, False)
    shape = winds.shape[1:]
    frac_first = jnp.clip(-winds - depart_first.astype(jnp.float32), 0.0, 1.0)
    midwind = tricubic(wind_wide, depart_first, frac_first, wide)
    frac_second = jnp.clip(-(winds + midwind) * 0.5 - depart_second.astype(jnp.float32), 0.0, 1.0)
    moved = tricubic(tracer_wide, depart_second, frac_second, narrow)
    tiles, links = target_device.shape
    rows_count, block_cols = (fluxes.shape[1], remap_weights.shape[3])
    items = tiles * links
    remapped = jnp.einsum(
        "trc,tkcb->tkrb", fluxes, remap_weights, preferred_element_type=jnp.float32
    )
    remapped = remapped.astype(jnp.bfloat16).reshape(items, rows_count, block_cols)
    lat_count = lax.axis_size("lat")
    lon_count = lax.axis_size("lon")
    devices = lat_count * lon_count
    slot_count = devices * CAP
    owners = target_device.reshape(items)
    item_iota = lax.broadcasted_iota(jnp.int32, (items, items), 1)
    item_rows = lax.broadcasted_iota(jnp.int32, (items, items), 0)
    earlier = jnp.logical_and(owners[:, None] == owners[None, :], item_iota < item_rows)
    rank = jnp.sum(earlier.astype(jnp.int32), axis=1)
    slot = owners * CAP + rank
    slot_iota = lax.broadcasted_iota(jnp.int32, (slot_count, items), 0)
    hit = slot[None, :] == slot_iota
    present = jnp.any(hit, axis=1)
    source_item = jnp.sum(
        jnp.where(hit, lax.broadcasted_iota(jnp.int32, (slot_count, items), 1), 0), axis=1
    )
    outgoing = jnp.take(remapped, source_item, axis=0)
    outgoing = jnp.where(present[:, None, None], outgoing, jnp.zeros_like(outgoing))
    labels = jnp.where(present, jnp.take(target_block.reshape(items), source_item), -1)
    data = outgoing.reshape(lat_count, lon_count, CAP, rows_count, block_cols)
    marks = labels.reshape(lat_count, lon_count, CAP)
    arrived, arrived_labels = (
        joined_exchange(data, ("lat", "lon"), ("lat", "lon"), (0, 1), (0, 1)),
        joined_exchange(marks, ("lat", "lon"), ("lat", "lon"), (0, 1), (0, 1)),
    )
    arrived_flat = arrived.reshape(slot_count, rows_count * block_cols)
    block_iota = lax.broadcasted_iota(jnp.int32, (BLK_DEV, slot_count), 0)
    selector = (arrived_labels.reshape(1, slot_count) == block_iota).astype(jnp.bfloat16)
    blocks = jnp.dot(selector, arrived_flat, preferred_element_type=jnp.float32)
    levels, lat_rows, lon_cols = shape
    grid = blocks.reshape(BLK_DEV, NTR, levels, block_cols).transpose(1, 2, 0, 3)
    return moved + grid


def solution(mesh):
    in_specs = (
        P(None, None, "lat", "lon"),
        P(None, None, "lat", "lon"),
        P(None, None, "lat", "lon"),
        P(None, None, "lat", "lon"),
        P(("lat", "lon"), None, None),
        P(("lat", "lon"), None, None, None),
        P(("lat", "lon"), None),
        P(("lat", "lon"), None),
    )
    out_specs = P(None, None, "lat", "lon")
    return jax.shard_map(body, mesh=mesh, in_specs=in_specs, out_specs=out_specs, check_vma=False)
```

profile of v0, /device:TPU:95, one launch (start us, length us, event | category | flops | bytes accessed | tf_op | source)
XLA Modules:
  0.0 536.2 jit_solution(1462676854617276079)
XLA Ops:
  0.0 3.4 fusion.797
  3.4 2.7 copy.44
  6.7 2.7 copy.43
  9.4 4.2 collective-permute-start.4
  14.5 4.8 collective-permute-start
  24.3 1.9 gather_fusion
  28.5 11.3 %all-to-all-start = ((s32[128,1,1,2]{3,2,1,0:T(1,128)}), s32[128,1,1,2]{3,2,1,0:T(1,128)}, u32[]{:S(2)}, u32[]{:S(2)}) async-start(s32[128,1,1,2]{3,2,1,0:T(1,128)} %bitcast.251), calls=%async_computation | async-start | bytes 131072 | tf_op jit(solution)/shard_map/all_to_all | solution.py:45
  41.9 8.3 %convolution_convert_fusion = bf16[48,4,128,128]{3,2,1,0:T(8,128)(2,1)} fusion(bf16[48,4,256,128]{3,2,1,0:T(8,128)(2,1)} %param.13, bf16[48,128,256]{2,1,0:T(8,128)(2,1)S(1)} %copy-done), kind=kOutput, calls=%fused_computation.8 | convolution fusion | flops 1613758464 | bytes 22020096 | tf_op jit(solution)/shard_map/trc,tkcb->tkrb/dot_general | solution.py:109
  50.2 11.5 %gather_fusion.1 = bf16[256,128,128]{1,2,0:T(8,128)(2,1)} fusion(bf16[192,128,128]{1,2,0:T(8,128)(2,1)} %bitcast.247, s32[1024]{0:T(1024)S(1)} %pad_clamp_fusion), kind=kCustom, calls=%fused_computation.1 | custom fusion | bytes 16778240 | tf_op jit(solution)/shard_map/jit(_take)/gather | solution.py:129
  61.7 12.0 %copy.38 = bf16[256,128,128]{2,1,0:T(8,128)(2,1)} copy(bf16[256,128,128]{1,2,0:T(8,128)(2,1)} %gather_fusion.1) | data formatting | bytes 16777216 | tf_op jit(solution)/shard_map/jit(_take)/gather | solution.py:129
  77.7 7.5 %select_select_fusion = bf16[128,1,1,2,128,128]{5,4,3,2,1,0:T(8,128)(2,1)} fusion(bf16[128,1,1,2,128,128]{5,4,3,2,1,0:T(8,128)(2,1)} %bitcast.248, pred[128,2]{1,0:T(8,128)(4,1)S(1)} %compare_and_fusion, pred[128,2]{1,0:T(8,128)(4,1)S(1)} %copy-done.70), kind=kLoop, calls=%fused_computation.3 | loop fusion | flops 8388608 | bytes 16777728 | tf_op jit(solution)/shard_map/jit(_where)/select_n | solution.py:130
  87.4 10.2 %all-to-all-start.1 = ((bf16[128,1,1,2,128,128]{5,4,3,2,1,0:T(8,128)(2,1)}), bf16[128,1,1,2,128,128]{5,4,3,2,1,0:T(8,128)(2,1)}, u32[]{:S(2)}, u32[]{:S(2)}) async-start(bf16[128,1,1,2,128,128]{5,4,3,2,1,0:T(8,128)(2,1)} %select_select_fusion), calls=%async_computation.1 | async-start | bytes 16777216 | tf_op jit(solution)/shard_map/all_to_all | solution.py:45
  98.7 1.8 pad_maximum_fusion.19
  100.5 2.3 collective-permute-start.3
  102.8 3.3 collective-permute-start.2
  106.1 1.7 copy.31
  107.9 2.0 copy.30
  109.9 1.8 pad_maximum_fusion.10
  111.8 1.9 collective-permute-start.7
  113.7 3.6 collective-permute-start.6
  117.3 73.7 %collective-permute-done.3 = f32[3,8,4,136]{3,2,1,0:T(4,128)} collective-permute-done((f32[3,8,4,136]{3,2,1,0:T(4,128)}, f32[3,8,4,136]{3,2,1,0:T(4,128)}, u32[]{:S(2)}, u32[]{:S(2)}) %collective-permute-start.3) | collective-permute-done | bytes 52256 | tf_op jit(solution)/shard_map/ppermute | solution.py:22
  191.0 1.6 pad_maximum_fusion.7
  199.3 1.8 maximum_maximum_fusion.3
  201.1 1.6 fusion.735
  202.8 1.9 maximum_maximum_fusion.4
  221.7 10.9 %fusion.535 = f32[3,8,16,128]{3,2,1,0:T(8,128)} fusion(f32[3,8,16,128]{3,2,1,0:T(8,128)} %mul.6969, f32[3,8,16,128]{3,2,1,0:T(8,128)S(1)} %mul.6704, f32[3,8,20,136]{3,2,1,0:T(8,128)S(1)} %get-tuple-element.72, f32[3,8,16,128]{3,2,1,0:T(8,128)S(1)} %mul.6701, f32[3,8,16,128]{3,2,1,0:T(8,128)S(1)} %mul.6698, f32[3,8,16,128]{3,2,1,0:T(8,128)S(1)} %mul.6695, ...), kind=kLoop, calls=%fused_computation.1020 | loop fusion | flops 18677760 | bytes 41484288 | tf_op jit(solution)/shard_map/add | solution.py:88
  232.8 1.7 mul.7268
  234.5 1.5 mul.7255
  236.1 1.5 mul.7242
  239.1 1.5 mul.7216
  240.7 1.5 mul.7203
  242.2 1.5 mul.7190
  243.7 1.5 mul.7177
  245.3 1.6 mul.7164
  246.8 1.5 mul.7151
  248.4 1.5 mul.7138
  249.9 1.5 mul.6982
  252.9 1.5 mul.7112
  254.5 1.5 mul.7099
  263.8 10.5 %fusion.326 = f32[3,8,16,128]{3,2,1,0:T(8,128)S(1)} fusion(f32[3,8,16,128]{3,2,1,0:T(8,128)} %max.8, f32[3,8,16,128]{3,2,1,0:T(8,128)} %min.12, f32[3,8,16,128]{3,2,1,0:T(8,128)} %convert_element_type.17, f32[3,8,16,128]{3,2,1,0:T(8,128)} %mul.7279, f32[3,8,16,128]{3,2,1,0:T(8,128)S(1)} %copy-done.9, f32[3,8,16,128]{3,2,1,0:T(8,128)} %mul.7268, ...), kind=kLoop, calls=%fused_computation.608 | loop fusion | flops 19365888 | bytes 43653120 | tf_op jit(solution)/shard_map/jit(clip)/min | solution.py:104
  278.9 4.2 maximum_maximum_fusion.2
  283.1 4.5 maximum_maximum_fusion.1
  287.6 2.5 fusion.209
  290.1 4.7 maximum_maximum_fusion
  294.8 33.6 %fusion.214 = f32[16,8,16,128]{3,2,1,0:T(8,128)} fusion(f32[16,9,22,134]{3,2,1,0:T(8,128)} %copy-done.2, f32[16,10,22,134]{3,2,1,0:T(8,128)S(1)} %get-tuple-element.53, f32[8,16,128]{2,1,0:T(8,128)} %get-tuple-element.151, f32[8,16,128]{2,1,0:T(8,128)S(1)} %copy-done.69, f32[8,16,128]{2,1,0:T(8,128)} %get-tuple-element.144, ...), kind=kLoop, calls=%fused_computation.405 | loop fusion | flops 39059456 | bytes 75563008 | tf_op jit(solution)/shard_map/add | solution.py:88
  328.5 23.2 %copy.47 = bf16[32,8,128,128]{3,1,2,0:T(8,128)(2,1)} copy(bf16[32,8,128,128]{3,2,1,0:T(8,128)(2,1)} %bitcast.130) | data formatting | bytes 16777216
  351.7 11.9 %copy.39 = bf16[16384,256]{1,0:T(8,128)(2,1)} copy(bf16[16384,256]{0,1:T(8,128)(2,1)} %bitcast.249) | data formatting | bytes 16777216 | tf_op jit(solution)/shard_map/dot_general | solution.py:141
  363.6 172.4 %fusion.1 = f32[16,8,16,128]{3,2,1,0:T(8,128)} fusion(bf16[16,8,128,256]{3,2,1,0:T(8,128)(2,1)} %bitcast.250, f32[16,8,16,128]{3,2,1,0:T(8,128)} %param.8, f32[16,8,16,3]{3,2,1,0:T(8,128)} %copy-done.5, f32[16,8,16,128]{3,2,1,0:T(8,128)} %get-tuple-element.139, f32[16,8,16,3]{3,2,1,0:T(8,128)} %copy-done.7, f32[16,10,22,134]{3,2,1,0:T(8,128)} %get-tuple-element.54, ...), kind=kOutput, calls=%fused_computation.21 | convolution fusion | flops 232263680 | bytes 187745280 | tf_op jit(solution)/shard_map/dot_general | solution.py:141
  (238 shorter events, 56.9 us)
Async XLA Ops:
  0.0 41.9 %copy-start = (bf16[48,128,256]{2,1,0:T(8,128)(2,1)S(1)}, bf16[48,128,256]{2,1,0:T(8,128)(2,1)}, u32[]{:S(2)}) copy-start(bf16[48,128,256]{2,1,0:T(8,128)(2,1)} %param.12) | copy-start | bytes 9437188
  0.0 19.2 %copy-start.72 = (s32[48,4]{0,1:T(4,128)S(1)}, s32[48,4]{0,1:T(4,128)}, u32[]{:S(2)}) copy-start(s32[48,4]{0,1:T(4,128)} %param.14) | copy-start | bytes 2308
  0.0 22.7 %copy-start.73 = (s32[48,4]{0,1:T(4,128)S(1)}, s32[48,4]{0,1:T(4,128)}, u32[]{:S(2)}) copy-start(s32[48,4]{0,1:T(4,128)} %param.15) | copy-start | bytes 2308
  6.1 100.0 %collective-permute-start.5 = (f32[16,8,16,3]{2,1,3,0:T(8,128)}, f32[16,8,16,3]{2,1,3,0:T(8,128)}, u32[]{:S(2)}, u32[]{:S(2)}) collective-permute-start(f32[16,8,16,3]{2,1,3,0:T(8,128)} %copy.44), channel_id=1, source_target_pairs={{1,0},{2,1},{3,2},{4,3},{5,4},{6,5},{7,6},{8,7},{9,8},{10,9},{11,1... | collective-permute-start | bytes 73736 | tf_op jit(solution)/shard_map/ppermute | solution.py:22
  9.4 98.5 %collective-permute-start.4 = (f32[16,8,16,3]{2,1,3,0:T(8,128)}, f32[16,8,16,3]{2,1,3,0:T(8,128)}, u32[]{:S(2)}, u32[]{:S(2)}) collective-permute-start(f32[16,8,16,3]{2,1,3,0:T(8,128)} %copy.43), channel_id=1, source_target_pairs={{0,1},{1,2},{2,3},{3,4},{4,5},{5,6},{6,7},{7,8},{8,9},{9,10},{10,1... | collective-permute-start | bytes 73736 | tf_op jit(solution)/shard_map/ppermute | solution.py:19
  14.4 84.2 %collective-permute-start.1 = (f32[3,8,16,4]{3,2,1,0:T(8,128)}, f32[3,8,16,4]{3,2,1,0:T(8,128)}, u32[]{:S(2)}, u32[]{:S(2)}) collective-permute-start(f32[3,8,16,4]{3,2,1,0:T(8,128)} %get-tuple-element.135), channel_id=1, source_target_pairs={{1,0},{2,1},{3,2},{4,3},{5,4},{6,5},{7,6},{8,7},{9,8},{10,9},{11,1... | collective-permute-start | bytes 18440 | tf_op jit(solution)/shard_map/ppermute | solution.py:22
  14.5 84.2 %collective-permute-start = (f32[3,8,16,4]{3,2,1,0:T(8,128)}, f32[3,8,16,4]{3,2,1,0:T(8,128)S(1)}, u32[]{:S(2)}, u32[]{:S(2)}) collective-permute-start(f32[3,8,16,4]{3,2,1,0:T(8,128)} %get-tuple-element.134), channel_id=1, source_target_pairs={{0,1},{1,2},{2,3},{3,4},{4,5},{5,6},{6,7},{7,8},{8,9},{9,10},{10,1... | collective-permute-start | bytes 18440 | tf_op jit(solution)/shard_map/ppermute | solution.py:19
  28.5 58.9 %all-to-all-start = ((s32[128,1,1,2]{3,2,1,0:T(1,128)}), s32[128,1,1,2]{3,2,1,0:T(1,128)}, u32[]{:S(2)}, u32[]{:S(2)}) async-start(s32[128,1,1,2]{3,2,1,0:T(1,128)} %bitcast.251), calls=%async_computation | async-start | bytes 131072 | tf_op jit(solution)/shard_map/all_to_all | solution.py:45
  87.4 241.1 %all-to-all-start.1 = ((bf16[128,1,1,2,128,128]{5,4,3,2,1,0:T(8,128)(2,1)}), bf16[128,1,1,2,128,128]{5,4,3,2,1,0:T(8,128)(2,1)}, u32[]{:S(2)}, u32[]{:S(2)}) async-start(bf16[128,1,1,2,128,128]{5,4,3,2,1,0:T(8,128)(2,1)} %select_select_fusion), calls=%async_computation.1 | async-start | bytes 16777216 | tf_op jit(solution)/shard_map/all_to_all | solution.py:45
  100.5 90.5 %collective-permute-start.3 = (f32[3,8,4,136]{3,2,1,0:T(4,128)}, f32[3,8,4,136]{3,2,1,0:T(4,128)}, u32[]{:S(2)}, u32[]{:S(2)}) collective-permute-start(f32[3,8,4,136]{3,2,1,0:T(4,128)} %get-tuple-element.74), channel_id=1, source_target_pairs={{16,0},{32,16},{48,32},{64,48},{80,64},{96,80},{112,96},{17,1},{33... | collective-permute-start | bytes 156680 | tf_op jit(solution)/shard_map/ppermute | solution.py:22
  102.8 88.2 %collective-permute-start.2 = (f32[3,8,4,136]{3,2,1,0:T(4,128)}, f32[3,8,4,136]{3,2,1,0:T(4,128)}, u32[]{:S(2)}, u32[]{:S(2)}) collective-permute-start(f32[3,8,4,136]{3,2,1,0:T(4,128)} %get-tuple-element.73), channel_id=1, source_target_pairs={{0,16},{16,32},{32,48},{48,64},{64,80},{80,96},{96,112},{1,17},{17... | collective-permute-start | bytes 156680 | tf_op jit(solution)/shard_map/ppermute | solution.py:19
  107.9 83.2 %copy-start.5 = (f32[16,8,16,3]{3,2,1,0:T(8,128)}, f32[16,8,16,3]{3,2,1,0:T(8,128)S(1)}, u32[]{:S(2)}) copy-start(f32[16,8,16,3]{3,2,1,0:T(8,128)S(1)} %copy.31) | copy-start | bytes 73732
  109.8 81.2 %copy-start.7 = (f32[16,8,16,3]{3,2,1,0:T(8,128)}, f32[16,8,16,3]{3,2,1,0:T(8,128)S(1)}, u32[]{:S(2)}) copy-start(f32[16,8,16,3]{3,2,1,0:T(8,128)S(1)} %copy.30) | copy-start | bytes 73732
  109.8 82.8 %copy-start.12 = (f32[8,16,128]{2,1,0:T(8,128)S(1)}, f32[8,16,128]{2,1,0:T(8,128)}, u32[]{:S(2)}) copy-start(f32[8,16,128]{2,1,0:T(8,128)} %get-tuple-element.117) | copy-start | bytes 196612
  109.8 82.8 %copy-start.13 = (f32[8,16,128]{2,1,0:T(8,128)S(1)}, f32[8,16,128]{2,1,0:T(8,128)}, u32[]{:S(2)}) copy-start(f32[8,16,128]{2,1,0:T(8,128)} %get-tuple-element.118) | copy-start | bytes 196612
  109.9 82.8 %copy-start.14 = (f32[8,16,128]{2,1,0:T(8,128)S(1)}, f32[8,16,128]{2,1,0:T(8,128)}, u32[]{:S(2)}) copy-start(f32[8,16,128]{2,1,0:T(8,128)} %get-tuple-element.119) | copy-start | bytes 196612
  109.9 82.8 %copy-start.16 = (f32[8,16,128]{2,1,0:T(8,128)S(1)}, f32[8,16,128]{2,1,0:T(8,128)}, u32[]{:S(2)}) copy-start(f32[8,16,128]{2,1,0:T(8,128)} %get-tuple-element.124) | copy-start | bytes 196612
  109.9 82.8 %copy-start.17 = (f32[8,16,128]{2,1,0:T(8,128)S(1)}, f32[8,16,128]{2,1,0:T(8,128)}, u32[]{:S(2)}) copy-start(f32[8,16,128]{2,1,0:T(8,128)} %get-tuple-element.113) | copy-start | bytes 196612
  109.9 82.8 %copy-start.18 = (f32[8,16,128]{2,1,0:T(8,128)S(1)}, f32[8,16,128]{2,1,0:T(8,128)}, u32[]{:S(2)}) copy-start(f32[8,16,128]{2,1,0:T(8,128)} %get-tuple-element.114) | copy-start | bytes 196612
  109.9 82.8 %copy-start.19 = (f32[8,16,128]{2,1,0:T(8,128)S(1)}, f32[8,16,128]{2,1,0:T(8,128)}, u32[]{:S(2)}) copy-start(f32[8,16,128]{2,1,0:T(8,128)} %get-tuple-element.115) | copy-start | bytes 196612
  109.9 82.8 %copy-start.20 = (f32[8,16,128]{2,1,0:T(8,128)S(1)}, f32[8,16,128]{2,1,0:T(8,128)}, u32[]{:S(2)}) copy-start(f32[8,16,128]{2,1,0:T(8,128)} %get-tuple-element.116) | copy-start | bytes 196612
  111.8 166.7 %collective-permute-start.7 = (f32[16,8,3,134]{3,2,1,0:T(4,128)}, f32[16,8,3,134]{3,2,1,0:T(4,128)S(1)}, u32[]{:S(2)}, u32[]{:S(2)}) collective-permute-start(f32[16,8,3,134]{3,2,1,0:T(4,128)} %get-tuple-element.62), channel_id=1, source_target_pairs={{16,0},{32,16},{48,32},{64,48},{80,64},{96,80},{112,96},{17,1},{33... | collective-permute-start | bytes 617480 | tf_op jit(solution)/shard_map/ppermute | solution.py:22
  113.7 164.8 %collective-permute-start.6 = (f32[16,8,3,134]{3,2,1,0:T(4,128)}, f32[16,8,3,134]{3,2,1,0:T(4,128)S(1)}, u32[]{:S(2)}, u32[]{:S(2)}) collective-permute-start(f32[16,8,3,134]{3,2,1,0:T(4,128)} %get-tuple-element.61), channel_id=1, source_target_pairs={{0,16},{16,32},{32,48},{48,64},{64,80},{80,96},{96,112},{1,17},{17... | collective-permute-start | bytes 617480 | tf_op jit(solution)/shard_map/ppermute | solution.py:19
  202.8 15.4 %copy-start.50 = (f32[8,16,128]{2,1,0:T(8,128)S(1)}, f32[8,16,128]{2,1,0:T(8,128)}, u32[]{:S(2)}) copy-start(f32[8,16,128]{2,1,0:T(8,128)} %get-tuple-element.190) | copy-start | bytes 196612
  202.8 16.1 %copy-start.49 = (f32[8,16,128]{2,1,0:T(8,128)S(1)}, f32[8,16,128]{2,1,0:T(8,128)}, u32[]{:S(2)}) copy-start(f32[8,16,128]{2,1,0:T(8,128)} %get-tuple-element.169) | copy-start | bytes 196612
  204.7 15.6 %copy-start.47 = (f32[8,16,128]{2,1,0:T(8,128)S(1)}, f32[8,16,128]{2,1,0:T(8,128)}, u32[]{:S(2)}) copy-start(f32[8,16,128]{2,1,0:T(8,128)} %get-tuple-element.187) | copy-start | bytes 196612
  204.7 16.3 %copy-start.66 = (f32[8,16,128]{2,1,0:T(8,128)S(1)}, f32[8,16,128]{2,1,0:T(8,128)}, u32[]{:S(2)}) copy-start(f32[8,16,128]{2,1,0:T(8,128)} %get-tuple-element.47) | copy-start | bytes 196612
  204.8 27.8 %copy-start.23 = (f32[3,8,16,128]{3,2,1,0:T(8,128)}, f32[3,8,16,128]{3,2,1,0:T(8,128)S(1)}, u32[]{:S(2)}) copy-start(f32[3,8,16,128]{3,2,1,0:T(8,128)S(1)} %mul.6695) | copy-start | bytes 589828
  204.8 27.8 %copy-start.25 = (f32[3,8,16,128]{3,2,1,0:T(8,128)}, f32[3,8,16,128]{3,2,1,0:T(8,128)S(1)}, u32[]{:S(2)}) copy-start(f32[3,8,16,128]{3,2,1,0:T(8,128)S(1)} %mul.6692) | copy-start | bytes 589828
  232.6 23.4 %copy-start.45 = (f32[8,16,128]{2,1,0:T(8,128)S(1)}, f32[8,16,128]{2,1,0:T(8,128)}, u32[]{:S(2)}) copy-start(f32[8,16,128]{2,1,0:T(8,128)} %get-tuple-element.91) | copy-start | bytes 196612
  232.7 24.1 %copy-start.44 = (f32[8,16,128]{2,1,0:T(8,128)S(1)}, f32[8,16,128]{2,1,0:T(8,128)}, u32[]{:S(2)}) copy-start(f32[8,16,128]{2,1,0:T(8,128)} %get-tuple-element.93) | copy-start | bytes 196612
  232.7 24.8 %copy-start.43 = (f32[8,16,128]{2,1,0:T(8,128)S(1)}, f32[8,16,128]{2,1,0:T(8,128)}, u32[]{:S(2)}) copy-start(f32[8,16,128]{2,1,0:T(8,128)} %get-tuple-element.39) | copy-start | bytes 196612
  232.7 25.5 %copy-start.39 = (f32[8,16,128]{2,1,0:T(8,128)S(1)}, f32[8,16,128]{2,1,0:T(8,128)}, u32[]{:S(2)}) copy-start(f32[8,16,128]{2,1,0:T(8,128)} %get-tuple-element.36) | copy-start | bytes 196612
  232.7 26.2 %copy-start.42 = (f32[8,16,128]{2,1,0:T(8,128)S(1)}, f32[8,16,128]{2,1,0:T(8,128)}, u32[]{:S(2)}) copy-start(f32[8,16,128]{2,1,0:T(8,128)} %get-tuple-element.125) | copy-start | bytes 196612
  232.7 26.9 %copy-start.41 = (f32[8,16,128]{2,1,0:T(8,128)S(1)}, f32[8,16,128]{2,1,0:T(8,128)}, u32[]{:S(2)}) copy-start(f32[8,16,128]{2,1,0:T(8,128)} %get-tuple-element.127) | copy-start | bytes 196612
  232.7 27.6 %copy-start.40 = (f32[8,16,128]{2,1,0:T(8,128)S(1)}, f32[8,16,128]{2,1,0:T(8,128)}, u32[]{:S(2)}) copy-start(f32[8,16,128]{2,1,0:T(8,128)} %get-tuple-element.129) | copy-start | bytes 196612
  232.7 28.3 %copy-start.64 = (f32[8,16,128]{2,1,0:T(8,128)S(1)}, f32[8,16,128]{2,1,0:T(8,128)}, u32[]{:S(2)}) copy-start(f32[8,16,128]{2,1,0:T(8,128)} %get-tuple-element.121) | copy-start | bytes 196612
  232.7 31.0 %copy-start.27 = (f32[3,8,16,128]{3,2,1,0:T(8,128)S(1)}, f32[3,8,16,128]{3,2,1,0:T(8,128)}, u32[]{:S(2)}) copy-start(f32[3,8,16,128]{3,2,1,0:T(8,128)} %mul.6689) | copy-start | bytes 589828
  232.7 31.0 %copy-start.28 = (f32[3,8,16,128]{3,2,1,0:T(8,128)S(1)}, f32[3,8,16,128]{3,2,1,0:T(8,128)}, u32[]{:S(2)}) copy-start(f32[3,8,16,128]{3,2,1,0:T(8,128)} %mul.6686) | copy-start | bytes 589828
  232.7 31.0 %copy-start.29 = (f32[3,8,16,128]{3,2,1,0:T(8,128)S(1)}, f32[3,8,16,128]{3,2,1,0:T(8,128)}, u32[]{:S(2)}) copy-start(f32[3,8,16,128]{3,2,1,0:T(8,128)} %mul.6683) | copy-start | bytes 589828
  232.8 31.0 %copy-start.30 = (f32[3,8,16,128]{3,2,1,0:T(8,128)S(1)}, f32[3,8,16,128]{3,2,1,0:T(8,128)}, u32[]{:S(2)}) copy-start(f32[3,8,16,128]{3,2,1,0:T(8,128)} %mul.6680) | copy-start | bytes 589828
  232.8 31.0 %copy-start.32 = (f32[3,8,16,128]{3,2,1,0:T(8,128)S(1)}, f32[3,8,16,128]{3,2,1,0:T(8,128)}, u32[]{:S(2)}) copy-start(f32[3,8,16,128]{3,2,1,0:T(8,128)} %fusion.535) | copy-start | bytes 589828
  232.8 31.0 %copy-start.33 = (f32[3,8,16,128]{3,2,1,0:T(8,128)S(1)}, f32[3,8,16,128]{3,2,1,0:T(8,128)}, u32[]{:S(2)}) copy-start(f32[3,8,16,128]{3,2,1,0:T(8,128)} %fusion.507) | copy-start | bytes 589828
  232.8 31.0 %copy-start.34 = (f32[3,8,16,128]{3,2,1,0:T(8,128)S(1)}, f32[3,8,16,128]{3,2,1,0:T(8,128)}, u32[]{:S(2)}) copy-start(f32[3,8,16,128]{3,2,1,0:T(8,128)} %fusion.516) | copy-start | bytes 589828
  232.8 31.0 %copy-start.35 = (f32[3,8,16,128]{3,2,1,0:T(8,128)S(1)}, f32[3,8,16,128]{3,2,1,0:T(8,128)}, u32[]{:S(2)}) copy-start(f32[3,8,16,128]{3,2,1,0:T(8,128)} %get-tuple-element.131) | copy-start | bytes 589828
  232.8 31.0 %copy-start.24 = (f32[3,8,16,128]{3,2,1,0:T(8,128)S(1)}, f32[3,8,16,128]{3,2,1,0:T(8,128)}, u32[]{:S(2)}) copy-start(f32[3,8,16,128]{3,2,1,0:T(8,128)} %copy-done.23) | copy-start | bytes 589828
  232.8 31.0 %copy-start.26 = (f32[3,8,16,128]{3,2,1,0:T(8,128)S(1)}, f32[3,8,16,128]{3,2,1,0:T(8,128)}, u32[]{:S(2)}) copy-start(f32[3,8,16,128]{3,2,1,0:T(8,128)} %copy-done.25) | copy-start | bytes 589828
  363.6 172.4 %copy-start.1 = (bf16[48,128,256]{2,1,0:T(8,128)(2,1)S(1)}, bf16[48,128,256]{2,1,0:T(8,128)(2,1)}, u32[]{:S(2)}) copy-start(bf16[48,128,256]{2,1,0:T(8,128)(2,1)} %param.12) | copy-start | bytes 9437188
  (36 other events, 302.1 us)
where the time goes:
time: 546 us; the launch traced here: 536 us
  matrix products  181 us (33%)
  local copies, waits for them, and re-layouts  131 us (24%)
  other arithmetic  107 us (20%)
  waiting for transfers between devices  73.7 us (13%)
  starting transfers between devices  42.2 us (8%)
    dot_general x1, matrix products, body(): blocks = jnp.dot(selector, arrived_flat, preferred_element_type=jnp.float32)  172 us
    ppermute x4, waiting for transfers between devices, padded_2(): lax.ppermute(lax.slice_in_dim(block, 0, width, axis=dim), axis, backward)  73.7 us
    add x3, other arithmetic, tricubic(): total = total + (level_w[above] * row_w[across])[None] * inner  46.1 us
    mul x43, local copies, waits for them, and re-layouts, tricubic(): total = total + (level_w[above] * row_w[across])[None] * inner  42.8 us
    unnamed x153, local copies, waits for them, and re-layouts  30.4 us
    gather x2, local copies, waits for them, and re-layouts, body(): outgoing = jnp.take(remapped, source_item, axis=0)  23.4 us
    all_to_all x2, starting transfers between devices, joined_exchange(): lax.all_to_all(pieces, axis, split_axis=0, concat_axis=0, tiled=True)  21.5 us
    ppermute x4, starting transfers between devices, padded_2(): lax.ppermute(lax.slice_in_dim(block, block.shape[dim] - width, None, axis...  16 us
  transfers between devices with their start and end apart: 10, of which 1 were waited for; matrix products, arithmetic and copies ran while one was open for 38% of the time, Pallas kernels for 0%

commit v1 on v0

v1 whole, which is shorter than its diff:
```python
import jax
import jax.numpy as jnp
from jax import lax
from jax.experimental import pallas as pl
from jax.experimental.pallas import tpu as pltpu
from jax.sharding import PartitionSpec as P

NTR = 16
LEV = 8
CAP = 2
BLK_DEV = 16
ROWS = 16
COLS = 128
WIDE = 4
NEAR = 3
WROWS = ROWS + 2 * WIDE
TROWS = ROWS + 2 * NEAR
TILE_STEP = 4
SLOT_STEP = 16
VMEM_LIMIT = 60 * 1024 * 1024


def params(*semantics):
    return pltpu.CompilerParams(
        dimension_semantics=semantics or None, vmem_limit_bytes=VMEM_LIMIT
    )


def remap_kernel(device_ref, block_ref, flux_ref, weight_ref, out_hbm, mark_ref, held, sems, counts):
    step = pl.program_id(0)
    steps = pl.num_programs(0)
    links = weight_ref.shape[1]
    bank = lax.rem(step, 2)

    @pl.when(step == 0)
    def _():
        def clear(i, carry):
            counts[i] = 0
            return carry

        lax.fori_loop(0, counts.shape[0], clear, 0)
        mark_ref[...] = jnp.full(mark_ref.shape, BLK_DEV, jnp.int32)

    def copy(which, slot, bank_at):
        return pltpu.make_async_copy(
            held.at[bank_at, which], out_hbm.at[slot], sems.at[bank_at, which]
        )

    @pl.when(step >= 2)
    def _():
        for which in range(TILE_STEP * links):
            copy(which, 0, bank).wait()

    lanes = lax.broadcasted_iota(jnp.int32, (1, COLS), 1)
    for part in range(TILE_STEP):
        flux = flux_ref[part]
        for pair in range(links // 2):
            both = jnp.concatenate(
                [weight_ref[part, 2 * pair], weight_ref[part, 2 * pair + 1]], axis=1
            )
            made = jnp.dot(flux, both, preferred_element_type=jnp.float32)
            made = made.astype(jnp.bfloat16)
            for side in range(2):
                link = 2 * pair + side
                which = part * links + link
                held[bank, which] = made[:, side * COLS : (side + 1) * COLS]
                tile = step * TILE_STEP + part
                owner = device_ref[tile, link]
                rank = counts[owner]
                counts[owner] = rank + 1
                mark_ref[owner] = jnp.where(
                    lanes == rank, block_ref[tile, link], mark_ref[owner]
                )
                copy(which, owner * CAP + rank, bank).start()

    @pl.when(step == steps - 1)
    def _():
        for which in range(TILE_STEP * links):
            copy(which, 0, 1 - bank).wait()
        for which in range(TILE_STEP * links):
            copy(which, 0, bank).wait()


def remap(fluxes, remap_weights, target_device, target_block, devices):
    tiles, rows, cells = fluxes.shape
    links, cols = remap_weights.shape[1], remap_weights.shape[3]
    return pl.pallas_call(
        remap_kernel,
        grid_spec=pltpu.PrefetchScalarGridSpec(
            num_scalar_prefetch=2,
            grid=(tiles // TILE_STEP,),
            in_specs=[
                pl.BlockSpec((TILE_STEP, rows, cells), lambda i, *_: (i, 0, 0)),
                pl.BlockSpec((TILE_STEP, links, cells, cols), lambda i, *_: (i, 0, 0, 0)),
            ],
            out_specs=[
                pl.BlockSpec(memory_space=pl.ANY),
                pl.BlockSpec((devices, 1, COLS), lambda i, *_: (0, 0, 0)),
            ],
            scratch_shapes=[
                pltpu.VMEM((2, TILE_STEP * links, rows, cols), jnp.bfloat16),
                pltpu.SemaphoreType.DMA((2, TILE_STEP * links)),
                pltpu.SMEM((devices,), jnp.int32),
            ],
        ),
        out_shape=[
            jax.ShapeDtypeStruct((devices * CAP, rows, cols), jnp.bfloat16),
            jax.ShapeDtypeStruct((devices, 1, COLS), jnp.int32),
        ],
        compiler_params=params("arbitrary"),
    )(target_device, target_block, fluxes, remap_weights)


def wind_piece(winds_ref, row, comp):
    return winds_ref[pl.ds(comp * LEV * ROWS + row, LEV, stride=ROWS), :]


def tracer_piece(tracers_ref, row, level, half):
    start = half * 8 * LEV * ROWS + level * ROWS + row
    return tracers_ref[pl.ds(start, 8, stride=LEV * ROWS), :]


WIND_MSG = WIDE * 3 * LEV
TRACER_MSG = NEAR * LEV * NTR


def edge_rows_kernel(tracers_ref, winds_ref, top_ref, bottom_ref):
    for target, wind_from, tracer_from in (
        (top_ref, 0, 0),
        (bottom_ref, ROWS - WIDE, ROWS - NEAR),
    ):
        for row in range(WIDE):
            for comp in range(3):
                at = (row * 3 + comp) * LEV
                target[at : at + LEV, :] = wind_piece(winds_ref, wind_from + row, comp)
        for row in range(NEAR):
            for level in range(LEV):
                for half in range(2):
                    at = WIND_MSG + (row * LEV + level) * NTR + half * 8
                    target[at : at + 8, :] = tracer_piece(
                        tracers_ref, tracer_from + row, level, half
                    )


def edge_rows(tracers, winds):
    shape = jax.ShapeDtypeStruct((WIND_MSG + TRACER_MSG, COLS), jnp.float32)
    return pl.pallas_call(
        edge_rows_kernel, out_shape=[shape, shape], compiler_params=params()
    )(tracers, winds)


EDGE = 2 * WIDE
PER_GROUP = COLS // EDGE
WIND_GROUPS = -(-WROWS // PER_GROUP)
GROUPS = TROWS + 3 * WIND_GROUPS


def edge_cols_kernel(tracers_ref, winds_ref, low_ref, high_ref, twide_ref, wwide_ref, edge_ref):
    per_row = LEV * NTR
    twide_ref[0:TRACER_MSG, :] = low_ref[WIND_MSG : WIND_MSG + TRACER_MSG, :]
    last = (NEAR + ROWS) * per_row
    twide_ref[last : last + TRACER_MSG, :] = high_ref[WIND_MSG : WIND_MSG + TRACER_MSG, :]
    wwide_ref[0:WIND_MSG, :] = low_ref[0:WIND_MSG, :]
    last = (WIDE + ROWS) * 3 * LEV
    wwide_ref[last : last + WIND_MSG, :] = high_ref[0:WIND_MSG, :]

    def rearrange(row, carry):
        for comp in range(3):
            at = pl.multiple_of((row + WIDE) * 3 * LEV + comp * LEV, 8)
            wwide_ref[pl.ds(at, LEV), :] = wind_piece(winds_ref, row, comp)
        for level in range(LEV):
            for half in range(2):
                at = pl.multiple_of((row + NEAR) * per_row + level * NTR + half * 8, 8)
                twide_ref[pl.ds(at, 8), :] = tracer_piece(tracers_ref, row, level, half)
        return carry

    lax.fori_loop(0, ROWS, rearrange, 0)
    group_of = lax.broadcasted_iota(jnp.int32, (8, COLS), 1) // EDGE

    def gather_tracers(row, carry):
        packed = jnp.zeros((8, COLS), jnp.float32)
        for spot in range(PER_GROUP):
            at = pl.multiple_of(row * per_row + spot * 8, 8)
            turned = pltpu.roll(twide_ref[pl.ds(at, 8), :], (WIDE + EDGE * spot) % COLS, 1)
            packed = jnp.where(group_of == spot, turned, packed)
        edge_ref[pl.ds(pl.multiple_of(row * 8, 8), 8), :] = packed
        return carry

    lax.fori_loop(0, TROWS, gather_tracers, 0)
    for comp in range(3):
        for part in range(WIND_GROUPS):
            packed = jnp.zeros((8, COLS), jnp.float32)
            for spot in range(min(PER_GROUP, WROWS - part * PER_GROUP)):
                at = ((part * PER_GROUP + spot) * 3 + comp) * LEV
                turned = pltpu.roll(wwide_ref[at : at + 8, :], (WIDE + EDGE * spot) % COLS, 1)
                packed = jnp.where(group_of == spot, turned, packed)
            at = (TROWS + comp * WIND_GROUPS + part) * 8
            edge_ref[at : at + 8, :] = packed


def edge_cols(tracers, winds, low, high):
    return pl.pallas_call(
        edge_cols_kernel,
        out_shape=[
            jax.ShapeDtypeStruct((TROWS * LEV * NTR, COLS), jnp.float32),
            jax.ShapeDtypeStruct((WROWS * 3 * LEV, COLS), jnp.float32),
            jax.ShapeDtypeStruct((GROUPS * 8, COLS), jnp.float32),
        ],
        compiler_params=params(),
    )(tracers, winds, low, high)


def cubic_weights(frac):
    first = -frac * (frac - 1.0) * (frac - 2.0) / 6.0
    second = (frac + 1.0) * (frac - 1.0) * (frac - 2.0) / 2.0
    third = -(frac + 1.0) * frac * (frac - 2.0) / 2.0
    fourth = (frac + 1.0) * frac * (frac - 1.0) / 6.0
    return (first, second, third, fourth)


def spread_weights(offset, frac, lowest, highest):
    stencil = cubic_weights(frac)
    hits = {value: offset == value for value in range(lowest, highest + 1)}
    spread = []
    for target in range(lowest - 1, highest + 3):
        weight = jnp.zeros(frac.shape, jnp.float32)
        for step in range(4):
            value = target - step + 1
            if value in hits:
                weight = weight + jnp.where(hits[value], stencil[step], 0.0)
        spread.append(weight)
    return spread


def column_shifts(main, edge, reach):
    lane = lax.broadcasted_iota(jnp.int32, main.shape, 1)
    shifted = []
    for step in range(-reach, reach + 1):
        if step == 0:
            shifted.append(main)
            continue
        inside = lane < COLS - step if step > 0 else lane >= -step
        turn = (COLS - step) % COLS
        shifted.append(jnp.where(inside, pltpu.roll(main, turn, 1), pltpu.roll(edge, turn, 1)))
    return shifted


def level_shift(value, step):
    if step == 0:
        return value
    level = lax.broadcasted_iota(jnp.int32, value.shape, 0)
    turned = pltpu.roll(value, (LEV - step) % LEV, 0)
    if step > 0:
        end = jnp.broadcast_to(value[LEV - 1 : LEV, :], value.shape)
        return jnp.where(level >= LEV - step, end, turned)
    end = jnp.broadcast_to(value[0:1, :], value.shape)
    return jnp.where(level < -step, end, turned)


W_TAPS = 9
T_TAPS = 7
L_TAPS = 5
SPREADS = L_TAPS + 2 * T_TAPS


def advect_kernel(
    twide_ref, wwide_ref, left_ref, right_ref, first_ref, second_ref, winds_ref, out_ref,
    wind_taps, tracer_taps, spread_ref,
):
    lane = lax.broadcasted_iota(jnp.int32, (8, COLS), 1)
    from_left = lax.rem(lane, EDGE) < WIDE

    def edge_at(group, spot):
        at = group * 8 if isinstance(group, int) else pl.multiple_of(group * 8, 8)
        both = jnp.where(from_left, left_ref[pl.ds(at, 8), :], right_ref[pl.ds(at, 8), :])
        return pltpu.roll(both, (COLS - WIDE - EDGE * spot) % COLS, 1)

    for comp in range(3):
        for row in range(WROWS):
            edge = edge_at(TROWS + comp * WIND_GROUPS + row // PER_GROUP, row % PER_GROUP)
            at = (row * 3 + comp) * LEV
            shifted = column_shifts(wwide_ref[at : at + LEV, :], edge, WIDE)
            for side in range(W_TAPS):
                for above in range(L_TAPS):
                    wind_taps[row, comp, above, side] = level_shift(shifted[side], above - 2)

    def wind_row(row, carry):
        def component(ref, comp):
            return ref[pl.ds(comp * LEV * ROWS + row, LEV, stride=ROWS), :]

        wind = [component(winds_ref, comp) for comp in range(3)]
        first = [component(first_ref, comp) for comp in range(3)]
        frac = [
            jnp.clip(-wind[comp] - first[comp].astype(jnp.float32), 0.0, 1.0)
            for comp in range(3)
        ]
        level_w = spread_weights(first[0], frac[0], -1, 0)
        row_w = spread_weights(first[1], frac[1], -3, 2)
        col_w = spread_weights(first[2], frac[2], -3, 2)
        total = [jnp.zeros((LEV, COLS), jnp.float32) for _ in range(3)]
        for above in range(L_TAPS):
            part = [jnp.zeros((LEV, COLS), jnp.float32) for _ in range(3)]
            for across in range(W_TAPS):
                for comp in range(3):
                    inner = col_w[0] * wind_taps[row + across, comp, above, 0]
                    for side in range(1, W_TAPS):
                        inner = inner + col_w[side] * wind_taps[row + across, comp, above, side]
                    part[comp] = part[comp] + row_w[across] * inner
            for comp in range(3):
                total[comp] = total[comp] + level_w[above] * part[comp]
        second = [component(second_ref, comp) for comp in range(3)]
        frac = [
            jnp.clip(
                -(wind[comp] + total[comp]) * 0.5 - second[comp].astype(jnp.float32), 0.0, 1.0
            )
            for comp in range(3)
        ]
        weights = spread_weights(second[0], frac[0], -1, 0)
        weights += spread_weights(second[1], frac[1], -2, 1)
        weights += spread_weights(second[2], frac[2], -2, 1)
        for which in range(SPREADS):
            spread_ref[row, which] = weights[which]
        return carry

    lax.fori_loop(0, ROWS, wind_row, 0)

    def tracer_shifts(row, carry):
        for spot in range(PER_GROUP):
            edge = edge_at(row, spot)
            at = pl.multiple_of(row * LEV * NTR + spot * 8, 8)
            shifted = column_shifts(twide_ref[pl.ds(at, 8), :], edge, NEAR)
            for side in range(T_TAPS):
                tracer_taps[row, spot, side] = shifted[side]
        return carry

    lax.fori_loop(0, TROWS, tracer_shifts, 0)

    def tracer_cell(cell, carry):
        row, level = cell // LEV, lax.rem(cell, LEV)

        def weight(which):
            return jnp.broadcast_to(spread_ref[row, which, pl.ds(level, 1), :], (8, COLS))

        row_w = [weight(L_TAPS + which) for which in range(T_TAPS)]
        col_w = [weight(L_TAPS + T_TAPS + which) for which in range(T_TAPS)]
        total = [jnp.zeros((8, COLS), jnp.float32) for _ in range(2)]
        for above in range(L_TAPS):
            source = jnp.clip(level + above - 2, 0, LEV - 1)
            level_w = weight(above)
            part = [jnp.zeros((8, COLS), jnp.float32) for _ in range(2)]
            for across in range(T_TAPS):
                for half in range(2):
                    taps = tracer_taps.at[row + across, source * 2 + half]
                    inner = col_w[0] * taps[0]
                    for side in range(1, T_TAPS):
                        inner = inner + col_w[side] * taps[side]
                    part[half] = part[half] + row_w[across] * inner
            for half in range(2):
                total[half] = total[half] + level_w * part[half]
        for half in range(2):
            start = half * 8 * LEV * ROWS + level * ROWS + row
            out_ref[pl.ds(start, 8, stride=LEV * ROWS), :] = total[half]
        return carry

    lax.fori_loop(0, ROWS * LEV, tracer_cell, 0)


def advect(twide, wwide, left, right, first, second, winds):
    return pl.pallas_call(
        advect_kernel,
        out_shape=jax.ShapeDtypeStruct((NTR * LEV * ROWS, COLS), jnp.float32),
        scratch_shapes=[
            pltpu.VMEM((WROWS, 3, L_TAPS, W_TAPS, LEV, COLS), jnp.float32),
            pltpu.VMEM((TROWS, LEV * 2, T_TAPS, 8, COLS), jnp.float32),
            pltpu.VMEM((ROWS, SPREADS, LEV, COLS), jnp.float32),
        ],
        compiler_params=params(),
    )(twide, wwide, left, right, first, second, winds)


def combine_kernel(mark_ref, arrived_ref, moved_ref, out_ref, total):
    step = pl.program_id(0)
    rows = arrived_ref.shape[1]

    @pl.when(step == 0)
    def _():
        total[...] = jnp.zeros(total.shape, jnp.float32)

    for which in range(SLOT_STEP):
        slot = step * SLOT_STEP + which
        block = mark_ref[slot // CAP, 0, lax.rem(slot, CAP)]
        at = pl.ds(pl.multiple_of(block * rows, rows), rows)
        total[at, :] = total[at, :] + arrived_ref[which].astype(jnp.float32)

    @pl.when(step == pl.num_programs(0) - 1)
    def _():
        for row in range(rows):
            picked = total[pl.ds(row, BLK_DEV, stride=rows), :]
            at = row * ROWS
            out_ref[at : at + ROWS, :] = moved_ref[at : at + ROWS, :] + picked


def combine(marks, arrived, moved):
    slots, rows, cols = arrived.shape
    return pl.pallas_call(
        combine_kernel,
        grid_spec=pltpu.PrefetchScalarGridSpec(
            num_scalar_prefetch=1,
            grid=(slots // SLOT_STEP,),
            in_specs=[
                pl.BlockSpec((SLOT_STEP, rows, cols), lambda i, *_: (i, 0, 0)),
                pl.BlockSpec(moved.shape, lambda i, *_: (0, 0)),
            ],
            out_specs=pl.BlockSpec(moved.shape, lambda i, *_: (0, 0)),
            scratch_shapes=[pltpu.VMEM(((BLK_DEV + 1) * rows, cols), jnp.float32)],
        ),
        out_shape=jax.ShapeDtypeStruct(moved.shape, jnp.float32),
        compiler_params=params("arbitrary"),
    )(marks, arrived, moved)


def body(
    tracers, winds, depart_first, depart_second, fluxes, remap_weights, target_device, target_block
):
    lat_count, lon_count = lax.axis_size("lat"), lax.axis_size("lon")
    both = ("lat", "lon")
    slots, marks = remap(
        fluxes, remap_weights, target_device, target_block, lat_count * lon_count
    )
    shape = tracers.shape
    tracers, winds, slots, marks = lax.optimization_barrier((tracers, winds, slots, marks))
    arrived = lax.all_to_all(slots, both, split_axis=0, concat_axis=0, tiled=True)
    flat = lambda field: field.reshape(-1, COLS)
    tracers, winds = flat(tracers), flat(winds)
    top, bottom = edge_rows(tracers, winds)
    up = [(i, i + 1) for i in range(lat_count - 1)]
    low = lax.ppermute(bottom, "lat", up)
    high = lax.ppermute(top, "lat", [(b, a) for a, b in up])
    twide, wwide, edge = edge_cols(tracers, winds, low, high)
    around = [(i, (i + 1) % lon_count) for i in range(lon_count)]
    left = lax.ppermute(edge, "lon", around)
    right = lax.ppermute(edge, "lon", [(b, a) for a, b in around])
    edge, marks = lax.optimization_barrier((edge, marks))
    arrived_marks = lax.all_to_all(marks, both, split_axis=0, concat_axis=0, tiled=True)
    moved = advect(
        twide, wwide, left, right, flat(depart_first), flat(depart_second), winds
    )
    return combine(arrived_marks, arrived, moved).reshape(shape)


def solution(mesh):
    in_specs = (
        P(None, None, "lat", "lon"),
        P(None, None, "lat", "lon"),
        P(None, None, "lat", "lon"),
        P(None, None, "lat", "lon"),
        P(("lat", "lon"), None, None),
        P(("lat", "lon"), None, None, None),
        P(("lat", "lon"), None),
        P(("lat", "lon"), None),
    )
    out_specs = P(None, None, "lat", "lon")
    return jax.shard_map(body, mesh=mesh, in_specs=in_specs, out_specs=out_specs, check_vma=False)
```

time: 546 us -> 229 us (0.42)
  the two profiles are of different devices: /device:TPU:95 before, /device:TPU:36 now
where the time goes in v1:
time: 229 us; the launch traced here: 228 us
  waiting for transfers between devices  106 us (46%)
  Pallas kernels  82.2 us (36%)
  blocking collectives  18.6 us (8%)
  starting transfers between devices  16.4 us (7%)
  local copies, waits for them, and re-layouts  4.17 us (2%)
    ppermute x1, waiting for transfers between devices, body(): right = lax.ppermute(edge, 'lon', [(b, a) for a, b in around])  102 us
    pallas_call x1, Pallas kernels, advect(): pl.pallas_call(advect_kernel, out_shape=jax.ShapeDtypeStruct((NTR * LEV *...  46.1 us
    all_to_all x1, blocking collectives, body(): lax.all_to_all(marks, both, split_axis=0, concat_axis=0, tiled=True)  18.6 us
    pallas_call x1, Pallas kernels, remap(): pl.pallas_call(remap_kernel, grid_spec=pltpu.PrefetchScalarGridSpec(num_s...  14.8 us
    pallas_call x1, Pallas kernels, combine(): pl.pallas_call(combine_kernel, grid_spec=pltpu.PrefetchScalarGridSpec(num...  13.8 us
    all_to_all x1, starting transfers between devices, body(): lax.all_to_all(slots, both, split_axis=0, concat_axis=0, tiled=True)  8.72 us
    pallas_call x1, Pallas kernels, edge_cols(): pl.pallas_call(edge_cols_kernel, out_shape=[jax.ShapeDtypeStruct((TROWS *...  5.31 us
  transfers between devices with their start and end apart: 5, of which 3 were waited for; matrix products, arithmetic and copies ran while one was open for 0% of the time, Pallas kernels for 20%

profile of v1, /device:TPU:36, one launch (start us, length us, event | category | flops | bytes accessed | tf_op | source)
XLA Modules:
  0.0 227.8 jit_solution(14476206023410703159)
XLA Ops:
  0.0 1.4 copy.9.device_ref
  1.4 1.4 copy.10.block_ref
  2.7 14.8 %shard_map.82 = (bf16[256,128,128]{2,1,0:T(8,128)(2,1)}, s32[128,1,128]{2,1,0:T(1,128)}) custom-call(s32[48,4]{1,0:T(8,128)} %copy.9.device_ref, s32[48,4]{1,0:T(8,128)} %copy.10.block_ref, bf16[48,128,256]{2,1,0:T(8,128)(2,1)} %flux_ref.1, bf16[48,4,256,128]{3,2,1,0:T(8,128)(2,1)} %weight_ref.1), custom_call_target="tpu_custom_call" | custom-call | tf_op jit(solution)/shard_map/pallas_call | solution.py:87
  17.6 2.2 shard_map.83
  19.8 1.9 collective-permute-start
  21.7 3.6 %collective-permute-start.1 = (f32[480,128]{1,0:T(8,128)}, f32[480,128]{1,0:T(8,128)S(1)}, u32[]{:S(2)}, u32[]{:S(2)}) collective-permute-start(f32[480,128]{1,0:T(8,128)} %get-tuple-element.22), channel_id=1, source_target_pairs={{16,0},{32,16},{48,32},{64,48},{80,64},{96,80},{112,96},{17,1},{33... | collective-permute-start | bytes 737288 | tf_op jit(solution)/shard_map/ppermute | solution.py:438
  25.4 2.1 collective-permute-done.low_ref
  27.5 0.0 copy-start
  27.5 1.9 collective-permute-done.1.high_ref
  29.4 0.0 copy-done
  29.4 0.0 copy-start.1
  29.4 0.7 copy-done.1
  30.1 5.3 %shard_map.84 = (f32[2816,128]{1,0:T(8,128)}, f32[576,128]{1,0:T(8,128)}, f32[224,128]{1,0:T(8,128)}) custom-call(f32[2048,128]{1,0:T(8,128)} %bitcast.6, f32[384,128]{1,0:T(8,128)} %bitcast.8, f32[480,128]{1,0:T(8,128)} %copy-done, f32[480,128]{1,0:T(8,128)} %copy-done.1), custom_call_target="tpu_custom_call" | custom-call | tf_op jit(solution)/shard_map/pallas_call | solution.py:202
  35.4 18.6 %all_to_all.10.mark_ref = s32[128,1,128]{2,1,0:T(1,128)} all-to-all(s32[128,1,128]{2,1,0:T(1,128)} %get-tuple-element.25), channel_id=1, replica_groups=mesh['lat'=8,'lon'=16] {'lat','lon'}, dimensions={0} | all-to-all | bytes 131072 | tf_op jit(solution)/shard_map/all_to_all | solution.py:444
  54.0 0.0 copy-start.4
  54.0 8.7 %all-to-all-start.1 = ((bf16[256,128,128]{2,1,0:T(8,128)(2,1)}), bf16[256,128,128]{2,1,0:T(8,128)(2,1)}, u32[]{:S(2)}, u32[]{:S(2)}) async-start(bf16[256,128,128]{2,1,0:T(8,128)(2,1)} %get-tuple-element.26), calls=%async_computation.1 | async-start | bytes 16777216 | tf_op jit(solution)/shard_map/all_to_all | solution.py:432
  62.8 0.0 copy-done.4
  62.8 0.6 collective-permute-start.3
  63.4 1.5 collective-permute-start.2
  64.9 102.4 %collective-permute-done.3.right_ref = f32[224,128]{1,0:T(8,128)S(1)} collective-permute-done((f32[224,128]{1,0:T(8,128)S(1)}, f32[224,128]{1,0:T(8,128)S(1)}, u32[]{:S(2)}, u32[]{:S(2)}) %collective-permute-start.3) | collective-permute-done | bytes 114720 | tf_op jit(solution)/shard_map/ppermute | solution.py:442
  167.3 0.0 copy-start.2
  167.3 0.0 collective-permute-done.2.left_ref
  167.3 0.0 copy-start.3
  167.3 0.6 copy-done.2
  167.9 0.1 copy-done.3
  168.0 46.1 %shard_map.85.moved_ref = f32[2048,128]{1,0:T(8,128)} custom-call(f32[2816,128]{1,0:T(8,128)} %get-tuple-element.27.twide_ref, f32[576,128]{1,0:T(8,128)} %get-tuple-element.28.wwide_ref, f32[224,128]{1,0:T(8,128)} %copy-done.3, f32[224,128]{1,0:T(8,128)} %copy-done.2, s32[384,128]{1,0:T(8,128)} %bitcast.10, s32[384,128]{1,0:T(8,128)} %bitcast.11, ...), custom_call_target="tpu_custom_call" | custom-call | tf_op jit(solution)/shard_map/pallas_call | solution.py:369
  214.1 0.0 all-to-all-done.1.arrived_ref
  214.1 13.8 %shard_map.86 = f32[2048,128]{1,0:T(8,128)} custom-call(s32[128,1,128]{2,1,0:T(1,128)} %all_to_all.10.mark_ref, bf16[256,128,128]{2,1,0:T(8,128)(2,1)} %all-to-all-done.1.arrived_ref, f32[2048,128]{1,0:T(8,128)} %shard_map.85.moved_ref), custom_call_target="tpu_custom_call" | custom-call | tf_op jit(solution)/shard_map/pallas_call | solution.py:405
Async XLA Ops:
  19.8 7.7 %collective-permute-start = (f32[480,128]{1,0:T(8,128)}, f32[480,128]{1,0:T(8,128)S(1)}, u32[]{:S(2)}, u32[]{:S(2)}) collective-permute-start(f32[480,128]{1,0:T(8,128)} %get-tuple-element.21), channel_id=1, source_target_pairs={{0,16},{16,32},{32,48},{48,64},{64,80},{80,96},{96,112},{1,17},{17... | collective-permute-start | bytes 737288 | tf_op jit(solution)/shard_map/ppermute | solution.py:437
  21.7 7.7 %collective-permute-start.1 = (f32[480,128]{1,0:T(8,128)}, f32[480,128]{1,0:T(8,128)S(1)}, u32[]{:S(2)}, u32[]{:S(2)}) collective-permute-start(f32[480,128]{1,0:T(8,128)} %get-tuple-element.22), channel_id=1, source_target_pairs={{16,0},{32,16},{48,32},{64,48},{80,64},{96,80},{112,96},{17,1},{33... | collective-permute-start | bytes 737288 | tf_op jit(solution)/shard_map/ppermute | solution.py:438
  27.5 1.9 copy-start
  29.4 0.7 copy-start.1
  54.0 8.7 %copy-start.4 = (f32[224,128]{1,0:T(8,128)S(1)}, f32[224,128]{1,0:T(8,128)}, u32[]{:S(2)}) copy-start(f32[224,128]{1,0:T(8,128)} %get-tuple-element.23) | copy-start | bytes 344068
  54.0 160.0 %all-to-all-start.1 = ((bf16[256,128,128]{2,1,0:T(8,128)(2,1)}), bf16[256,128,128]{2,1,0:T(8,128)(2,1)}, u32[]{:S(2)}, u32[]{:S(2)}) async-start(bf16[256,128,128]{2,1,0:T(8,128)(2,1)} %get-tuple-element.26), calls=%async_computation.1 | async-start | bytes 16777216 | tf_op jit(solution)/shard_map/all_to_all | solution.py:432
  62.8 104.5 %collective-permute-start.3 = (f32[224,128]{1,0:T(8,128)S(1)}, f32[224,128]{1,0:T(8,128)S(1)}, u32[]{:S(2)}, u32[]{:S(2)}) collective-permute-start(f32[224,128]{1,0:T(8,128)S(1)} %copy-done.4), channel_id=1, source_target_pairs={{1,0},{2,1},{3,2},{4,3},{5,4},{6,5},{7,6},{8,7},{9,8},{10,9},{11,1... | collective-permute-start | bytes 344072 | tf_op jit(solution)/shard_map/ppermute | solution.py:442
  63.4 103.9 %collective-permute-start.2 = (f32[224,128]{1,0:T(8,128)S(1)}, f32[224,128]{1,0:T(8,128)S(1)}, u32[]{:S(2)}, u32[]{:S(2)}) collective-permute-start(f32[224,128]{1,0:T(8,128)S(1)} %copy-done.4), channel_id=1, source_target_pairs={{0,1},{1,2},{2,3},{3,4},{4,5},{5,6},{6,7},{7,8},{8,9},{9,10},{10,1... | collective-permute-start | bytes 344072 | tf_op jit(solution)/shard_map/ppermute | solution.py:441
  167.3 0.6 copy-start.2
  167.3 0.7 copy-start.3

commit v2 on v1

v2 whole, which is shorter than its diff:
```python
import jax
import jax.numpy as jnp
from jax import lax
from jax.experimental import pallas as pl
from jax.experimental.pallas import tpu as pltpu
from jax.sharding import PartitionSpec as P

NTR = 16
LEV = 8
CAP = 2
BLK_DEV = 16
ROWS = 16
COLS = 128
WIDE = 4
NEAR = 3
WROWS = ROWS + 2 * WIDE
TROWS = ROWS + 2 * NEAR
EDGE = 2 * WIDE
PER_GROUP = COLS // EDGE
TILE_STEP = 4
SOURCE_STEP = 8
SUMS = 4
MARK_ROWS = 8
VMEM_LIMIT = 60 * 1024 * 1024


def params(*semantics):
    return pltpu.CompilerParams(
        dimension_semantics=semantics or None, vmem_limit_bytes=VMEM_LIMIT
    )


def remap_kernel(
    device_ref, block_ref, flux_ref, weight_ref, out_hbm, held, marks, sent, sems, mark_sem, counts
):
    step = pl.program_id(0)
    steps = pl.num_programs(0)
    links, rows = weight_ref.shape[1], flux_ref.shape[1]
    bank = lax.rem(step, 2)

    @pl.when(step == 0)
    def _():
        def clear(i, carry):
            counts[i] = 0
            return carry

        lax.fori_loop(0, counts.shape[0], clear, 0)
        marks[...] = jnp.full(marks.shape, BLK_DEV, jnp.float32)

    def copy(which, owner, rank, bank_at):
        into = pl.ds(pl.multiple_of(rank * rows, rows), rows)
        return pltpu.make_async_copy(
            held.at[bank_at, which], out_hbm.at[owner, into], sems.at[bank_at, which]
        )

    @pl.when(step >= 2)
    def _():
        for which in range(TILE_STEP * links):
            copy(which, 0, 0, bank).wait()

    for part in range(TILE_STEP):
        flux = flux_ref[part]
        for pair in range(links // 2):
            both = jnp.concatenate(
                [weight_ref[part, 2 * pair], weight_ref[part, 2 * pair + 1]], axis=1
            )
            made = jnp.dot(flux, both, preferred_element_type=jnp.float32)
            made = made.astype(jnp.bfloat16)
            for side in range(2):
                which = part * links + 2 * pair + side
                held[bank, which] = made[:, side * COLS : (side + 1) * COLS]
    for part in range(TILE_STEP):
        for link in range(links):
            tile = step * TILE_STEP + part
            owner = device_ref[link, tile]
            rank = counts[owner]
            counts[owner] = rank + 1
            copy(part * links + link, owner, rank, bank).start()
            value = block_ref[link, tile].astype(jnp.float32)
            marks[owner, pl.ds(rank, 1), :] = jnp.full((1, COLS), value, jnp.float32)

    @pl.when(step == steps - 1)
    def _():
        sent[...] = marks[...].astype(jnp.bfloat16)
        last = pltpu.make_async_copy(
            sent, out_hbm.at[:, pl.ds(CAP * rows, MARK_ROWS)], mark_sem
        )
        last.start()
        for which in range(TILE_STEP * links):
            copy(which, 0, 0, 1 - bank).wait()
        for which in range(TILE_STEP * links):
            copy(which, 0, 0, bank).wait()
        last.wait()


def remap(fluxes, remap_weights, target_device, target_block, devices):
    tiles, rows, cells = fluxes.shape
    links, cols = remap_weights.shape[1], remap_weights.shape[3]
    return pl.pallas_call(
        remap_kernel,
        grid_spec=pltpu.PrefetchScalarGridSpec(
            num_scalar_prefetch=2,
            grid=(tiles // TILE_STEP,),
            in_specs=[
                pl.BlockSpec((TILE_STEP, rows, cells), lambda i, *_: (i, 0, 0)),
                pl.BlockSpec((TILE_STEP, links, cells, cols), lambda i, *_: (i, 0, 0, 0)),
            ],
            out_specs=pl.BlockSpec(memory_space=pl.ANY),
            scratch_shapes=[
                pltpu.VMEM((2, TILE_STEP * links, rows, cols), jnp.bfloat16),
                pltpu.VMEM((devices, MARK_ROWS, cols), jnp.float32),
                pltpu.VMEM((devices, MARK_ROWS, cols), jnp.bfloat16),
                pltpu.SemaphoreType.DMA((2, TILE_STEP * links)),
                pltpu.SemaphoreType.DMA,
                pltpu.SMEM((devices,), jnp.int32),
            ],
        ),
        out_shape=jax.ShapeDtypeStruct((devices, CAP * rows + MARK_ROWS, cols), jnp.bfloat16),
        compiler_params=params("arbitrary"),
    )(target_device.T, target_block.T, fluxes, remap_weights)


def wind_piece(winds_ref, row, comp):
    return winds_ref[pl.ds(comp * LEV * ROWS + row, LEV, stride=ROWS), :]


def tracer_piece(tracers_ref, row, level, half):
    start = half * 8 * LEV * ROWS + level * ROWS + row
    return tracers_ref[pl.ds(start, 8, stride=LEV * ROWS), :]


WIND_MSG = WIDE * 3 * LEV
TRACER_MSG = NEAR * LEV * NTR
TRACER_EDGE = WIND_MSG + TRACER_MSG
WIND_EDGE = TRACER_EDGE + NEAR * 8
MSG = WIND_EDGE + 3 * 8
EDGE_ROWS = (ROWS + 3) * 8


def edge_cols_kernel(tracers_ref, winds_ref, edge_ref):
    group_of = lax.broadcasted_iota(jnp.int32, (8, COLS), 1) // EDGE

    def packed(pieces):
        held = jnp.zeros((8, COLS), jnp.float32)
        for spot, piece in enumerate(pieces):
            turned = pltpu.roll(piece, (WIDE + EDGE * spot) % COLS, 1)
            held = jnp.where(group_of == spot, turned, held)
        return held

    def tracer_row(row, carry):
        pieces = [tracer_piece(tracers_ref, row, spot // 2, spot % 2) for spot in range(PER_GROUP)]
        edge_ref[pl.ds(pl.multiple_of(row * 8, 8), 8), :] = packed(pieces)
        return carry

    lax.fori_loop(0, ROWS, tracer_row, 0)
    for comp in range(3):
        at = (ROWS + comp) * 8
        edge_ref[at : at + 8, :] = packed([wind_piece(winds_ref, row, comp) for row in range(ROWS)])


def edge_cols(tracers, winds):
    return pl.pallas_call(
        edge_cols_kernel,
        out_shape=jax.ShapeDtypeStruct((EDGE_ROWS, COLS), jnp.float32),
        compiler_params=params(),
    )(tracers, winds)


def edge_rows_kernel(tracers_ref, winds_ref, left_ref, right_ref, top_ref, bottom_ref, both_ref):
    lane = lax.broadcasted_iota(jnp.int32, (EDGE_ROWS, COLS), 1)
    both_ref[...] = jnp.where(lax.rem(lane, EDGE) < WIDE, left_ref[...], right_ref[...])
    for target, wind_from, tracer_from in (
        (top_ref, 0, 0),
        (bottom_ref, ROWS - WIDE, ROWS - NEAR),
    ):
        for row in range(WIDE):
            for comp in range(3):
                at = (row * 3 + comp) * LEV
                target[at : at + LEV, :] = wind_piece(winds_ref, wind_from + row, comp)
        for row in range(NEAR):
            for level in range(LEV):
                for half in range(2):
                    at = WIND_MSG + (row * LEV + level) * NTR + half * 8
                    target[at : at + 8, :] = tracer_piece(
                        tracers_ref, tracer_from + row, level, half
                    )
        target[TRACER_EDGE:WIND_EDGE, :] = both_ref[tracer_from * 8 : (tracer_from + NEAR) * 8, :]
        target[WIND_EDGE:MSG, :] = both_ref[ROWS * 8 : EDGE_ROWS, :]


def edge_rows(tracers, winds, left, right):
    shape = jax.ShapeDtypeStruct((MSG, COLS), jnp.float32)
    return pl.pallas_call(
        edge_rows_kernel,
        out_shape=[shape, shape, jax.ShapeDtypeStruct((EDGE_ROWS, COLS), jnp.float32)],
        compiler_params=params(),
    )(tracers, winds, left, right)


def cubic_weights(frac):
    first = -frac * (frac - 1.0) * (frac - 2.0) / 6.0
    second = (frac + 1.0) * (frac - 1.0) * (frac - 2.0) / 2.0
    third = -(frac + 1.0) * frac * (frac - 2.0) / 2.0
    fourth = (frac + 1.0) * frac * (frac - 1.0) / 6.0
    return (first, second, third, fourth)


def spread_weights(offset, frac, lowest, highest):
    stencil = cubic_weights(frac)
    hits = {value: offset == value for value in range(lowest, highest + 1)}
    spread = []
    for target in range(lowest - 1, highest + 3):
        weight = jnp.zeros(frac.shape, jnp.float32)
        for step in range(4):
            value = target - step + 1
            if value in hits:
                weight = weight + jnp.where(hits[value], stencil[step], 0.0)
        spread.append(weight)
    return spread


def column_shifts(main, edge, reach):
    lane = lax.broadcasted_iota(jnp.int32, main.shape, 1)
    shifted = []
    for step in range(-reach, reach + 1):
        if step == 0:
            shifted.append(main)
            continue
        inside = lane < COLS - step if step > 0 else lane >= -step
        turn = (COLS - step) % COLS
        shifted.append(jnp.where(inside, pltpu.roll(main, turn, 1), pltpu.roll(edge, turn, 1)))
    return shifted


def level_shift(value, step):
    if step == 0:
        return value
    level = lax.broadcasted_iota(jnp.int32, value.shape, 0)
    turned = pltpu.roll(value, (LEV - step) % LEV, 0)
    if step > 0:
        end = jnp.broadcast_to(value[LEV - 1 : LEV, :], value.shape)
        return jnp.where(level >= LEV - step, end, turned)
    end = jnp.broadcast_to(value[0:1, :], value.shape)
    return jnp.where(level < -step, end, turned)


W_TAPS = 9
T_TAPS = 7
L_TAPS = 5
SPREADS = L_TAPS + 2 * T_TAPS


def advect_kernel(
    tracers_ref, low_ref, high_ref, both_ref, first_ref, second_ref, winds_ref, out_ref,
    wind_taps, tracer_taps, spread_ref,
):
    def edge_piece(ref, at, spot):
        return pltpu.roll(ref[pl.ds(at, 8), :], (COLS - WIDE - EDGE * spot) % COLS, 1)

    for comp in range(3):
        for row in range(WROWS):
            if row < WIDE:
                at = (row * 3 + comp) * LEV
                main = low_ref[at : at + LEV, :]
                edge = edge_piece(low_ref, WIND_EDGE + comp * 8, ROWS - WIDE + row)
            elif row < WIDE + ROWS:
                main = wind_piece(winds_ref, row - WIDE, comp)
                edge = edge_piece(both_ref, (ROWS + comp) * 8, row - WIDE)
            else:
                at = ((row - WIDE - ROWS) * 3 + comp) * LEV
                main = high_ref[at : at + LEV, :]
                edge = edge_piece(high_ref, WIND_EDGE + comp * 8, row - WIDE - ROWS)
            shifted = column_shifts(main, edge, WIDE)
            for side in range(W_TAPS):
                for above in range(L_TAPS):
                    wind_taps[row, comp, above, side] = level_shift(shifted[side], above - 2)

    def wind_row(row, carry):
        def component(ref, comp):
            return ref[pl.ds(comp * LEV * ROWS + row, LEV, stride=ROWS), :]

        wind = [component(winds_ref, comp) for comp in range(3)]
        first = [component(first_ref, comp) for comp in range(3)]
        frac = [
            jnp.clip(-wind[comp] - first[comp].astype(jnp.float32), 0.0, 1.0)
            for comp in range(3)
        ]
        level_w = spread_weights(first[0], frac[0], -1, 0)
        row_w = spread_weights(first[1], frac[1], -3, 2)
        col_w = spread_weights(first[2], frac[2], -3, 2)
        total = [jnp.zeros((LEV, COLS), jnp.float32) for _ in range(3)]
        for above in range(L_TAPS):
            part = [jnp.zeros((LEV, COLS), jnp.float32) for _ in range(3)]
            for across in range(W_TAPS):
                for comp in range(3):
                    inner = col_w[0] * wind_taps[row + across, comp, above, 0]
                    for side in range(1, W_TAPS):
                        inner = inner + col_w[side] * wind_taps[row + across, comp, above, side]
                    part[comp] = part[comp] + row_w[across] * inner
            for comp in range(3):
                total[comp] = total[comp] + level_w[above] * part[comp]
        second = [component(second_ref, comp) for comp in range(3)]
        frac = [
            jnp.clip(
                -(wind[comp] + total[comp]) * 0.5 - second[comp].astype(jnp.float32), 0.0, 1.0
            )
            for comp in range(3)
        ]
        weights = spread_weights(second[0], frac[0], -1, 0)
        weights += spread_weights(second[1], frac[1], -2, 1)
        weights += spread_weights(second[2], frac[2], -2, 1)
        for which in range(SPREADS):
            spread_ref[row, which] = weights[which]
        return carry

    lax.fori_loop(0, ROWS, wind_row, 0)

    def own_shifts(row, carry):
        for spot in range(PER_GROUP):
            main = tracer_piece(tracers_ref, row, spot // 2, spot % 2)
            edge = edge_piece(both_ref, pl.multiple_of(row * 8, 8), spot)
            shifted = column_shifts(main, edge, NEAR)
            for side in range(T_TAPS):
                tracer_taps[row + NEAR, spot, side] = shifted[side]
        return carry

    lax.fori_loop(0, ROWS, own_shifts, 0)
    for ref, onto in ((low_ref, 0), (high_ref, NEAR + ROWS)):

        def halo_shifts(row, carry, ref=ref, onto=onto):
            for spot in range(PER_GROUP):
                at = pl.multiple_of(WIND_MSG + row * LEV * NTR + spot * 8, 8)
                edge = edge_piece(ref, pl.multiple_of(TRACER_EDGE + row * 8, 8), spot)
                shifted = column_shifts(ref[pl.ds(at, 8), :], edge, NEAR)
                for side in range(T_TAPS):
                    tracer_taps[row + onto, spot, side] = shifted[side]
            return carry

        lax.fori_loop(0, NEAR, halo_shifts, 0)

    def tracer_cell(cell, carry):
        row, level = cell // LEV, lax.rem(cell, LEV)

        def weight(which):
            return jnp.broadcast_to(spread_ref[row, which, pl.ds(level, 1), :], (8, COLS))

        row_w = [weight(L_TAPS + which) for which in range(T_TAPS)]
        col_w = [weight(L_TAPS + T_TAPS + which) for which in range(T_TAPS)]
        total = [jnp.zeros((8, COLS), jnp.float32) for _ in range(2)]
        for above in range(L_TAPS):
            source = jnp.clip(level + above - 2, 0, LEV - 1)
            level_w = weight(above)
            part = [jnp.zeros((8, COLS), jnp.float32) for _ in range(2)]
            for across in range(T_TAPS):
                for half in range(2):
                    taps = tracer_taps.at[row + across, source * 2 + half]
                    inner = col_w[0] * taps[0]
                    for side in range(1, T_TAPS):
                        inner = inner + col_w[side] * taps[side]
                    part[half] = part[half] + row_w[across] * inner
            for half in range(2):
                total[half] = total[half] + level_w * part[half]
        for half in range(2):
            start = half * 8 * LEV * ROWS + level * ROWS + row
            out_ref[pl.ds(start, 8, stride=LEV * ROWS), :] = total[half]
        return carry

    lax.fori_loop(0, ROWS * LEV, tracer_cell, 0)


def advect(tracers, low, high, both, first, second, winds):
    return pl.pallas_call(
        advect_kernel,
        out_shape=jax.ShapeDtypeStruct((NTR * LEV * ROWS, COLS), jnp.float32),
        scratch_shapes=[
            pltpu.VMEM((WROWS, 3, L_TAPS, W_TAPS, LEV, COLS), jnp.float32),
            pltpu.VMEM((TROWS, LEV * 2, T_TAPS, 8, COLS), jnp.float32),
            pltpu.VMEM((ROWS, SPREADS, LEV, COLS), jnp.float32),
        ],
        compiler_params=params(),
    )(tracers, low, high, both, first, second, winds)


def combine_kernel(arrived_ref, moved_ref, out_ref, *totals):
    step = pl.program_id(0)
    rows = (arrived_ref.shape[1] - MARK_ROWS) // CAP

    @pl.when(step == 0)
    def _():
        for total in totals:
            total[...] = jnp.zeros(total.shape, jnp.float32)

    blocks = []
    for which in range(SOURCE_STEP):
        marks = arrived_ref[which, CAP * rows : CAP * rows + MARK_ROWS, :]
        marks = marks.astype(jnp.float32).astype(jnp.int32)
        blocks += [marks[rank, 0] for rank in range(CAP)]
    for which in range(SOURCE_STEP):
        for rank in range(CAP):
            total = totals[(which * CAP + rank) % SUMS]
            at = pl.ds(pl.multiple_of(blocks[which * CAP + rank] * rows, rows), rows)
            piece = arrived_ref[which, rank * rows : (rank + 1) * rows, :]
            total[at, :] = total[at, :] + piece.astype(jnp.float32)

    @pl.when(step == pl.num_programs(0) - 1)
    def _():
        for row in range(rows):
            at = row * ROWS
            picked = moved_ref[at : at + ROWS, :]
            for total in totals:
                picked = picked + total[pl.ds(row, BLK_DEV, stride=rows), :]
            out_ref[at : at + ROWS, :] = picked


def combine(arrived, moved):
    sources, deep, cols = arrived.shape
    rows = (deep - MARK_ROWS) // CAP
    return pl.pallas_call(
        combine_kernel,
        grid=(sources // SOURCE_STEP,),
        in_specs=[
            pl.BlockSpec((SOURCE_STEP, deep, cols), lambda i: (i, 0, 0)),
            pl.BlockSpec(moved.shape, lambda i: (0, 0)),
        ],
        out_specs=pl.BlockSpec(moved.shape, lambda i: (0, 0)),
        scratch_shapes=[pltpu.VMEM(((BLK_DEV + 1) * rows, cols), jnp.float32)] * SUMS,
        out_shape=jax.ShapeDtypeStruct(moved.shape, jnp.float32),
        compiler_params=params("arbitrary"),
    )(arrived, moved)


def halo_advect(tracers, winds, left, right, depart_first, depart_second):
    lat_count = lax.axis_size("lat")
    top, bottom, both = edge_rows(tracers, winds, left, right)
    up = [(i, i + 1) for i in range(lat_count - 1)]
    low = lax.ppermute(bottom, "lat", up)
    high = lax.ppermute(top, "lat", [(b, a) for a, b in up])
    return advect(tracers, low, high, both, depart_first, depart_second, winds)


def side_columns(tracers, winds):
    lon_count = lax.axis_size("lon")
    edge = edge_cols(tracers, winds)
    around = [(i, (i + 1) % lon_count) for i in range(lon_count)]
    left = lax.ppermute(edge, "lon", around)
    right = lax.ppermute(edge, "lon", [(b, a) for a, b in around])
    return left, right


def body(
    tracers, winds, depart_first, depart_second, fluxes, remap_weights, target_device, target_block
):
    shape = tracers.shape
    devices = lax.axis_size("lat") * lax.axis_size("lon")
    tracers, winds, depart_first, depart_second = (
        field.reshape(-1, COLS) for field in (tracers, winds, depart_first, depart_second)
    )
    left, right = side_columns(tracers, winds)
    chunks = remap(fluxes, remap_weights, target_device, target_block, devices)
    chunks, left, right = lax.optimization_barrier((chunks, left, right))
    arrived = lax.all_to_all(chunks, ("lat", "lon"), split_axis=0, concat_axis=0, tiled=True)
    moved = halo_advect(tracers, winds, left, right, depart_first, depart_second)
    return combine(arrived, moved).reshape(shape)


def solution(mesh):
    in_specs = (
        P(None, None, "lat", "lon"),
        P(None, None, "lat", "lon"),
        P(None, None, "lat", "lon"),
        P(None, None, "lat", "lon"),
        P(("lat", "lon"), None, None),
        P(("lat", "lon"), None, None, None),
        P(("lat", "lon"), None),
        P(("lat", "lon"), None),
    )
    out_specs = P(None, None, "lat", "lon")
    return jax.shard_map(body, mesh=mesh, in_specs=in_specs, out_specs=out_specs, check_vma=False)
```

time: 229 us -> 195 us (0.85)
  the two profiles are of different devices: /device:TPU:36 before, /device:TPU:71 now
where the time goes in v2:
time: 195 us; the launch traced here: 194 us
  waiting for transfers between devices  92.6 us (47%)
  Pallas kernels  80.2 us (41%)
  starting transfers between devices  20.9 us (11%)
    ppermute x1, waiting for transfers between devices, halo_advect(): low = lax.ppermute(bottom, 'lat', up)  75.7 us
    pallas_call x1, Pallas kernels, advect(): pl.pallas_call(advect_kernel, out_shape=jax.ShapeDtypeStruct((NTR * LEV *...  46.1 us
    ppermute x1, waiting for transfers between devices, halo_advect(): high = lax.ppermute(top, 'lat', [(b, a) for a, b in up])  16.8 us
    pallas_call x1, Pallas kernels, remap(): pl.pallas_call(remap_kernel, grid_spec=pltpu.PrefetchScalarGridSpec(num_s...  14.2 us
    pallas_call x1, Pallas kernels, combine(): pl.pallas_call(combine_kernel, grid=(sources // SOURCE_STEP,), in_specs=[...  13.9 us
    all_to_all x1, starting transfers between devices, body(): lax.all_to_all(chunks, ('lat', 'lon'), split_axis=0, concat_axis=0, tiled...  12.1 us
  transfers between devices with their start and end apart: 5, of which 2 were waited for; matrix products, arithmetic and copies ran while one was open for 0% of the time, Pallas kernels for 32%

profile of v2, /device:TPU:71, one launch (start us, length us, event | category | flops | bytes accessed | tf_op | source)
XLA Modules:
  0.0 194.4 jit_solution(16752239138911098871)
XLA Ops:
  0.0 3.7 %shard_map.83 = f32[152,128]{1,0:T(8,128)} custom-call(f32[2048,128]{1,0:T(8,128)} %bitcast.7, f32[384,128]{1,0:T(8,128)} %bitcast.10), custom_call_target="tpu_custom_call" | custom-call | tf_op jit(solution)/shard_map/pallas_call | solution.py:162
  3.7 0.5 collective-permute-start.1
  4.3 3.0 %collective-permute-start = (f32[152,128]{1,0:T(8,128)}, f32[152,128]{1,0:T(8,128)S(1)}, u32[]{:S(2)}, u32[]{:S(2)}) collective-permute-start(f32[152,128]{1,0:T(8,128)} %shard_map.83), channel_id=1, source_target_pairs={{0,1},{1,2},{2,3},{3,4},{4,5},{5,6},{6,7},{7,8},{8,9},{9,10},{10,1... | collective-permute-start | bytes 233480 | tf_op jit(solution)/shard_map/ppermute | solution.py:445
  7.3 14.2 %shard_map.82 = bf16[128,264,128]{2,1,0:T(8,128)(2,1)} custom-call(s32[4,48]{1,0:T(4,128)} %bitcast.15, s32[4,48]{1,0:T(4,128)} %bitcast.16, bf16[48,128,256]{2,1,0:T(8,128)(2,1)} %flux_ref.1, bf16[48,4,256,128]{3,2,1,0:T(8,128)(2,1)} %weight_ref.1), custom_call_target="tpu_custom_call" | custom-call | tf_op jit(solution)/shard_map/pallas_call | solution.py:99
  21.5 0.0 collective-permute-done.1.right_ref
  21.5 0.0 copy-start.2
  21.5 0.0 collective-permute-done.left_ref
  21.5 0.0 copy-start.3
  21.6 12.1 %all-to-all-start = ((bf16[128,264,128]{2,1,0:T(8,128)(2,1)}), bf16[128,264,128]{2,1,0:T(8,128)(2,1)}, u32[]{:S(2)}, u32[]{:S(2)}) async-start(bf16[128,264,128]{2,1,0:T(8,128)(2,1)} %shard_map.82), calls=%async_computation | async-start | bytes 17301504 | tf_op jit(solution)/shard_map/all_to_all | solution.py:461
  33.6 0.0 copy-done.2
  33.6 0.0 copy-done.3
  33.6 2.3 %shard_map.84 = (f32[528,128]{1,0:T(8,128)}, f32[528,128]{1,0:T(8,128)}, f32[152,128]{1,0:T(8,128)}) custom-call(f32[2048,128]{1,0:T(8,128)} %bitcast.8, f32[384,128]{1,0:T(8,128)} %bitcast.11, f32[152,128]{1,0:T(8,128)} %copy-done.3, f32[152,128]{1,0:T(8,128)} %copy-done.2), custom_call_target="tpu_custom_call" | custom-call | tf_op jit(solution)/shard_map/pallas_call | solution.py:193
  36.0 3.3 %collective-permute-start.2 = (f32[528,128]{1,0:T(8,128)}, f32[528,128]{1,0:T(8,128)S(1)}, u32[]{:S(2)}, u32[]{:S(2)}) collective-permute-start(f32[528,128]{1,0:T(8,128)} %get-tuple-element.14), channel_id=1, source_target_pairs={{0,16},{16,32},{32,48},{48,64},{64,80},{80,96},{96,112},{1,17},{17... | collective-permute-start | bytes 811016 | tf_op jit(solution)/shard_map/ppermute | solution.py:436
  39.3 1.9 collective-permute-start.3
  41.2 75.7 %collective-permute-done.2.low_ref = f32[528,128]{1,0:T(8,128)S(1)} collective-permute-done((f32[528,128]{1,0:T(8,128)}, f32[528,128]{1,0:T(8,128)S(1)}, u32[]{:S(2)}, u32[]{:S(2)}) %collective-permute-start.2) | collective-permute-done | bytes 270368 | tf_op jit(solution)/shard_map/ppermute | solution.py:436
  116.9 0.0 copy-start
  116.9 16.8 %collective-permute-done.3.high_ref = f32[528,128]{1,0:T(8,128)S(1)} collective-permute-done((f32[528,128]{1,0:T(8,128)}, f32[528,128]{1,0:T(8,128)S(1)}, u32[]{:S(2)}, u32[]{:S(2)}) %collective-permute-start.3) | collective-permute-done | bytes 270368 | tf_op jit(solution)/shard_map/ppermute | solution.py:437
  133.8 0.0 copy-start.1
  133.8 0.0 copy-done
  133.8 0.7 copy-done.1
  134.5 46.1 %shard_map.85.moved_ref = f32[2048,128]{1,0:T(8,128)} custom-call(f32[2048,128]{1,0:T(8,128)} %bitcast.9, f32[528,128]{1,0:T(8,128)} %copy-done, f32[528,128]{1,0:T(8,128)} %copy-done.1, f32[152,128]{1,0:T(8,128)} %get-tuple-element.16.both_ref, s32[384,128]{1,0:T(8,128)} %bitcast.13, s32[384,128]{1,0:T(8,128)} %bitcast.14, f32[384,128]{1,0:T(8,128)} %bitcast.12), custom_call_target="tpu_custom_call" | custom-call | tf_op jit(solution)/shard_map/pallas_call | solution.py:372
  180.6 0.0 all-to-all-done.arrived_ref
  180.6 13.9 %shard_map.86 = f32[2048,128]{1,0:T(8,128)} custom-call(bf16[128,264,128]{2,1,0:T(8,128)(2,1)} %all-to-all-done.arrived_ref, f32[2048,128]{1,0:T(8,128)} %shard_map.85.moved_ref), custom_call_target="tpu_custom_call" | custom-call | tf_op jit(solution)/shard_map/pallas_call | solution.py:418
Async XLA Ops:
  3.7 17.8 %collective-permute-start.1 = (f32[152,128]{1,0:T(8,128)}, f32[152,128]{1,0:T(8,128)S(1)}, u32[]{:S(2)}, u32[]{:S(2)}) collective-permute-start(f32[152,128]{1,0:T(8,128)} %shard_map.83), channel_id=1, source_target_pairs={{1,0},{2,1},{3,2},{4,3},{5,4},{6,5},{7,6},{8,7},{9,8},{10,9},{11,1... | collective-permute-start | bytes 233480 | tf_op jit(solution)/shard_map/ppermute | solution.py:446
  4.3 17.3 %collective-permute-start = (f32[152,128]{1,0:T(8,128)}, f32[152,128]{1,0:T(8,128)S(1)}, u32[]{:S(2)}, u32[]{:S(2)}) collective-permute-start(f32[152,128]{1,0:T(8,128)} %shard_map.83), channel_id=1, source_target_pairs={{0,1},{1,2},{2,3},{3,4},{4,5},{5,6},{6,7},{7,8},{8,9},{9,10},{10,1... | collective-permute-start | bytes 233480 | tf_op jit(solution)/shard_map/ppermute | solution.py:445
  21.5 12.1 %copy-start.2 = (f32[152,128]{1,0:T(8,128)}, f32[152,128]{1,0:T(8,128)S(1)}, u32[]{:S(2)}) copy-start(f32[152,128]{1,0:T(8,128)S(1)} %collective-permute-done.1.right_ref) | copy-start | bytes 233476
  21.5 12.1 %copy-start.3 = (f32[152,128]{1,0:T(8,128)}, f32[152,128]{1,0:T(8,128)S(1)}, u32[]{:S(2)}) copy-start(f32[152,128]{1,0:T(8,128)S(1)} %collective-permute-done.left_ref) | copy-start | bytes 233476
  21.6 159.0 %all-to-all-start = ((bf16[128,264,128]{2,1,0:T(8,128)(2,1)}), bf16[128,264,128]{2,1,0:T(8,128)(2,1)}, u32[]{:S(2)}, u32[]{:S(2)}) async-start(bf16[128,264,128]{2,1,0:T(8,128)(2,1)} %shard_map.82), calls=%async_computation | async-start | bytes 17301504 | tf_op jit(solution)/shard_map/all_to_all | solution.py:461
  36.0 80.9 %collective-permute-start.2 = (f32[528,128]{1,0:T(8,128)}, f32[528,128]{1,0:T(8,128)S(1)}, u32[]{:S(2)}, u32[]{:S(2)}) collective-permute-start(f32[528,128]{1,0:T(8,128)} %get-tuple-element.14), channel_id=1, source_target_pairs={{0,16},{16,32},{32,48},{48,64},{64,80},{80,96},{96,112},{1,17},{17... | collective-permute-start | bytes 811016 | tf_op jit(solution)/shard_map/ppermute | solution.py:436
  39.3 94.5 %collective-permute-start.3 = (f32[528,128]{1,0:T(8,128)}, f32[528,128]{1,0:T(8,128)S(1)}, u32[]{:S(2)}, u32[]{:S(2)}) collective-permute-start(f32[528,128]{1,0:T(8,128)} %get-tuple-element.15), channel_id=1, source_target_pairs={{16,0},{32,16},{48,32},{64,48},{80,64},{96,80},{112,96},{17,1},{33... | collective-permute-start | bytes 811016 | tf_op jit(solution)/shard_map/ppermute | solution.py:437
  116.9 16.9 %copy-start = (f32[528,128]{1,0:T(8,128)}, f32[528,128]{1,0:T(8,128)S(1)}, u32[]{:S(2)}) copy-start(f32[528,128]{1,0:T(8,128)S(1)} %collective-permute-done.2.low_ref) | copy-start | bytes 811012
  133.8 0.7 copy-start.1

commit v3 on v2

--- a/solution.py
+++ b/solution.py
@@ -1,3 +1,5 @@
+import functools
+
 import jax
 import jax.numpy as jnp
 from jax import lax
@@ -17,10 +19,11 @@
 TROWS = ROWS + 2 * NEAR
 EDGE = 2 * WIDE
 PER_GROUP = COLS // EDGE
-TILE_STEP = 4
+TILE_STEP = 2
 SOURCE_STEP = 8
-SUMS = 4
+SUMS = 2
 MARK_ROWS = 8
+OUT_PARTS = 4
 VMEM_LIMIT = 60 * 1024 * 1024
 
 
@@ -31,93 +34,110 @@
 
 
 def remap_kernel(
-    device_ref, block_ref, flux_ref, weight_ref, out_hbm, held, marks, sent, sems, mark_sem, counts
+    first, tiles, final, device_ref, block_ref, flux_hbm, weight_hbm, *refs
 ):
-    step = pl.program_id(0)
-    steps = pl.num_programs(0)
-    links, rows = weight_ref.shape[1], flux_ref.shape[1]
-    bank = lax.rem(step, 2)
-
-    @pl.when(step == 0)
-    def _():
-        def clear(i, carry):
-            counts[i] = 0
-            return carry
-
-        lax.fori_loop(0, counts.shape[0], clear, 0)
+    out_hbm, flux_buf, weight_buf, held, marks, sent, flux_sems, weight_sems, out_sem, mark_sem, counts = refs[-11:]
+    links, rows = weight_hbm.shape[1], flux_hbm.shape[1]
+    groups = tiles // TILE_STEP
+
+    def loads(group):
+        at = pl.ds(group * TILE_STEP, TILE_STEP)
+        source = pl.ds(first + group * TILE_STEP, TILE_STEP)
+        return (
+            pltpu.make_async_copy(flux_hbm.at[source], flux_buf.at[at], flux_sems.at[group]),
+            pltpu.make_async_copy(weight_hbm.at[source], weight_buf.at[at], weight_sems.at[group]),
+        )
+
+    for group in range(groups):
+        for load in loads(group):
+            load.start()
+
+    def clear(i, carry):
+        counts[i] = 0
+        return carry
+
+    lax.fori_loop(0, counts.shape[0], clear, 0, unroll=8)
+    if final:
         marks[...] = jnp.full(marks.shape, BLK_DEV, jnp.float32)
 
-    def copy(which, owner, rank, bank_at):
-        into = pl.ds(pl.multiple_of(rank * rows, rows), rows)
-        return pltpu.make_async_copy(
-            held.at[bank_at, which], out_hbm.at[owner, into], sems.at[bank_at, which]
-        )
-
-    @pl.when(step >= 2)
-    def _():
-        for which in range(TILE_STEP * links):
-            copy(which, 0, 0, bank).wait()
-
-    for part in range(TILE_STEP):
-        flux = flux_ref[part]
-        for pair in range(links // 2):
-            both = jnp.concatenate(
-                [weight_ref[part, 2 * pair], weight_ref[part, 2 * pair + 1]], axis=1
-            )
-            made = jnp.dot(flux, both, preferred_element_type=jnp.float32)
-            made = made.astype(jnp.bfloat16)
-            for side in range(2):
-                which = part * links + 2 * pair + side
-                held[bank, which] = made[:, side * COLS : (side + 1) * COLS]
-    for part in range(TILE_STEP):
-        for link in range(links):
-            tile = step * TILE_STEP + part
-            owner = device_ref[link, tile]
-            rank = counts[owner]
-            counts[owner] = rank + 1
-            copy(part * links + link, owner, rank, bank).start()
+    def place(tile, link):
+        owner = device_ref[link, tile]
+        rank = counts[owner]
+        counts[owner] = rank + 1
+        if final:
             value = block_ref[link, tile].astype(jnp.float32)
             marks[owner, pl.ds(rank, 1), :] = jnp.full((1, COLS), value, jnp.float32)
-
-    @pl.when(step == steps - 1)
-    def _():
+        return owner, pl.ds(pl.multiple_of(rank * rows, rows), rows)
+
+    def earlier(tile, carry):
+        for link in range(links):
+            place(tile, link)
+        return carry
+
+    lax.fori_loop(0, first, earlier, 0)
+
+    def work(group, carry):
+        for load in loads(group):
+            load.wait()
+        for part in range(TILE_STEP):
+            at = group * TILE_STEP + part
+            flux = flux_buf[at]
+            for pair in range(links // 2):
+                both = jnp.concatenate(
+                    [weight_buf[at, 2 * pair], weight_buf[at, 2 * pair + 1]], axis=1
+                )
+                made = jnp.dot(flux, both, preferred_element_type=jnp.float32)
+                made = made.astype(jnp.bfloat16)
+                for side in range(2):
+                    into = pl.ds(side * rows, rows)
+                    held[at * (links // 2) + pair, into] = made[:, side * COLS : (side + 1) * COLS]
+        for part in range(TILE_STEP):
+            at = group * TILE_STEP + part
+            for link in range(links):
+                owner, into = place(first + at, link)
+                source = held.at[at * (links // 2) + link // 2, pl.ds(link % 2 * rows, rows)]
+                pltpu.make_async_copy(source, out_hbm.at[owner, into], out_sem).start()
+        return carry
+
+    lax.fori_loop(0, groups, work, 0)
+    if final:
         sent[...] = marks[...].astype(jnp.bfloat16)
         last = pltpu.make_async_copy(
             sent, out_hbm.at[:, pl.ds(CAP * rows, MARK_ROWS)], mark_sem
         )
         last.start()
-        for which in range(TILE_STEP * links):
-            copy(which, 0, 0, 1 - bank).wait()
-        for which in range(TILE_STEP * links):
-            copy(which, 0, 0, bank).wait()
         last.wait()
-
-
-def remap(fluxes, remap_weights, target_device, target_block, devices):
-    tiles, rows, cells = fluxes.shape
+    everything = out_hbm.at[pl.ds(0, tiles * links // 2), pl.ds(0, 2 * rows)]
+    pltpu.make_async_copy(held, everything, out_sem).wait()
+
+
+def remap(fluxes, remap_weights, target_device, target_block, devices, first, tiles, chunks=None):
+    rows, cells = fluxes.shape[1:]
     links, cols = remap_weights.shape[1], remap_weights.shape[3]
+    final = chunks is not None
+    anywhere = pl.BlockSpec(memory_space=pl.ANY)
+    inputs = (target_device.T, target_block.T, fluxes, remap_weights) + ((chunks,) if final else ())
+    groups = tiles // TILE_STEP
     return pl.pallas_call(
-        remap_kernel,
-        grid_spec=pltpu.PrefetchScalarGridSpec(
-            num_scalar_prefetch=2,
-            grid=(tiles // TILE_STEP,),
-            in_specs=[
-                pl.BlockSpec((TILE_STEP, rows, cells), lambda i, *_: (i, 0, 0)),
-                pl.BlockSpec((TILE_STEP, links, cells, cols), lambda i, *_: (i, 0, 0, 0)),
-            ],
-            out_specs=pl.BlockSpec(memory_space=pl.ANY),
-            scratch_shapes=[
-                pltpu.VMEM((2, TILE_STEP * links, rows, cols), jnp.bfloat16),
-                pltpu.VMEM((devices, MARK_ROWS, cols), jnp.float32),
-                pltpu.VMEM((devices, MARK_ROWS, cols), jnp.bfloat16),
-                pltpu.SemaphoreType.DMA((2, TILE_STEP * links)),
-                pltpu.SemaphoreType.DMA,
-                pltpu.SMEM((devices,), jnp.int32),
-            ],
-        ),
+        functools.partial(remap_kernel, first, tiles, final),
+        in_specs=[pl.BlockSpec(memory_space=pltpu.SMEM)] * 2 + [anywhere] * (3 if final else 2),
+        out_specs=anywhere,
+        scratch_shapes=[
+            pltpu.VMEM((tiles, rows, cells), jnp.bfloat16),
+            pltpu.VMEM((tiles, links, cells, cols), jnp.bfloat16),
+            pltpu.VMEM((tiles * links // 2, 2 * rows, cols), jnp.bfloat16),
+            pltpu.VMEM((devices, MARK_ROWS, cols), jnp.float32),
+            pltpu.VMEM((devices, MARK_ROWS, cols), jnp.bfloat16),
+            pltpu.SemaphoreType.DMA((groups,)),
+            pltpu.SemaphoreType.DMA((groups,)),
+            pltpu.SemaphoreType.DMA,
+            pltpu.SemaphoreType.DMA,
+            pltpu.SMEM((devices,), jnp.int32),
+        ],
         out_shape=jax.ShapeDtypeStruct((devices, CAP * rows + MARK_ROWS, cols), jnp.bfloat16),
-        compiler_params=params("arbitrary"),
-    )(target_device.T, target_block.T, fluxes, remap_weights)
+        input_output_aliases={4: 0} if final else {},
+        compiler_params=params(),
+    )(*inputs)
 
 
 def wind_piece(winds_ref, row, comp):
@@ -381,61 +401,78 @@
     )(tracers, low, high, both, first, second, winds)
 
 
-def combine_kernel(arrived_ref, moved_ref, out_ref, *totals):
-    step = pl.program_id(0)
-    rows = (arrived_ref.shape[1] - MARK_ROWS) // CAP
-
-    @pl.when(step == 0)
-    def _():
-        for total in totals:
-            total[...] = jnp.zeros(total.shape, jnp.float32)
-
-    blocks = []
-    for which in range(SOURCE_STEP):
-        marks = arrived_ref[which, CAP * rows : CAP * rows + MARK_ROWS, :]
-        marks = marks.astype(jnp.float32).astype(jnp.int32)
-        blocks += [marks[rank, 0] for rank in range(CAP)]
-    for which in range(SOURCE_STEP):
-        for rank in range(CAP):
-            total = totals[(which * CAP + rank) % SUMS]
-            at = pl.ds(pl.multiple_of(blocks[which * CAP + rank] * rows, rows), rows)
-            piece = arrived_ref[which, rank * rows : (rank + 1) * rows, :]
-            total[at, :] = total[at, :] + piece.astype(jnp.float32)
-
-    @pl.when(step == pl.num_programs(0) - 1)
-    def _():
-        for row in range(rows):
+def combine_kernel(
+    arrived_hbm, moved_hbm, out_hbm, arrived_buf, moved_buf, out_buf, arrived_sems, moved_sem, out_sems, *totals
+):
+    sources, deep, cols = arrived_hbm.shape
+    rows = (deep - MARK_ROWS) // CAP
+    groups = sources // SOURCE_STEP
+
+    def load(group):
+        at = pl.ds(group * SOURCE_STEP, SOURCE_STEP)
+        return pltpu.make_async_copy(arrived_hbm.at[at], arrived_buf.at[at], arrived_sems.at[group])
+
+    for group in range(groups):
+        load(group).start()
+    moved_load = pltpu.make_async_copy(moved_hbm, moved_buf, moved_sem)
+    moved_load.start()
+    for total in totals:
+        total[...] = jnp.zeros(total.shape, jnp.float32)
+
+    def add(group, carry):
+        load(group).wait()
+        blocks = []
+        for which in range(SOURCE_STEP):
+            marks = arrived_buf[group * SOURCE_STEP + which, CAP * rows : deep, :]
+            marks = marks.astype(jnp.float32).astype(jnp.int32)
+            blocks += [marks[rank, 0] for rank in range(CAP)]
+        for which in range(SOURCE_STEP):
+            for rank in range(CAP):
+                item = which * CAP + rank
+                total = totals[item % SUMS]
+                at = pl.ds(pl.multiple_of(blocks[item] * rows, rows), rows)
+                piece = arrived_buf[group * SOURCE_STEP + which, rank * rows : (rank + 1) * rows, :]
+                total[at, :] = total[at, :] + piece.astype(jnp.float32)
+        return carry
+
+    lax.fori_loop(0, groups, add, 0)
+    moved_load.wait()
+    share = rows // OUT_PARTS
+    stores = []
+    for part in range(OUT_PARTS):
+        for row in range(part * share, (part + 1) * share):
             at = row * ROWS
-            picked = moved_ref[at : at + ROWS, :]
+            picked = moved_buf[at : at + ROWS, :]
             for total in totals:
                 picked = picked + total[pl.ds(row, BLK_DEV, stride=rows), :]
-            out_ref[at : at + ROWS, :] = picked
+            out_buf[at : at + ROWS, :] = picked
+        at = pl.ds(part * share * ROWS, share * ROWS)
+        stores.append(pltpu.make_async_copy(out_buf.at[at], out_hbm.at[at], out_sems.at[part]))
+        stores[-1].start()
+    for store in stores:
+        store.wait()
 
 
 def combine(arrived, moved):
     sources, deep, cols = arrived.shape
     rows = (deep - MARK_ROWS) // CAP
+    anywhere = pl.BlockSpec(memory_space=pl.ANY)
     return pl.pallas_call(
         combine_kernel,
-        grid=(sources // SOURCE_STEP,),
-        in_specs=[
-            pl.BlockSpec((SOURCE_STEP, deep, cols), lambda i: (i, 0, 0)),
-            pl.BlockSpec(moved.shape, lambda i: (0, 0)),
-        ],
-        out_specs=pl.BlockSpec(moved.shape, lambda i: (0, 0)),
-        scratch_shapes=[pltpu.VMEM(((BLK_DEV + 1) * rows, cols), jnp.float32)] * SUMS,
+        in_specs=[anywhere] * 2,
+        out_specs=anywhere,
+        scratch_shapes=[
+            pltpu.VMEM(arrived.shape, arrived.dtype),
+            pltpu.VMEM(moved.shape, moved.dtype),
+            pltpu.VMEM(moved.shape, moved.dtype),
+            pltpu.SemaphoreType.DMA((sources // SOURCE_STEP,)),
+            pltpu.SemaphoreType.DMA,
+            pltpu.SemaphoreType.DMA((OUT_PARTS,)),
+        ]
+        + [pltpu.VMEM(((BLK_DEV + 1) * rows, cols), jnp.float32)] * SUMS,
         out_shape=jax.ShapeDtypeStruct(moved.shape, jnp.float32),
-        compiler_params=params("arbitrary"),
+        compiler_params=params(),
     )(arrived, moved)
-
-
-def halo_advect(tracers, winds, left, right, depart_first, depart_second):
-    lat_count = lax.axis_size("lat")
-    top, bottom, both = edge_rows(tracers, winds, left, right)
-    up = [(i, i + 1) for i in range(lat_count - 1)]
-    low = lax.ppermute(bottom, "lat", up)
-    high = lax.ppermute(top, "lat", [(b, a) for a, b in up])
-    return advect(tracers, low, high, both, depart_first, depart_second, winds)
 
 
 def side_columns(tracers, winds):
@@ -445,6 +482,14 @@
     left = lax.ppermute(edge, "lon", around)
     right = lax.ppermute(edge, "lon", [(b, a) for a, b in around])
     return left, right
+
+
+def outer_rows(top, bottom):
+    lat_count = lax.axis_size("lat")
+    up = [(i, i + 1) for i in range(lat_count - 1)]
+    low = lax.ppermute(bottom, "lat", up)
+    high = lax.ppermute(top, "lat", [(b, a) for a, b in up])
+    return low, high
 
 
 def body(
@@ -455,11 +500,19 @@
     tracers, winds, depart_first, depart_second = (
         field.reshape(-1, COLS) for field in (tracers, winds, depart_first, depart_second)
     )
+    tiles = fluxes.shape[0]
+    half = tiles // 2
+    emission = (fluxes, remap_weights, target_device, target_block, devices)
     left, right = side_columns(tracers, winds)
-    chunks = remap(fluxes, remap_weights, target_device, target_block, devices)
+    chunks = remap(*emission, 0, half)
     chunks, left, right = lax.optimization_barrier((chunks, left, right))
+    top, bottom, both = edge_rows(tracers, winds, left, right)
+    chunks, top, bottom = lax.optimization_barrier((chunks, top, bottom))
+    low, high = outer_rows(top, bottom)
+    chunks = remap(*emission, half, tiles - half, chunks)
+    chunks, low, high = lax.optimization_barrier((chunks, low, high))
     arrived = lax.all_to_all(chunks, ("lat", "lon"), split_axis=0, concat_axis=0, tiled=True)
-    moved = halo_advect(tracers, winds, left, right, depart_first, depart_second)
+    moved = advect(tracers, low, high, both, depart_first, depart_second, winds)
     return combine(arrived, moved).reshape(shape)
 
 

time: 195 us -> 158 us (0.81)
  the two profiles are of different devices: /device:TPU:71 before, /device:TPU:36 now
where the time goes in v3:
time: 158 us; the launch traced here: 157 us
  Pallas kernels  69.8 us (44%)
  waiting for transfers between devices  64.4 us (41%)
  starting transfers between devices  21 us (13%)
    all_to_all x1, waiting for transfers between devices, body(): lax.all_to_all(chunks, ('lat', 'lon'), split_axis=0, concat_axis=0, tiled...  64.4 us
    pallas_call x1, Pallas kernels, advect(): pl.pallas_call(advect_kernel, out_shape=jax.ShapeDtypeStruct((NTR * LEV *...  46.1 us
    all_to_all x1, starting transfers between devices, body(): lax.all_to_all(chunks, ('lat', 'lon'), split_axis=0, concat_axis=0, tiled...  13.5 us
    pallas_call x2, Pallas kernels, remap(): pl.pallas_call(functools.partial(remap_kernel, first, tiles, final), in_s...  11.8 us
    pallas_call x1, Pallas kernels, combine(): pl.pallas_call(combine_kernel, in_specs=[anywhere] * 2, out_specs=anywher...  5.87 us
    pallas_call x1, Pallas kernels, edge_cols(): pl.pallas_call(edge_cols_kernel, out_shape=jax.ShapeDtypeStruct((EDGE_ROW...  3.73 us
    ppermute x1, starting transfers between devices, outer_rows(): high = lax.ppermute(top, 'lat', [(b, a) for a, b in up])  3.64 us
  transfers between devices with their start and end apart: 5, of which 1 were waited for; matrix products, arithmetic and copies ran while one was open for 0% of the time, Pallas kernels for 37%

profile of v3, /device:TPU:36, one launch (start us, length us, event | category | flops | bytes accessed | tf_op | source)
XLA Modules:
  0.0 156.6 jit_solution(3214065973948087550)
XLA Ops:
  0.0 3.7 %shard_map.83 = f32[152,128]{1,0:T(8,128)} custom-call(f32[2048,128]{1,0:T(8,128)} %bitcast.7, f32[384,128]{1,0:T(8,128)} %bitcast.10), custom_call_target="tpu_custom_call" | custom-call | tf_op jit(solution)/shard_map/pallas_call | solution.py:182
  3.7 0.5 collective-permute-start.1
  4.3 1.5 collective-permute-start
  5.8 5.8 %shard_map.82.refs_0_ = bf16[128,264,128]{2,1,0:T(8,128)(2,1)} custom-call(s32[4,48]{1,0:T(4,128)} %bitcast.15, s32[4,48]{1,0:T(4,128)} %bitcast.17, bf16[48,128,256]{2,1,0:T(8,128)(2,1)} %flux_hbm.3, bf16[48,4,256,128]{3,2,1,0:T(8,128)(2,1)} %weight_hbm.3), custom_call_target="tpu_custom_call" | custom-call | tf_op jit(solution)/shard_map/pallas_call | solution.py:121
  11.6 0.0 collective-permute-done.1.right_ref
  11.6 0.0 copy-start.2
  11.6 0.0 collective-permute-done.left_ref
  11.6 0.6 copy-done.2
  12.2 0.0 copy-start.3
  12.2 0.6 copy-done.3
  12.9 2.3 %shard_map.84 = (f32[528,128]{1,0:T(8,128)}, f32[528,128]{1,0:T(8,128)}, f32[152,128]{1,0:T(8,128)}) custom-call(f32[2048,128]{1,0:T(8,128)} %bitcast.8, f32[384,128]{1,0:T(8,128)} %bitcast.11, f32[152,128]{1,0:T(8,128)} %copy-done.3, f32[152,128]{1,0:T(8,128)} %copy-done.2), custom_call_target="tpu_custom_call" | custom-call | tf_op jit(solution)/shard_map/pallas_call | solution.py:213
  15.2 1.9 %collective-permute-start.2 = (f32[528,128]{1,0:T(8,128)}, f32[528,128]{1,0:T(8,128)S(1)}, u32[]{:S(2)}, u32[]{:S(2)}) collective-permute-start(f32[528,128]{1,0:T(8,128)} %get-tuple-element.23), channel_id=1, source_target_pairs={{0,16},{16,32},{32,48},{48,64},{64,80},{80,96},{96,112},{1,17},{17... | collective-permute-start | bytes 811016 | tf_op jit(solution)/shard_map/ppermute | solution.py:490
  17.1 3.6 %collective-permute-start.3 = (f32[528,128]{1,0:T(8,128)}, f32[528,128]{1,0:T(8,128)S(1)}, u32[]{:S(2)}, u32[]{:S(2)}) collective-permute-start(f32[528,128]{1,0:T(8,128)} %get-tuple-element.24), channel_id=1, source_target_pairs={{16,0},{32,16},{48,32},{64,48},{80,64},{96,80},{112,96},{17,1},{33... | collective-permute-start | bytes 811016 | tf_op jit(solution)/shard_map/ppermute | solution.py:491
  20.7 5.9 %shard_map.85 = bf16[128,264,128]{2,1,0:T(8,128)(2,1)} custom-call(s32[4,48]{1,0:T(4,128)} %bitcast.16, s32[4,48]{1,0:T(4,128)} %bitcast.18, bf16[48,128,256]{2,1,0:T(8,128)(2,1)} %flux_hbm.3, bf16[48,4,256,128]{3,2,1,0:T(8,128)(2,1)} %weight_hbm.3, bf16[128,264,128]{2,1,0:T(8,128)(2,1)} %shard_map.82.refs_0_), custom_call_target="tpu_custom_call", output_to_operand_aliasing={{}: (4, {})} | custom-call | tf_op jit(solution)/shard_map/pallas_call | solution.py:121
  26.7 0.0 collective-permute-done.2.low_ref
  26.7 0.0 copy-start
  26.7 0.0 collective-permute-done.3.high_ref
  26.7 0.0 copy-start.1
  26.7 13.5 %all-to-all-start = ((bf16[128,264,128]{2,1,0:T(8,128)(2,1)}), bf16[128,264,128]{2,1,0:T(8,128)(2,1)}, u32[]{:S(2)}, u32[]{:S(2)}) async-start(bf16[128,264,128]{2,1,0:T(8,128)(2,1)} %shard_map.85), calls=%async_computation | async-start | bytes 17301504 | tf_op jit(solution)/shard_map/all_to_all | solution.py:514
  40.2 0.0 copy-done
  40.2 0.0 copy-done.1
  40.2 46.1 %shard_map.86.moved_hbm = f32[2048,128]{1,0:T(8,128)} custom-call(f32[2048,128]{1,0:T(8,128)} %bitcast.9, f32[528,128]{1,0:T(8,128)} %copy-done, f32[528,128]{1,0:T(8,128)} %copy-done.1, f32[152,128]{1,0:T(8,128)} %get-tuple-element.28.both_ref, s32[384,128]{1,0:T(8,128)} %bitcast.13, s32[384,128]{1,0:T(8,128)} %bitcast.14, f32[384,128]{1,0:T(8,128)} %bitcast.12), custom_call_target="tpu_custom_call" | custom-call | tf_op jit(solution)/shard_map/pallas_call | solution.py:392
  86.3 64.4 %all-to-all-done.arrived_hbm = bf16[128,264,128]{2,1,0:T(8,128)(2,1)} async-done(((bf16[128,264,128]{2,1,0:T(8,128)(2,1)}), bf16[128,264,128]{2,1,0:T(8,128)(2,1)}, u32[]{:S(2)}, u32[]{:S(2)}) %all-to-all-start) | async-done | bytes 8650784 | tf_op jit(solution)/shard_map/all_to_all | solution.py:514
  150.7 5.9 %shard_map.87 = f32[2048,128]{1,0:T(8,128)} custom-call(bf16[128,264,128]{2,1,0:T(8,128)(2,1)} %all-to-all-done.arrived_hbm, f32[2048,128]{1,0:T(8,128)} %shard_map.86.moved_hbm), custom_call_target="tpu_custom_call" | custom-call | tf_op jit(solution)/shard_map/pallas_call | solution.py:460
Async XLA Ops:
  3.7 7.9 %collective-permute-start.1 = (f32[152,128]{1,0:T(8,128)}, f32[152,128]{1,0:T(8,128)S(1)}, u32[]{:S(2)}, u32[]{:S(2)}) collective-permute-start(f32[152,128]{1,0:T(8,128)} %shard_map.83), channel_id=1, source_target_pairs={{1,0},{2,1},{3,2},{4,3},{5,4},{6,5},{7,6},{8,7},{9,8},{10,9},{11,1... | collective-permute-start | bytes 233480 | tf_op jit(solution)/shard_map/ppermute | solution.py:483
  4.3 7.3 %collective-permute-start = (f32[152,128]{1,0:T(8,128)}, f32[152,128]{1,0:T(8,128)S(1)}, u32[]{:S(2)}, u32[]{:S(2)}) collective-permute-start(f32[152,128]{1,0:T(8,128)} %shard_map.83), channel_id=1, source_target_pairs={{0,1},{1,2},{2,3},{3,4},{4,5},{5,6},{6,7},{7,8},{8,9},{9,10},{10,1... | collective-permute-start | bytes 233480 | tf_op jit(solution)/shard_map/ppermute | solution.py:482
  11.6 0.6 copy-start.2
  12.2 0.6 copy-start.3
  15.2 11.5 %collective-permute-start.2 = (f32[528,128]{1,0:T(8,128)}, f32[528,128]{1,0:T(8,128)S(1)}, u32[]{:S(2)}, u32[]{:S(2)}) collective-permute-start(f32[528,128]{1,0:T(8,128)} %get-tuple-element.23), channel_id=1, source_target_pairs={{0,16},{16,32},{32,48},{48,64},{64,80},{80,96},{96,112},{1,17},{17... | collective-permute-start | bytes 811016 | tf_op jit(solution)/shard_map/ppermute | solution.py:490
  17.1 9.6 %collective-permute-start.3 = (f32[528,128]{1,0:T(8,128)}, f32[528,128]{1,0:T(8,128)S(1)}, u32[]{:S(2)}, u32[]{:S(2)}) collective-permute-start(f32[528,128]{1,0:T(8,128)} %get-tuple-element.24), channel_id=1, source_target_pairs={{16,0},{32,16},{48,32},{64,48},{80,64},{96,80},{112,96},{17,1},{33... | collective-permute-start | bytes 811016 | tf_op jit(solution)/shard_map/ppermute | solution.py:491
  26.7 13.5 %copy-start = (f32[528,128]{1,0:T(8,128)}, f32[528,128]{1,0:T(8,128)S(1)}, u32[]{:S(2)}) copy-start(f32[528,128]{1,0:T(8,128)S(1)} %collective-permute-done.2.low_ref) | copy-start | bytes 811012
  26.7 13.5 %copy-start.1 = (f32[528,128]{1,0:T(8,128)}, f32[528,128]{1,0:T(8,128)S(1)}, u32[]{:S(2)}) copy-start(f32[528,128]{1,0:T(8,128)S(1)} %collective-permute-done.3.high_ref) | copy-start | bytes 811012
  26.7 124.0 %all-to-all-start = ((bf16[128,264,128]{2,1,0:T(8,128)(2,1)}), bf16[128,264,128]{2,1,0:T(8,128)(2,1)}, u32[]{:S(2)}, u32[]{:S(2)}) async-start(bf16[128,264,128]{2,1,0:T(8,128)(2,1)} %shard_map.85), calls=%async_computation | async-start | bytes 17301504 | tf_op jit(solution)/shard_map/all_to_all | solution.py:514

commit v4 on v3

--- a/solution.py
+++ b/solution.py
@@ -19,33 +19,30 @@
 TROWS = ROWS + 2 * NEAR
 EDGE = 2 * WIDE
 PER_GROUP = COLS // EDGE
-TILE_STEP = 2
+TILE_STEP = 4
 SOURCE_STEP = 8
 SUMS = 2
 MARK_ROWS = 8
 OUT_PARTS = 4
-VMEM_LIMIT = 60 * 1024 * 1024
-
-
-def params(*semantics):
-    return pltpu.CompilerParams(
-        dimension_semantics=semantics or None, vmem_limit_bytes=VMEM_LIMIT
-    )
+
+
+def params(mebibytes):
+    return pltpu.CompilerParams(vmem_limit_bytes=mebibytes * 1024 * 1024)
 
 
 def remap_kernel(
-    first, tiles, final, device_ref, block_ref, flux_hbm, weight_hbm, *refs
+    device_ref, block_ref, flux_hbm, weight_hbm, out_hbm, flux_buf, weight_buf, held, marks, sent,
+    flux_sems, weight_sems, out_sem, mark_sem, counts,
 ):
-    out_hbm, flux_buf, weight_buf, held, marks, sent, flux_sems, weight_sems, out_sem, mark_sem, counts = refs[-11:]
+    tiles = flux_hbm.shape[0]
     links, rows = weight_hbm.shape[1], flux_hbm.shape[1]
     groups = tiles // TILE_STEP
 
     def loads(group):
         at = pl.ds(group * TILE_STEP, TILE_STEP)
-        source = pl.ds(first + group * TILE_STEP, TILE_STEP)
         return (
-            pltpu.make_async_copy(flux_hbm.at[source], flux_buf.at[at], flux_sems.at[group]),
-            pltpu.make_async_copy(weight_hbm.at[source], weight_buf.at[at], weight_sems.at[group]),
+            pltpu.make_async_copy(flux_hbm.at[at], flux_buf.at[at], flux_sems.at[group]),
+            pltpu.make_async_copy(weight_hbm.at[at], weight_buf.at[at], weight_sems.at[group]),
         )
 
     for group in range(groups):
@@ -57,24 +54,15 @@
         return carry
 
     lax.fori_loop(0, counts.shape[0], clear, 0, unroll=8)
-    if final:
-        marks[...] = jnp.full(marks.shape, BLK_DEV, jnp.float32)
+    marks[...] = jnp.full(marks.shape, BLK_DEV, jnp.float32)
 
     def place(tile, link):
         owner = device_ref[link, tile]
         rank = counts[owner]
         counts[owner] = rank + 1
-        if final:
-            value = block_ref[link, tile].astype(jnp.float32)
-            marks[owner, pl.ds(rank, 1), :] = jnp.full((1, COLS), value, jnp.float32)
+        value = block_ref[link, tile].astype(jnp.float32)
+        marks[owner, pl.ds(rank, 1), :] = jnp.full((1, COLS), value, jnp.float32)
         return owner, pl.ds(pl.multiple_of(rank * rows, rows), rows)
-
-    def earlier(tile, carry):
-        for link in range(links):
-            place(tile, link)
-        return carry
-
-    lax.fori_loop(0, first, earlier, 0)
 
     def work(group, carry):
         for load in loads(group):
@@ -94,37 +82,32 @@
         for part in range(TILE_STEP):
             at = group * TILE_STEP + part
             for link in range(links):
-                owner, into = place(first + at, link)
+                owner, into = place(at, link)
                 source = held.at[at * (links // 2) + link // 2, pl.ds(link % 2 * rows, rows)]
                 pltpu.make_async_copy(source, out_hbm.at[owner, into], out_sem).start()
         return carry
 
     lax.fori_loop(0, groups, work, 0)
-    if final:
-        sent[...] = marks[...].astype(jnp.bfloat16)
-        last = pltpu.make_async_copy(
-            sent, out_hbm.at[:, pl.ds(CAP * rows, MARK_ROWS)], mark_sem
-        )
-        last.start()
-        last.wait()
+    sent[...] = marks[...].astype(jnp.bfloat16)
+    last = pltpu.make_async_copy(sent, out_hbm.at[:, pl.ds(CAP * rows, MARK_ROWS)], mark_sem)
+    last.start()
+    last.wait()
     everything = out_hbm.at[pl.ds(0, tiles * links // 2), pl.ds(0, 2 * rows)]
     pltpu.make_async_copy(held, everything, out_sem).wait()
 
 
-def remap(fluxes, remap_weights, target_device, target_block, devices, first, tiles, chunks=None):
-    rows, cells = fluxes.shape[1:]
+def remap(fluxes, remap_weights, target_device, target_block, devices):
+    tiles, rows, cells = fluxes.shape
     links, cols = remap_weights.shape[1], remap_weights.shape[3]
-    final = chunks is not None
     anywhere = pl.BlockSpec(memory_space=pl.ANY)
-    inputs = (target_device.T, target_block.T, fluxes, remap_weights) + ((chunks,) if final else ())
     groups = tiles // TILE_STEP
     return pl.pallas_call(
-        functools.partial(remap_kernel, first, tiles, final),
-        in_specs=[pl.BlockSpec(memory_space=pltpu.SMEM)] * 2 + [anywhere] * (3 if final else 2),
+        remap_kernel,
+        in_specs=[pl.BlockSpec(memory_space=pltpu.SMEM)] * 2 + [anywhere] * 2,
         out_specs=anywhere,
         scratch_shapes=[
-            pltpu.VMEM((tiles, rows, cells), jnp.bfloat16),
-            pltpu.VMEM((tiles, links, cells, cols), jnp.bfloat16),
+            pltpu.VMEM(fluxes.shape, jnp.bfloat16),
+            pltpu.VMEM(remap_weights.shape, jnp.bfloat16),
             pltpu.VMEM((tiles * links // 2, 2 * rows, cols), jnp.bfloat16),
             pltpu.VMEM((devices, MARK_ROWS, cols), jnp.float32),
             pltpu.VMEM((devices, MARK_ROWS, cols), jnp.bfloat16),
@@ -135,9 +118,8 @@
             pltpu.SMEM((devices,), jnp.int32),
         ],
         out_shape=jax.ShapeDtypeStruct((devices, CAP * rows + MARK_ROWS, cols), jnp.bfloat16),
-        input_output_aliases={4: 0} if final else {},
-        compiler_params=params(),
-    )(*inputs)
+        compiler_params=params(60),
+    )(target_device.T, target_block.T, fluxes, remap_weights)
 
 
 def wind_piece(winds_ref, row, comp):
@@ -151,13 +133,19 @@
 
 WIND_MSG = WIDE * 3 * LEV
 TRACER_MSG = NEAR * LEV * NTR
-TRACER_EDGE = WIND_MSG + TRACER_MSG
-WIND_EDGE = TRACER_EDGE + NEAR * 8
-MSG = WIND_EDGE + 3 * 8
-EDGE_ROWS = (ROWS + 3) * 8
-
-
-def edge_cols_kernel(tracers_ref, winds_ref, edge_ref):
+MSG = WIND_MSG + TRACER_MSG
+EDGE_ROWS = (NTR + LEV) * 8
+LOADS = 8
+
+
+def pack_kernel(tracers_hbm, winds_hbm, edge_ref, top_ref, bottom_ref, tracers_ref, winds_ref, sems):
+    share = NTR * LEV * ROWS // LOADS
+    loads = [pltpu.make_async_copy(winds_hbm, winds_ref, sems.at[LOADS])]
+    for part in range(LOADS):
+        at = pl.ds(part * share, share)
+        loads.append(pltpu.make_async_copy(tracers_hbm.at[at], tracers_ref.at[at], sems.at[part]))
+    for load in loads:
+        load.start()
     group_of = lax.broadcasted_iota(jnp.int32, (8, COLS), 1) // EDGE
 
     def packed(pieces):
@@ -167,28 +155,19 @@
             held = jnp.where(group_of == spot, turned, held)
         return held
 
-    def tracer_row(row, carry):
-        pieces = [tracer_piece(tracers_ref, row, spot // 2, spot % 2) for spot in range(PER_GROUP)]
-        edge_ref[pl.ds(pl.multiple_of(row * 8, 8), 8), :] = packed(pieces)
-        return carry
-
-    lax.fori_loop(0, ROWS, tracer_row, 0)
-    for comp in range(3):
-        at = (ROWS + comp) * 8
-        edge_ref[at : at + 8, :] = packed([wind_piece(winds_ref, row, comp) for row in range(ROWS)])
-
-
-def edge_cols(tracers, winds):
-    return pl.pallas_call(
-        edge_cols_kernel,
-        out_shape=jax.ShapeDtypeStruct((EDGE_ROWS, COLS), jnp.float32),
-        compiler_params=params(),
-    )(tracers, winds)
-
-
-def edge_rows_kernel(tracers_ref, winds_ref, left_ref, right_ref, top_ref, bottom_ref, both_ref):
-    lane = lax.broadcasted_iota(jnp.int32, (EDGE_ROWS, COLS), 1)
-    both_ref[...] = jnp.where(lax.rem(lane, EDGE) < WIDE, left_ref[...], right_ref[...])
+    loads[0].wait()
+    for level in range(LEV):
+        starts = [
+            comp * LEV * ROWS + level * ROWS + half * 8 for comp in range(3) for half in range(2)
+        ]
+        at = (NTR + level) * 8
+        edge_ref[at : at + 8, :] = packed([winds_ref[start : start + 8, :] for start in starts])
+    for tracer in range(NTR):
+        if tracer % (NTR // LOADS) == 0:
+            loads[1 + tracer // (NTR // LOADS)].wait()
+        starts = [tracer * LEV * ROWS + spot * 8 for spot in range(PER_GROUP)]
+        at = tracer * 8
+        edge_ref[at : at + 8, :] = packed([tracers_ref[start : start + 8, :] for start in starts])
     for target, wind_from, tracer_from in (
         (top_ref, 0, 0),
         (bottom_ref, ROWS - WIDE, ROWS - NEAR),
@@ -204,17 +183,22 @@
                     target[at : at + 8, :] = tracer_piece(
                         tracers_ref, tracer_from + row, level, half
                     )
-        target[TRACER_EDGE:WIND_EDGE, :] = both_ref[tracer_from * 8 : (tracer_from + NEAR) * 8, :]
-        target[WIND_EDGE:MSG, :] = both_ref[ROWS * 8 : EDGE_ROWS, :]
-
-
-def edge_rows(tracers, winds, left, right):
-    shape = jax.ShapeDtypeStruct((MSG, COLS), jnp.float32)
+
+
+def pack(tracers, winds):
+    shapes = [jax.ShapeDtypeStruct((rows, COLS), jnp.float32) for rows in (EDGE_ROWS, MSG, MSG)]
     return pl.pallas_call(
-        edge_rows_kernel,
-        out_shape=[shape, shape, jax.ShapeDtypeStruct((EDGE_ROWS, COLS), jnp.float32)],
-        compiler_params=params(),
-    )(tracers, winds, left, right)
+        pack_kernel,
+        in_specs=[pl.BlockSpec(memory_space=pl.ANY)] * 2,
+        out_specs=[pl.BlockSpec(memory_space=pltpu.VMEM)] * 3,
+        out_shape=shapes,
+        scratch_shapes=[
+            pltpu.VMEM(tracers.shape, jnp.float32),
+            pltpu.VMEM(winds.shape, jnp.float32),
+            pltpu.SemaphoreType.DMA((LOADS + 1,)),
+        ],
+        compiler_params=params(60),
+    )(tracers, winds)
 
 
 def cubic_weights(frac):
@@ -271,25 +255,35 @@
 
 
 def advect_kernel(
-    tracers_ref, low_ref, high_ref, both_ref, first_ref, second_ref, winds_ref, out_ref,
-    wind_taps, tracer_taps, spread_ref,
+    tracers_ref, low_ref, high_ref, left_ref, right_ref, low_left_ref, low_right_ref,
+    high_left_ref, high_right_ref, first_ref, second_ref, winds_ref, out_ref,
+    own_edge, low_edge, high_edge, wind_taps, tracer_taps, spread_ref,
 ):
-    def edge_piece(ref, at, spot):
-        return pltpu.roll(ref[pl.ds(at, 8), :], (COLS - WIDE - EDGE * spot) % COLS, 1)
+    lane = lax.broadcasted_iota(jnp.int32, (EDGE_ROWS, COLS), 1)
+    from_left = lax.rem(lane, EDGE) < WIDE
+    own_edge[...] = jnp.where(from_left, left_ref[...], right_ref[...])
+    low_edge[...] = jnp.where(from_left, low_left_ref[...], low_right_ref[...])
+    high_edge[...] = jnp.where(from_left, high_left_ref[...], high_right_ref[...])
+
+    def edge_piece(ref, start, spot):
+        return pltpu.roll(ref[pl.ds(start, 8, stride=8), :], (COLS - WIDE - EDGE * spot) % COLS, 1)
+
+    def wind_edge(ref, row, comp):
+        return edge_piece(ref, NTR * 8 + row % 8, comp * 2 + row // 8)
 
     for comp in range(3):
         for row in range(WROWS):
             if row < WIDE:
                 at = (row * 3 + comp) * LEV
                 main = low_ref[at : at + LEV, :]
-                edge = edge_piece(low_ref, WIND_EDGE + comp * 8, ROWS - WIDE + row)
+                edge = wind_edge(low_edge, ROWS - WIDE + row, comp)
             elif row < WIDE + ROWS:
                 main = wind_piece(winds_ref, row - WIDE, comp)
-                edge = edge_piece(both_ref, (ROWS + comp) * 8, row - WIDE)
+                edge = wind_edge(own_edge, row - WIDE, comp)
             else:
                 at = ((row - WIDE - ROWS) * 3 + comp) * LEV
                 main = high_ref[at : at + LEV, :]
-                edge = edge_piece(high_ref, WIND_EDGE + comp * 8, row - WIDE - ROWS)
+                edge = wind_edge(high_edge, row - WIDE - ROWS, comp)
             shifted = column_shifts(main, edge, WIDE)
             for side in range(W_TAPS):
                 for above in range(L_TAPS):
@@ -335,25 +329,32 @@
 
     lax.fori_loop(0, ROWS, wind_row, 0)
 
-    def own_shifts(row, carry):
+    def keep_shifts(main_of, ref, onto, within, upper):
         for spot in range(PER_GROUP):
-            main = tracer_piece(tracers_ref, row, spot // 2, spot % 2)
-            edge = edge_piece(both_ref, pl.multiple_of(row * 8, 8), spot)
-            shifted = column_shifts(main, edge, NEAR)
+            level, half = spot // 2, spot % 2
+            edge = edge_piece(ref, half * 64 + within, level * 2 + upper)
+            shifted = column_shifts(main_of(level, half), edge, NEAR)
             for side in range(T_TAPS):
-                tracer_taps[row + NEAR, spot, side] = shifted[side]
-        return carry
-
-    lax.fori_loop(0, ROWS, own_shifts, 0)
-    for ref, onto in ((low_ref, 0), (high_ref, NEAR + ROWS)):
-
-        def halo_shifts(row, carry, ref=ref, onto=onto):
-            for spot in range(PER_GROUP):
-                at = pl.multiple_of(WIND_MSG + row * LEV * NTR + spot * 8, 8)
-                edge = edge_piece(ref, pl.multiple_of(TRACER_EDGE + row * 8, 8), spot)
-                shifted = column_shifts(ref[pl.ds(at, 8), :], edge, NEAR)
-                for side in range(T_TAPS):
-                    tracer_taps[row + onto, spot, side] = shifted[side]
+                tracer_taps[onto, spot, side] = shifted[side]
+
+    for upper in range(2):
+
+        def own_shifts(within, carry, upper=upper):
+            row = upper * 8 + within
+            main_of = functools.partial(tracer_piece, tracers_ref, row)
+            keep_shifts(main_of, own_edge, row + NEAR, within, upper)
+            return carry
+
+        lax.fori_loop(0, 8, own_shifts, 0)
+    for ref, edges, onto, upper in ((low_ref, low_edge, 0, 1), (high_ref, high_edge, NEAR + ROWS, 0)):
+
+        def halo_shifts(row, carry, ref=ref, edges=edges, onto=onto, upper=upper):
+            def main_of(level, half):
+                at = WIND_MSG + row * LEV * NTR + level * NTR + half * 8
+                return ref[pl.ds(pl.multiple_of(at, 8), 8), :]
+
+            within = row + (8 - NEAR if upper else 0)
+            keep_shifts(main_of, edges, row + onto, within, upper)
             return carry
 
         lax.fori_loop(0, NEAR, halo_shifts, 0)
@@ -388,17 +389,20 @@
     lax.fori_loop(0, ROWS * LEV, tracer_cell, 0)
 
 
-def advect(tracers, low, high, both, first, second, winds):
+def advect(tracers, low, high, edges, first, second, winds):
     return pl.pallas_call(
         advect_kernel,
+        in_specs=[pl.BlockSpec(memory_space=pltpu.VMEM)] * (6 + len(edges)),
+        out_specs=pl.BlockSpec(memory_space=pltpu.VMEM),
         out_shape=jax.ShapeDtypeStruct((NTR * LEV * ROWS, COLS), jnp.float32),
-        scratch_shapes=[
+        scratch_shapes=[pltpu.VMEM((EDGE_ROWS, COLS), jnp.float32)] * 3
+        + [
             pltpu.VMEM((WROWS, 3, L_TAPS, W_TAPS, LEV, COLS), jnp.float32),
             pltpu.VMEM((TROWS, LEV * 2, T_TAPS, 8, COLS), jnp.float32),
             pltpu.VMEM((ROWS, SPREADS, LEV, COLS), jnp.float32),
         ],
-        compiler_params=params(),
-    )(tracers, low, high, both, first, second, winds)
+        compiler_params=params(60),
+    )(tracers, low, high, *edges, first, second, winds)
 
 
 def combine_kernel(
@@ -471,25 +475,26 @@
         ]
         + [pltpu.VMEM(((BLK_DEV + 1) * rows, cols), jnp.float32)] * SUMS,
         out_shape=jax.ShapeDtypeStruct(moved.shape, jnp.float32),
-        compiler_params=params(),
+        compiler_params=params(60),
     )(arrived, moved)
 
 
-def side_columns(tracers, winds):
-    lon_count = lax.axis_size("lon")
-    edge = edge_cols(tracers, winds)
-    around = [(i, (i + 1) % lon_count) for i in range(lon_count)]
-    left = lax.ppermute(edge, "lon", around)
-    right = lax.ppermute(edge, "lon", [(b, a) for a, b in around])
-    return left, right
-
-
-def outer_rows(top, bottom):
-    lat_count = lax.axis_size("lat")
-    up = [(i, i + 1) for i in range(lat_count - 1)]
-    low = lax.ppermute(bottom, "lat", up)
-    high = lax.ppermute(top, "lat", [(b, a) for a, b in up])
-    return low, high
+def halos(packed):
+    edge, top, bottom = packed
+    lats, lons = lax.axis_size("lat"), lax.axis_size("lon")
+
+    def received(value, lat_step, lon_step):
+        pairs = []
+        for lat in range(lats):
+            for lon in range(lons):
+                if 0 <= lat + lat_step < lats:
+                    source = (lat + lat_step) * lons + (lon + lon_step) % lons
+                    pairs.append((source, lat * lons + lon))
+        return lax.ppermute(value, ("lat", "lon"), pairs)
+
+    low, high = received(bottom, -1, 0), received(top, 1, 0)
+    edges = [received(edge, lat, lon) for lat in (0, -1, 1) for lon in (-1, 1)]
+    return low, high, edges
 
 
 def body(
@@ -500,19 +505,11 @@
     tracers, winds, depart_first, depart_second = (
         field.reshape(-1, COLS) for field in (tracers, winds, depart_first, depart_second)
     )
-    tiles = fluxes.shape[0]
-    half = tiles // 2
-    emission = (fluxes, remap_weights, target_device, target_block, devices)
-    left, right = side_columns(tracers, winds)
-    chunks = remap(*emission, 0, half)
-    chunks, left, right = lax.optimization_barrier((chunks, left, right))
-    top, bottom, both = edge_rows(tracers, winds, left, right)
-    chunks, top, bottom = lax.optimization_barrier((chunks, top, bottom))
-    low, high = outer_rows(top, bottom)
-    chunks = remap(*emission, half, tiles - half, chunks)
-    chunks, low, high = lax.optimization_barrier((chunks, low, high))
+    low, high, edges = halos(pack(tracers, winds))
+    chunks = remap(fluxes, remap_weights, target_device, target_block, devices)
+    chunks, low, high, edges = lax.optimization_barrier((chunks, low, high, edges))
     arrived = lax.all_to_all(chunks, ("lat", "lon"), split_axis=0, concat_axis=0, tiled=True)
-    moved = advect(tracers, low, high, both, depart_first, depart_second, winds)
+    moved = advect(tracers, low, high, edges, depart_first, depart_second, winds)
     return combine(arrived, moved).reshape(shape)
 
 

time: 158 us -> 167 us (1.057)
  starting transfers between devices: 21 us -> 34.4 us
  Pallas kernels: 69.8 us -> 64.3 us
    ppermute x4 -> x8, starting transfers between devices: 7.58 us -> 21 us  [received(): return lax.ppermute(value, ('lat', 'lon'), pairs)]
    pallas_call x5 -> x3, Pallas kernels: 63.9 us -> 58.4 us  [the longest x1 46.3 us: advect(): pl.pallas_call(advect_kernel, in_specs=[pl.BlockSpec(memory_space=pltpu.V...]
  transfers between devices with their start and end apart: 5 -> 9, of which waited for: 1 -> 2; matrix products, arithmetic and copies ran while one was open for 0% -> 0% of each run, Pallas kernels for 37% -> 34%
where the time goes in v4:
time: 167 us; the launch traced here: 165 us
  waiting for transfers between devices  65 us (39%)
  Pallas kernels  64.3 us (39%)
  starting transfers between devices  34.4 us (21%)
    all_to_all x1, waiting for transfers between devices, body(): lax.all_to_all(chunks, ('lat', 'lon'), split_axis=0, concat_axis=0, tiled...  64.2 us
    pallas_call x1, Pallas kernels, advect(): pl.pallas_call(advect_kernel, in_specs=[pl.BlockSpec(memory_space=pltpu.V...  46.3 us
    ppermute x8, starting transfers between devices, received(): return lax.ppermute(value, ('lat', 'lon'), pairs)  21 us
    all_to_all x1, starting transfers between devices, body(): lax.all_to_all(chunks, ('lat', 'lon'), split_axis=0, concat_axis=0, tiled...  13.4 us
    pallas_call x1, Pallas kernels, remap(): pl.pallas_call(remap_kernel, in_specs=[pl.BlockSpec(memory_space=pltpu.SM...  9.32 us
    pallas_call x1, Pallas kernels, combine(): pl.pallas_call(combine_kernel, in_specs=[anywhere] * 2, out_specs=anywher...  5.87 us
  transfers between devices with their start and end apart: 9, of which 2 were waited for; matrix products, arithmetic and copies ran while one was open for 0% of the time, Pallas kernels for 34%

profile of v4, /device:TPU:36, one launch (start us, length us, event | category | flops | bytes accessed | tf_op | source)
XLA Modules:
  0.0 164.7 jit_solution(14523890843708724007)
XLA Ops:
  0.0 2.8 %shard_map.83 = (f32[192,128]{1,0:T(8,128)}, f32[480,128]{1,0:T(8,128)}, f32[480,128]{1,0:T(8,128)}) custom-call(f32[2048,128]{1,0:T(8,128)} %bitcast.7, f32[384,128]{1,0:T(8,128)} %bitcast.9), custom_call_target="tpu_custom_call" | custom-call | tf_op jit(solution)/shard_map/pallas_call | solution.py:190
  2.8 1.9 %collective-permute-start = (f32[480,128]{1,0:T(8,128)}, f32[480,128]{1,0:T(8,128)S(1)}, u32[]{:S(2)}, u32[]{:S(2)}) collective-permute-start(f32[480,128]{1,0:T(8,128)} %get-tuple-element.17), channel_id=1, source_target_pairs={{0,16},{1,17},{2,18},{3,19},{4,20},{5,21},{6,22},{7,23},{8,24},{9,... | collective-permute-start | bytes 737288 | tf_op jit(solution)/shard_map/ppermute | solution.py:493
  4.7 3.6 %collective-permute-start.1 = (f32[480,128]{1,0:T(8,128)}, f32[480,128]{1,0:T(8,128)S(1)}, u32[]{:S(2)}, u32[]{:S(2)}) collective-permute-start(f32[480,128]{1,0:T(8,128)} %get-tuple-element.18), channel_id=1, source_target_pairs={{16,0},{17,1},{18,2},{19,3},{20,4},{21,5},{22,6},{23,7},{24,8},{25... | collective-permute-start | bytes 737288 | tf_op jit(solution)/shard_map/ppermute | solution.py:493
  8.4 1.3 collective-permute-start.2
  9.7 0.8 collective-permute-start.3
  10.5 2.4 %collective-permute-start.4 = (f32[192,128]{1,0:T(8,128)}, f32[192,128]{1,0:T(8,128)S(1)}, u32[]{:S(2)}, u32[]{:S(2)}) collective-permute-start(f32[192,128]{1,0:T(8,128)} %get-tuple-element.19), channel_id=1, source_target_pairs={{15,16},{0,17},{1,18},{2,19},{3,20},{4,21},{5,22},{6,23},{7,24},{8... | collective-permute-start | bytes 294920 | tf_op jit(solution)/shard_map/ppermute | solution.py:493
  12.9 0.7 collective-permute-done.2.left_ref
  13.7 0.0 copy-start.2
  13.7 3.7 %collective-permute-start.5 = (f32[192,128]{1,0:T(8,128)}, f32[192,128]{1,0:T(8,128)S(1)}, u32[]{:S(2)}, u32[]{:S(2)}) collective-permute-start(f32[192,128]{1,0:T(8,128)} %get-tuple-element.19), channel_id=1, source_target_pairs={{1,16},{2,17},{3,18},{4,19},{5,20},{6,21},{7,22},{8,23},{9,24},{10... | collective-permute-start | bytes 294920 | tf_op jit(solution)/shard_map/ppermute | solution.py:493
  17.4 0.0 collective-permute-done.3.right_ref
  17.4 0.0 copy-start.3
  17.4 4.2 %collective-permute-start.6 = (f32[192,128]{1,0:T(8,128)}, f32[192,128]{1,0:T(8,128)S(1)}, u32[]{:S(2)}, u32[]{:S(2)}) collective-permute-start(f32[192,128]{1,0:T(8,128)} %get-tuple-element.19), channel_id=1, source_target_pairs={{31,0},{16,1},{17,2},{18,3},{19,4},{20,5},{21,6},{22,7},{23,8},{24... | collective-permute-start | bytes 294920 | tf_op jit(solution)/shard_map/ppermute | solution.py:493
  21.7 0.0 collective-permute-done.4.low_left_ref
  21.7 0.0 copy-start.4
  21.7 2.9 %collective-permute-start.7 = (f32[192,128]{1,0:T(8,128)}, f32[192,128]{1,0:T(8,128)S(1)}, u32[]{:S(2)}, u32[]{:S(2)}) collective-permute-start(f32[192,128]{1,0:T(8,128)} %get-tuple-element.19), channel_id=1, source_target_pairs={{17,0},{18,1},{19,2},{20,3},{21,4},{22,5},{23,6},{24,7},{25,8},{26... | collective-permute-start | bytes 294920 | tf_op jit(solution)/shard_map/ppermute | solution.py:493
  24.6 9.3 %shard_map.82 = bf16[128,264,128]{2,1,0:T(8,128)(2,1)} custom-call(s32[4,48]{1,0:T(4,128)} %bitcast.13, s32[4,48]{1,0:T(4,128)} %bitcast.14, bf16[48,128,256]{2,1,0:T(8,128)(2,1)} %flux_hbm.1, bf16[48,4,256,128]{3,2,1,0:T(8,128)(2,1)} %weight_hbm.1), custom_call_target="tpu_custom_call" | custom-call | tf_op jit(solution)/shard_map/pallas_call | solution.py:104
  34.0 0.0 copy-done.2
  34.0 0.0 copy-done.3
  34.0 0.0 copy-done.4
  34.0 0.0 collective-permute-done.5.low_right_ref
  34.0 0.0 copy-start.5
  34.0 0.0 collective-permute-done.6.high_left_ref
  34.0 0.0 copy-start.6
  34.0 0.0 collective-permute-done.7.high_right_ref
  34.0 0.0 copy-start.7
  34.0 0.0 collective-permute-done.low_ref
  34.1 0.0 copy-start
  34.1 0.0 collective-permute-done.1.high_ref
  34.1 0.0 copy-start.1
  34.1 0.5 copy-done.5
  34.6 0.0 copy-done.6
  34.7 0.0 copy-done.7
  34.7 0.1 copy-done
  34.8 0.1 copy-done.1
  34.9 13.4 %all-to-all-start = ((bf16[128,264,128]{2,1,0:T(8,128)(2,1)}), bf16[128,264,128]{2,1,0:T(8,128)(2,1)}, u32[]{:S(2)}, u32[]{:S(2)}) async-start(bf16[128,264,128]{2,1,0:T(8,128)(2,1)} %shard_map.82), calls=%async_computation | async-start | bytes 17301504 | tf_op jit(solution)/shard_map/all_to_all | solution.py:511
  48.3 46.3 %shard_map.84.moved_hbm = f32[2048,128]{1,0:T(8,128)} custom-call(f32[2048,128]{1,0:T(8,128)} %bitcast.8, f32[480,128]{1,0:T(8,128)} %copy-done, f32[480,128]{1,0:T(8,128)} %copy-done.1, f32[192,128]{1,0:T(8,128)} %copy-done.2, f32[192,128]{1,0:T(8,128)} %copy-done.3, f32[192,128]{1,0:T(8,128)} %copy-done.4, f32[192,128]{1,0:T(8,128)} %copy-done.5, ...), custom_call_target="tpu_custom_call" | custom-call | tf_op jit(solution)/shard_map/pallas_call | solution.py:393
  94.6 64.2 %all-to-all-done.arrived_hbm = bf16[128,264,128]{2,1,0:T(8,128)(2,1)} async-done(((bf16[128,264,128]{2,1,0:T(8,128)(2,1)}), bf16[128,264,128]{2,1,0:T(8,128)(2,1)}, u32[]{:S(2)}, u32[]{:S(2)}) %all-to-all-start) | async-done | bytes 8650784 | tf_op jit(solution)/shard_map/all_to_all | solution.py:511
  158.8 5.9 %shard_map.85 = f32[2048,128]{1,0:T(8,128)} custom-call(bf16[128,264,128]{2,1,0:T(8,128)(2,1)} %all-to-all-done.arrived_hbm, f32[2048,128]{1,0:T(8,128)} %shard_map.84.moved_hbm), custom_call_target="tpu_custom_call" | custom-call | tf_op jit(solution)/shard_map/pallas_call | solution.py:464
Async XLA Ops:
  2.8 31.2 %collective-permute-start = (f32[480,128]{1,0:T(8,128)}, f32[480,128]{1,0:T(8,128)S(1)}, u32[]{:S(2)}, u32[]{:S(2)}) collective-permute-start(f32[480,128]{1,0:T(8,128)} %get-tuple-element.17), channel_id=1, source_target_pairs={{0,16},{1,17},{2,18},{3,19},{4,20},{5,21},{6,22},{7,23},{8,24},{9,... | collective-permute-start | bytes 737288 | tf_op jit(solution)/shard_map/ppermute | solution.py:493
  4.7 29.3 %collective-permute-start.1 = (f32[480,128]{1,0:T(8,128)}, f32[480,128]{1,0:T(8,128)S(1)}, u32[]{:S(2)}, u32[]{:S(2)}) collective-permute-start(f32[480,128]{1,0:T(8,128)} %get-tuple-element.18), channel_id=1, source_target_pairs={{16,0},{17,1},{18,2},{19,3},{20,4},{21,5},{22,6},{23,7},{24,8},{25... | collective-permute-start | bytes 737288 | tf_op jit(solution)/shard_map/ppermute | solution.py:493
  8.4 5.3 %collective-permute-start.2 = (f32[192,128]{1,0:T(8,128)}, f32[192,128]{1,0:T(8,128)S(1)}, u32[]{:S(2)}, u32[]{:S(2)}) collective-permute-start(f32[192,128]{1,0:T(8,128)} %get-tuple-element.19), channel_id=1, source_target_pairs={{15,0},{0,1},{1,2},{2,3},{3,4},{4,5},{5,6},{6,7},{7,8},{8,9},{9,10... | collective-permute-start | bytes 294920 | tf_op jit(solution)/shard_map/ppermute | solution.py:493
  9.7 7.8 %collective-permute-start.3 = (f32[192,128]{1,0:T(8,128)}, f32[192,128]{1,0:T(8,128)S(1)}, u32[]{:S(2)}, u32[]{:S(2)}) collective-permute-start(f32[192,128]{1,0:T(8,128)} %get-tuple-element.19), channel_id=1, source_target_pairs={{1,0},{2,1},{3,2},{4,3},{5,4},{6,5},{7,6},{8,7},{9,8},{10,9},{11,1... | collective-permute-start | bytes 294920 | tf_op jit(solution)/shard_map/ppermute | solution.py:493
  10.5 11.2 %collective-permute-start.4 = (f32[192,128]{1,0:T(8,128)}, f32[192,128]{1,0:T(8,128)S(1)}, u32[]{:S(2)}, u32[]{:S(2)}) collective-permute-start(f32[192,128]{1,0:T(8,128)} %get-tuple-element.19), channel_id=1, source_target_pairs={{15,16},{0,17},{1,18},{2,19},{3,20},{4,21},{5,22},{6,23},{7,24},{8... | collective-permute-start | bytes 294920 | tf_op jit(solution)/shard_map/ppermute | solution.py:493
  13.7 20.3 %copy-start.2 = (f32[192,128]{1,0:T(8,128)}, f32[192,128]{1,0:T(8,128)S(1)}, u32[]{:S(2)}) copy-start(f32[192,128]{1,0:T(8,128)S(1)} %collective-permute-done.2.left_ref) | copy-start | bytes 294916
  13.7 20.3 %collective-permute-start.5 = (f32[192,128]{1,0:T(8,128)}, f32[192,128]{1,0:T(8,128)S(1)}, u32[]{:S(2)}, u32[]{:S(2)}) collective-permute-start(f32[192,128]{1,0:T(8,128)} %get-tuple-element.19), channel_id=1, source_target_pairs={{1,16},{2,17},{3,18},{4,19},{5,20},{6,21},{7,22},{8,23},{9,24},{10... | collective-permute-start | bytes 294920 | tf_op jit(solution)/shard_map/ppermute | solution.py:493
  17.4 16.5 %copy-start.3 = (f32[192,128]{1,0:T(8,128)}, f32[192,128]{1,0:T(8,128)S(1)}, u32[]{:S(2)}) copy-start(f32[192,128]{1,0:T(8,128)S(1)} %collective-permute-done.3.right_ref) | copy-start | bytes 294916
  17.4 16.6 %collective-permute-start.6 = (f32[192,128]{1,0:T(8,128)}, f32[192,128]{1,0:T(8,128)S(1)}, u32[]{:S(2)}, u32[]{:S(2)}) collective-permute-start(f32[192,128]{1,0:T(8,128)} %get-tuple-element.19), channel_id=1, source_target_pairs={{31,0},{16,1},{17,2},{18,3},{19,4},{20,5},{21,6},{22,7},{23,8},{24... | collective-permute-start | bytes 294920 | tf_op jit(solution)/shard_map/ppermute | solution.py:493
  21.7 12.3 %copy-start.4 = (f32[192,128]{1,0:T(8,128)}, f32[192,128]{1,0:T(8,128)S(1)}, u32[]{:S(2)}) copy-start(f32[192,128]{1,0:T(8,128)S(1)} %collective-permute-done.4.low_left_ref) | copy-start | bytes 294916
  21.7 12.3 %collective-permute-start.7 = (f32[192,128]{1,0:T(8,128)}, f32[192,128]{1,0:T(8,128)S(1)}, u32[]{:S(2)}, u32[]{:S(2)}) collective-permute-start(f32[192,128]{1,0:T(8,128)} %get-tuple-element.19), channel_id=1, source_target_pairs={{17,0},{18,1},{19,2},{20,3},{21,4},{22,5},{23,6},{24,7},{25,8},{26... | collective-permute-start | bytes 294920 | tf_op jit(solution)/shard_map/ppermute | solution.py:493
  34.0 0.6 copy-start.5
  34.0 0.7 copy-start.6
  34.0 0.7 copy-start.7
  34.1 0.8 copy-start
  34.1 0.8 copy-start.1
  34.9 124.0 %all-to-all-start = ((bf16[128,264,128]{2,1,0:T(8,128)(2,1)}), bf16[128,264,128]{2,1,0:T(8,128)(2,1)}, u32[]{:S(2)}, u32[]{:S(2)}) async-start(bf16[128,264,128]{2,1,0:T(8,128)(2,1)} %shard_map.82), calls=%async_computation | async-start | bytes 17301504 | tf_op jit(solution)/shard_map/all_to_all | solution.py:511

commit v5 on v4

--- a/solution.py
+++ b/solution.py
@@ -138,7 +138,7 @@
 LOADS = 8
 
 
-def pack_kernel(tracers_hbm, winds_hbm, edge_ref, top_ref, bottom_ref, tracers_ref, winds_ref, sems):
+def pack_kernel(tracers_hbm, winds_hbm, edge_ref, tracers_ref, winds_ref, sems):
     share = NTR * LEV * ROWS // LOADS
     loads = [pltpu.make_async_copy(winds_hbm, winds_ref, sems.at[LOADS])]
     for part in range(LOADS):
@@ -168,6 +168,30 @@
         starts = [tracer * LEV * ROWS + spot * 8 for spot in range(PER_GROUP)]
         at = tracer * 8
         edge_ref[at : at + 8, :] = packed([tracers_ref[start : start + 8, :] for start in starts])
+
+
+def pack(tracers, winds):
+    return pl.pallas_call(
+        pack_kernel,
+        in_specs=[pl.BlockSpec(memory_space=pl.ANY)] * 2,
+        out_specs=pl.BlockSpec(memory_space=pltpu.VMEM),
+        out_shape=jax.ShapeDtypeStruct((EDGE_ROWS, COLS), jnp.float32),
+        scratch_shapes=[
+            pltpu.VMEM(tracers.shape, jnp.float32),
+            pltpu.VMEM(winds.shape, jnp.float32),
+            pltpu.SemaphoreType.DMA((LOADS + 1,)),
+        ],
+        compiler_params=params(60),
+    )(tracers, winds)
+
+
+def merged_edges(left, right):
+    lane = lax.broadcasted_iota(jnp.int32, left.shape, 1)
+    return jnp.where(lax.rem(lane, EDGE) < WIDE, left, right)
+
+
+def rows_kernel(tracers_ref, winds_ref, left_ref, right_ref, top_ref, bottom_ref):
+    both = merged_edges(left_ref[...], right_ref[...])
     for target, wind_from, tracer_from in (
         (top_ref, 0, 0),
         (bottom_ref, ROWS - WIDE, ROWS - NEAR),
@@ -183,22 +207,15 @@
                     target[at : at + 8, :] = tracer_piece(
                         tracers_ref, tracer_from + row, level, half
                     )
-
-
-def pack(tracers, winds):
-    shapes = [jax.ShapeDtypeStruct((rows, COLS), jnp.float32) for rows in (EDGE_ROWS, MSG, MSG)]
+        target[MSG : MSG + EDGE_ROWS, :] = both
+
+
+def outer_rows(tracers, winds, left, right):
     return pl.pallas_call(
-        pack_kernel,
-        in_specs=[pl.BlockSpec(memory_space=pl.ANY)] * 2,
-        out_specs=[pl.BlockSpec(memory_space=pltpu.VMEM)] * 3,
-        out_shape=shapes,
-        scratch_shapes=[
-            pltpu.VMEM(tracers.shape, jnp.float32),
-            pltpu.VMEM(winds.shape, jnp.float32),
-            pltpu.SemaphoreType.DMA((LOADS + 1,)),
-        ],
+        rows_kernel,
+        out_shape=[jax.ShapeDtypeStruct((MSG + EDGE_ROWS, COLS), jnp.float32)] * 2,
         compiler_params=params(60),
-    )(tracers, winds)
+    )(tracers, winds, left, right)
 
 
 def cubic_weights(frac):
@@ -252,157 +269,249 @@
 T_TAPS = 7
 L_TAPS = 5
 SPREADS = L_TAPS + 2 * T_TAPS
-
-
-def advect_kernel(
-    tracers_ref, low_ref, high_ref, left_ref, right_ref, low_left_ref, low_right_ref,
-    high_left_ref, high_right_ref, first_ref, second_ref, winds_ref, out_ref,
-    own_edge, low_edge, high_edge, wind_taps, tracer_taps, spread_ref,
+SIDE_ROWS = 2 * WIDE
+SIDE_TAPS = WIDE + 2 * NEAR
+
+
+def edge_piece(ref, start, spot):
+    return pltpu.roll(ref[pl.ds(start, 8, stride=8), :], (COLS - WIDE - EDGE * spot) % COLS, 1)
+
+
+def keep_wind_taps(taps, onto, comp, main, edge):
+    shifted = column_shifts(main, edge, WIDE)
+    for side in range(W_TAPS):
+        for above in range(L_TAPS):
+            taps[onto, comp, above, side] = level_shift(shifted[side], above - 2)
+
+
+def keep_tracer_taps(taps, onto, main_of, edges, base, within, upper):
+    for spot in range(PER_GROUP):
+        level, half = spot // 2, spot % 2
+        edge = edge_piece(edges, base + half * 64 + within, level * 2 + upper)
+        shifted = column_shifts(main_of(level, half), edge, NEAR)
+        for side in range(T_TAPS):
+            taps[onto, spot, side] = shifted[side]
+
+
+def components(ref, row):
+    return [ref[pl.ds(comp * LEV * ROWS + row, LEV, stride=ROWS), :] for comp in range(3)]
+
+
+def first_weights(winds_ref, first_ref, row):
+    wind, first = components(winds_ref, row), components(first_ref, row)
+    frac = [jnp.clip(-w - d.astype(jnp.float32), 0.0, 1.0) for w, d in zip(wind, first)]
+    level_w = spread_weights(first[0], frac[0], -1, 0)
+    row_w = spread_weights(first[1], frac[1], -3, 2)
+    col_w = spread_weights(first[2], frac[2], -3, 2)
+    return wind, level_w, row_w, col_w
+
+
+def wind_sum(taps, rows, total, level_w, row_w, col_w):
+    total = list(total)
+    for above in range(L_TAPS):
+        part = [jnp.zeros((LEV, COLS), jnp.float32) for _ in range(3)]
+        for across, place in rows:
+            for comp in range(3):
+                inner = col_w[0] * taps[place, comp, above, 0]
+                for side in range(1, W_TAPS):
+                    inner = inner + col_w[side] * taps[place, comp, above, side]
+                part[comp] = part[comp] + row_w[across] * inner
+        for comp in range(3):
+            total[comp] = total[comp] + level_w[above] * part[comp]
+    return total
+
+
+def keep_second_weights(spread_ref, place, wind, midwind, second_ref, row):
+    second = components(second_ref, row)
+    frac = [
+        jnp.clip(-(w + m) * 0.5 - d.astype(jnp.float32), 0.0, 1.0)
+        for w, m, d in zip(wind, midwind, second)
+    ]
+    weights = spread_weights(second[0], frac[0], -1, 0)
+    weights += spread_weights(second[1], frac[1], -2, 1)
+    weights += spread_weights(second[2], frac[2], -2, 1)
+    for which in range(SPREADS):
+        spread_ref[place, which] = weights[which]
+
+
+def move_cell(taps, first_tap, spread_ref, place, level, row, out_ref):
+    def weight(which):
+        return jnp.broadcast_to(spread_ref[place, which, pl.ds(level, 1), :], (8, COLS))
+
+    row_w = [weight(L_TAPS + which) for which in range(T_TAPS)]
+    col_w = [weight(L_TAPS + T_TAPS + which) for which in range(T_TAPS)]
+    total = [jnp.zeros((8, COLS), jnp.float32) for _ in range(2)]
+    for above in range(L_TAPS):
+        source = jnp.clip(level + above - 2, 0, LEV - 1)
+        level_w = weight(above)
+        part = [jnp.zeros((8, COLS), jnp.float32) for _ in range(2)]
+        for across in range(T_TAPS):
+            for half in range(2):
+                piece = taps.at[first_tap + across, source * 2 + half]
+                inner = col_w[0] * piece[0]
+                for side in range(1, T_TAPS):
+                    inner = inner + col_w[side] * piece[side]
+                part[half] = part[half] + row_w[across] * inner
+        for half in range(2):
+            total[half] = total[half] + level_w * part[half]
+    for half in range(2):
+        start = half * 8 * LEV * ROWS + level * ROWS + row
+        out_ref[pl.ds(start, 8, stride=LEV * ROWS), :] = total[half]
+
+
+def inner_kernel(
+    tracers_ref, winds_ref, left_ref, right_ref, first_ref, second_ref, out_ref, partial_ref,
+    taps_hbm, edges, wind_taps, tracer_taps, spread_ref, taps_sem,
 ):
-    lane = lax.broadcasted_iota(jnp.int32, (EDGE_ROWS, COLS), 1)
-    from_left = lax.rem(lane, EDGE) < WIDE
-    own_edge[...] = jnp.where(from_left, left_ref[...], right_ref[...])
-    low_edge[...] = jnp.where(from_left, low_left_ref[...], low_right_ref[...])
-    high_edge[...] = jnp.where(from_left, high_left_ref[...], high_right_ref[...])
-
-    def edge_piece(ref, start, spot):
-        return pltpu.roll(ref[pl.ds(start, 8, stride=8), :], (COLS - WIDE - EDGE * spot) % COLS, 1)
-
-    def wind_edge(ref, row, comp):
-        return edge_piece(ref, NTR * 8 + row % 8, comp * 2 + row // 8)
-
-    for comp in range(3):
-        for row in range(WROWS):
-            if row < WIDE:
-                at = (row * 3 + comp) * LEV
-                main = low_ref[at : at + LEV, :]
-                edge = wind_edge(low_edge, ROWS - WIDE + row, comp)
-            elif row < WIDE + ROWS:
-                main = wind_piece(winds_ref, row - WIDE, comp)
-                edge = wind_edge(own_edge, row - WIDE, comp)
-            else:
-                at = ((row - WIDE - ROWS) * 3 + comp) * LEV
-                main = high_ref[at : at + LEV, :]
-                edge = wind_edge(high_edge, row - WIDE - ROWS, comp)
-            shifted = column_shifts(main, edge, WIDE)
-            for side in range(W_TAPS):
-                for above in range(L_TAPS):
-                    wind_taps[row, comp, above, side] = level_shift(shifted[side], above - 2)
-
-    def wind_row(row, carry):
-        def component(ref, comp):
-            return ref[pl.ds(comp * LEV * ROWS + row, LEV, stride=ROWS), :]
-
-        wind = [component(winds_ref, comp) for comp in range(3)]
-        first = [component(first_ref, comp) for comp in range(3)]
-        frac = [
-            jnp.clip(-wind[comp] - first[comp].astype(jnp.float32), 0.0, 1.0)
-            for comp in range(3)
-        ]
-        level_w = spread_weights(first[0], frac[0], -1, 0)
-        row_w = spread_weights(first[1], frac[1], -3, 2)
-        col_w = spread_weights(first[2], frac[2], -3, 2)
-        total = [jnp.zeros((LEV, COLS), jnp.float32) for _ in range(3)]
-        for above in range(L_TAPS):
-            part = [jnp.zeros((LEV, COLS), jnp.float32) for _ in range(3)]
-            for across in range(W_TAPS):
-                for comp in range(3):
-                    inner = col_w[0] * wind_taps[row + across, comp, above, 0]
-                    for side in range(1, W_TAPS):
-                        inner = inner + col_w[side] * wind_taps[row + across, comp, above, side]
-                    part[comp] = part[comp] + row_w[across] * inner
-            for comp in range(3):
-                total[comp] = total[comp] + level_w[above] * part[comp]
-        second = [component(second_ref, comp) for comp in range(3)]
-        frac = [
-            jnp.clip(
-                -(wind[comp] + total[comp]) * 0.5 - second[comp].astype(jnp.float32), 0.0, 1.0
-            )
-            for comp in range(3)
-        ]
-        weights = spread_weights(second[0], frac[0], -1, 0)
-        weights += spread_weights(second[1], frac[1], -2, 1)
-        weights += spread_weights(second[2], frac[2], -2, 1)
-        for which in range(SPREADS):
-            spread_ref[row, which] = weights[which]
-        return carry
-
-    lax.fori_loop(0, ROWS, wind_row, 0)
-
-    def keep_shifts(main_of, ref, onto, within, upper):
-        for spot in range(PER_GROUP):
-            level, half = spot // 2, spot % 2
-            edge = edge_piece(ref, half * 64 + within, level * 2 + upper)
-            shifted = column_shifts(main_of(level, half), edge, NEAR)
-            for side in range(T_TAPS):
-                tracer_taps[onto, spot, side] = shifted[side]
-
+    edges[...] = merged_edges(left_ref[...], right_ref[...])
     for upper in range(2):
 
-        def own_shifts(within, carry, upper=upper):
+        def own_taps(within, carry, upper=upper):
             row = upper * 8 + within
             main_of = functools.partial(tracer_piece, tracers_ref, row)
-            keep_shifts(main_of, own_edge, row + NEAR, within, upper)
+            keep_tracer_taps(tracer_taps, row, main_of, edges, 0, within, upper)
             return carry
 
-        lax.fori_loop(0, 8, own_shifts, 0)
-    for ref, edges, onto, upper in ((low_ref, low_edge, 0, 1), (high_ref, high_edge, NEAR + ROWS, 0)):
-
-        def halo_shifts(row, carry, ref=ref, edges=edges, onto=onto, upper=upper):
+        lax.fori_loop(0, 8, own_taps, 0)
+    save = pltpu.make_async_copy(tracer_taps, taps_hbm, taps_sem)
+    save.start()
+    for comp in range(3):
+        for row in range(ROWS):
+            edge = edge_piece(edges, NTR * 8 + row % 8, comp * 2 + row // 8)
+            keep_wind_taps(wind_taps, row + WIDE, comp, wind_piece(winds_ref, row, comp), edge)
+    for place in (0, WIDE + ROWS):
+        wind_taps[pl.ds(place, WIDE)] = jnp.zeros((WIDE,) + wind_taps.shape[1:], jnp.float32)
+
+    def midwind_of(row):
+        wind, level_w, row_w, col_w = first_weights(winds_ref, first_ref, row)
+        zero = [jnp.zeros((LEV, COLS), jnp.float32)] * 3
+        rows = [(across, row + across) for across in range(W_TAPS)]
+        return wind, wind_sum(wind_taps, rows, zero, level_w, row_w, col_w)
+
+    def middle_row(place, carry):
+        row = place + WIDE
+        wind, midwind = midwind_of(row)
+        keep_second_weights(spread_ref, place, wind, midwind, second_ref, row)
+        return carry
+
+    lax.fori_loop(0, ROWS - SIDE_ROWS, middle_row, 0)
+
+    def side_row(place, carry):
+        row = jnp.where(place < WIDE, place, place + ROWS - SIDE_ROWS)
+        midwind = midwind_of(row)[1]
+        for comp in range(3):
+            partial_ref[place, comp] = midwind[comp]
+        return carry
+
+    lax.fori_loop(0, SIDE_ROWS, side_row, 0)
+
+    def cell(index, carry):
+        place, level = index // LEV, lax.rem(index, LEV)
+        row = place + WIDE
+        move_cell(tracer_taps, row - NEAR, spread_ref, place, level, row, out_ref)
+        return carry
+
+    lax.fori_loop(0, (ROWS - SIDE_ROWS) * LEV, cell, 0)
+    save.wait()
+
+
+def inner_advect(tracers, winds, left, right, first, second):
+    vmem = pl.BlockSpec(memory_space=pltpu.VMEM)
+    taps = (ROWS, PER_GROUP, T_TAPS, 8, COLS)
+    return pl.pallas_call(
+        inner_kernel,
+        in_specs=[vmem] * 6,
+        out_specs=[vmem, vmem, pl.BlockSpec(memory_space=pl.ANY)],
+        out_shape=[
+            jax.ShapeDtypeStruct((NTR * LEV * ROWS, COLS), jnp.float32),
+            jax.ShapeDtypeStruct((SIDE_ROWS, 3, LEV, COLS), jnp.float32),
+            jax.ShapeDtypeStruct(taps, jnp.float32),
+        ],
+        scratch_shapes=[
+            pltpu.VMEM((EDGE_ROWS, COLS), jnp.float32),
+            pltpu.VMEM((WROWS, 3, L_TAPS, W_TAPS, LEV, COLS), jnp.float32),
+            pltpu.VMEM(taps, jnp.float32),
+            pltpu.VMEM((ROWS - SIDE_ROWS, SPREADS, LEV, COLS), jnp.float32),
+            pltpu.SemaphoreType.DMA,
+        ],
+        compiler_params=params(60),
+    )(tracers, winds, left, right, first, second)
+
+
+def outer_kernel(
+    low_ref, high_ref, partial_ref, winds_ref, first_ref, second_ref, taps_hbm, inner_hbm, out_ref,
+    wind_taps, tracer_taps, spread_ref, sems,
+):
+    own = SIDE_TAPS - NEAR
+    loads = (
+        pltpu.make_async_copy(taps_hbm.at[pl.ds(0, own)], tracer_taps.at[pl.ds(NEAR, own)], sems.at[0]),
+        pltpu.make_async_copy(
+            taps_hbm.at[pl.ds(ROWS - own, own)], tracer_taps.at[pl.ds(SIDE_TAPS, own)], sems.at[1]
+        ),
+        pltpu.make_async_copy(inner_hbm, out_ref, sems.at[2]),
+    )
+    for load in loads:
+        load.start()
+    for comp in range(3):
+        for ref, onto, upper in ((low_ref, 0, 1), (high_ref, WIDE, 0)):
+            for row in range(WIDE):
+                at = (row * 3 + comp) * LEV
+                within = row + (8 - WIDE if upper else 0)
+                edge = edge_piece(ref, MSG + NTR * 8 + within, comp * 2 + upper)
+                keep_wind_taps(wind_taps, onto + row, comp, ref[at : at + LEV, :], edge)
+    for place in range(SIDE_ROWS):
+        row = place if place < WIDE else place + ROWS - SIDE_ROWS
+        wind, level_w, row_w, col_w = first_weights(winds_ref, first_ref, row)
+        if place < WIDE:
+            rows = [(across, place + across) for across in range(WIDE - place)]
+        else:
+            rows = [
+                (across, row + across - ROWS) for across in range(WIDE + ROWS - row, W_TAPS)
+            ]
+        total = [partial_ref[place, comp] for comp in range(3)]
+        midwind = wind_sum(wind_taps, rows, total, level_w, row_w, col_w)
+        keep_second_weights(spread_ref, place, wind, midwind, second_ref, row)
+    for ref, onto, upper in ((low_ref, 0, 1), (high_ref, SIDE_TAPS + own, 0)):
+
+        def halo_taps(row, carry, ref=ref, onto=onto, upper=upper):
             def main_of(level, half):
                 at = WIND_MSG + row * LEV * NTR + level * NTR + half * 8
                 return ref[pl.ds(pl.multiple_of(at, 8), 8), :]
 
             within = row + (8 - NEAR if upper else 0)
-            keep_shifts(main_of, edges, row + onto, within, upper)
+            keep_tracer_taps(tracer_taps, row + onto, main_of, ref, MSG, within, upper)
             return carry
 
-        lax.fori_loop(0, NEAR, halo_shifts, 0)
-
-    def tracer_cell(cell, carry):
-        row, level = cell // LEV, lax.rem(cell, LEV)
-
-        def weight(which):
-            return jnp.broadcast_to(spread_ref[row, which, pl.ds(level, 1), :], (8, COLS))
-
-        row_w = [weight(L_TAPS + which) for which in range(T_TAPS)]
-        col_w = [weight(L_TAPS + T_TAPS + which) for which in range(T_TAPS)]
-        total = [jnp.zeros((8, COLS), jnp.float32) for _ in range(2)]
-        for above in range(L_TAPS):
-            source = jnp.clip(level + above - 2, 0, LEV - 1)
-            level_w = weight(above)
-            part = [jnp.zeros((8, COLS), jnp.float32) for _ in range(2)]
-            for across in range(T_TAPS):
-                for half in range(2):
-                    taps = tracer_taps.at[row + across, source * 2 + half]
-                    inner = col_w[0] * taps[0]
-                    for side in range(1, T_TAPS):
-                        inner = inner + col_w[side] * taps[side]
-                    part[half] = part[half] + row_w[across] * inner
-            for half in range(2):
-                total[half] = total[half] + level_w * part[half]
-        for half in range(2):
-            start = half * 8 * LEV * ROWS + level * ROWS + row
-            out_ref[pl.ds(start, 8, stride=LEV * ROWS), :] = total[half]
+        lax.fori_loop(0, NEAR, halo_taps, 0)
+    for load in loads:
+        load.wait()
+
+    def cell(index, carry):
+        place, level = index // LEV, lax.rem(index, LEV)
+        late = place >= WIDE
+        row = jnp.where(late, place + ROWS - SIDE_ROWS, place)
+        first_tap = jnp.where(late, place - WIDE + SIDE_TAPS, place)
+        move_cell(tracer_taps, first_tap, spread_ref, place, level, row, out_ref)
         return carry
 
-    lax.fori_loop(0, ROWS * LEV, tracer_cell, 0)
-
-
-def advect(tracers, low, high, edges, first, second, winds):
+    lax.fori_loop(0, SIDE_ROWS * LEV, cell, 0)
+
+
+def outer_advect(low, high, partial, winds, first, second, taps, inner):
+    vmem = pl.BlockSpec(memory_space=pltpu.VMEM)
     return pl.pallas_call(
-        advect_kernel,
-        in_specs=[pl.BlockSpec(memory_space=pltpu.VMEM)] * (6 + len(edges)),
-        out_specs=pl.BlockSpec(memory_space=pltpu.VMEM),
+        outer_kernel,
+        in_specs=[vmem] * 6 + [pl.BlockSpec(memory_space=pl.ANY)] * 2,
+        out_specs=vmem,
         out_shape=jax.ShapeDtypeStruct((NTR * LEV * ROWS, COLS), jnp.float32),
-        scratch_shapes=[pltpu.VMEM((EDGE_ROWS, COLS), jnp.float32)] * 3
-        + [
-            pltpu.VMEM((WROWS, 3, L_TAPS, W_TAPS, LEV, COLS), jnp.float32),
-            pltpu.VMEM((TROWS, LEV * 2, T_TAPS, 8, COLS), jnp.float32),
-            pltpu.VMEM((ROWS, SPREADS, LEV, COLS), jnp.float32),
+        scratch_shapes=[
+            pltpu.VMEM((SIDE_ROWS, 3, L_TAPS, W_TAPS, LEV, COLS), jnp.float32),
+            pltpu.VMEM((2 * SIDE_TAPS, PER_GROUP, T_TAPS, 8, COLS), jnp.float32),
+            pltpu.VMEM((SIDE_ROWS, SPREADS, LEV, COLS), jnp.float32),
+            pltpu.SemaphoreType.DMA((3,)),
         ],
         compiler_params=params(60),
-    )(tracers, low, high, *edges, first, second, winds)
+    )(low, high, partial, winds, first, second, taps, inner)
 
 
 def combine_kernel(
@@ -479,22 +588,21 @@
     )(arrived, moved)
 
 
-def halos(packed):
-    edge, top, bottom = packed
-    lats, lons = lax.axis_size("lat"), lax.axis_size("lon")
-
-    def received(value, lat_step, lon_step):
-        pairs = []
-        for lat in range(lats):
-            for lon in range(lons):
-                if 0 <= lat + lat_step < lats:
-                    source = (lat + lat_step) * lons + (lon + lon_step) % lons
-                    pairs.append((source, lat * lons + lon))
-        return lax.ppermute(value, ("lat", "lon"), pairs)
-
-    low, high = received(bottom, -1, 0), received(top, 1, 0)
-    edges = [received(edge, lat, lon) for lat in (0, -1, 1) for lon in (-1, 1)]
-    return low, high, edges
+def side_columns(tracers, winds):
+    lons = lax.axis_size("lon")
+    edge = pack(tracers, winds)
+    around = [(i, (i + 1) % lons) for i in range(lons)]
+    return lax.ppermute(edge, "lon", around), lax.ppermute(edge, "lon", [(b, a) for a, b in around])
+
+
+def advect(tracers, winds, left, right, first, second):
+    lats = lax.axis_size("lat")
+    top, bottom = outer_rows(tracers, winds, left, right)
+    up = [(i, i + 1) for i in range(lats - 1)]
+    low = lax.ppermute(bottom, "lat", up)
+    high = lax.ppermute(top, "lat", [(b, a) for a, b in up])
+    inner, partial, taps = inner_advect(tracers, winds, left, right, first, second)
+    return outer_advect(low, high, partial, winds, first, second, taps, inner)
 
 
 def body(
@@ -505,11 +613,11 @@
     tracers, winds, depart_first, depart_second = (
         field.reshape(-1, COLS) for field in (tracers, winds, depart_first, depart_second)
     )
-    low, high, edges = halos(pack(tracers, winds))
+    left, right = side_columns(tracers, winds)
     chunks = remap(fluxes, remap_weights, target_device, target_block, devices)
-    chunks, low, high, edges = lax.optimization_barrier((chunks, low, high, edges))
+    chunks, left, right = lax.optimization_barrier((chunks, left, right))
     arrived = lax.all_to_all(chunks, ("lat", "lon"), split_axis=0, concat_axis=0, tiled=True)
-    moved = advect(tracers, low, high, edges, depart_first, depart_second, winds)
+    moved = advect(tracers, winds, left, right, depart_first, depart_second)
     return combine(arrived, moved).reshape(shape)
 
 

time: 167 us -> 154 us (0.922)
  the two profiles are of different devices: /device:TPU:36 before, /device:TPU:71 now
where the time goes in v5:
time: 154 us
  Pallas kernels  69.3 us (45%)
  waiting for transfers between devices  62.5 us (41%)
  starting transfers between devices  21 us (14%)
    ppermute x1, waiting for transfers between devices, advect(): low = lax.ppermute(bottom, 'lat', up)  49.8 us
    pallas_call x1, Pallas kernels, inner_advect(): pl.pallas_call(inner_kernel, in_specs=[vmem] * 6, out_specs=[vmem, vmem,...  31 us
    pallas_call x1, Pallas kernels, outer_advect(): pl.pallas_call(outer_kernel, in_specs=[vmem] * 6 + [pl.BlockSpec(memory_s...  18.1 us
    ppermute x1, waiting for transfers between devices, advect(): high = lax.ppermute(top, 'lat', [(b, a) for a, b in up])  12.7 us
    all_to_all x1, starting transfers between devices, body(): lax.all_to_all(chunks, ('lat', 'lon'), split_axis=0, concat_axis=0, tiled...  12.1 us
    pallas_call x1, Pallas kernels, remap(): pl.pallas_call(remap_kernel, in_specs=[pl.BlockSpec(memory_space=pltpu.SM...  9.32 us
    pallas_call x1, Pallas kernels, combine(): pl.pallas_call(combine_kernel, in_specs=[anywhere] * 2, out_specs=anywher...  5.87 us
    ppermute x1, starting transfers between devices, advect(): low = lax.ppermute(bottom, 'lat', up)  3.3 us
  transfers between devices with their start and end apart: 5, of which 2 were waited for; matrix products, arithmetic and copies ran while one was open for 0% of the time, Pallas kernels for 39%

profile of v5, /device:TPU:71, one launch (start us, length us, event | category | flops | bytes accessed | tf_op | source)
XLA Modules:
  0.0 154.2 jit_solution(13485848676846349564)
XLA Ops:
  0.0 2.6 %shard_map.83 = f32[192,128]{1,0:T(8,128)} custom-call(f32[2048,128]{1,0:T(8,128)} %bitcast.7, f32[384,128]{1,0:T(8,128)} %bitcast.10), custom_call_target="tpu_custom_call" | custom-call | tf_op jit(solution)/shard_map/pallas_call | solution.py:174
  2.6 0.6 collective-permute-start.1
  3.2 3.0 %collective-permute-start = (f32[192,128]{1,0:T(8,128)}, f32[192,128]{1,0:T(8,128)S(1)}, u32[]{:S(2)}, u32[]{:S(2)}) collective-permute-start(f32[192,128]{1,0:T(8,128)} %shard_map.83), channel_id=1, source_target_pairs={{0,1},{1,2},{2,3},{3,4},{4,5},{5,6},{6,7},{7,8},{8,9},{9,10},{10,1... | collective-permute-start | bytes 294920 | tf_op jit(solution)/shard_map/ppermute | solution.py:595
  6.2 9.3 %shard_map.82 = bf16[128,264,128]{2,1,0:T(8,128)(2,1)} custom-call(s32[4,48]{1,0:T(4,128)} %bitcast.18, s32[4,48]{1,0:T(4,128)} %bitcast.19, bf16[48,128,256]{2,1,0:T(8,128)(2,1)} %flux_hbm.1, bf16[48,4,256,128]{3,2,1,0:T(8,128)(2,1)} %weight_hbm.1), custom_call_target="tpu_custom_call" | custom-call | tf_op jit(solution)/shard_map/pallas_call | solution.py:104
  15.6 0.0 collective-permute-done.1.right_ref
  15.6 0.0 copy-start
  15.6 0.0 collective-permute-done.left_ref
  15.6 0.0 copy-start.1
  15.6 0.6 copy-done
  16.2 0.0 copy-done.1
  16.2 12.1 %all-to-all-start = ((bf16[128,264,128]{2,1,0:T(8,128)(2,1)}), bf16[128,264,128]{2,1,0:T(8,128)(2,1)}, u32[]{:S(2)}, u32[]{:S(2)}) async-start(bf16[128,264,128]{2,1,0:T(8,128)(2,1)} %shard_map.82), calls=%async_computation | async-start | bytes 17301504 | tf_op jit(solution)/shard_map/all_to_all | solution.py:619
  28.4 2.4 %shard_map.84 = (f32[672,128]{1,0:T(8,128)}, f32[672,128]{1,0:T(8,128)}) custom-call(f32[2048,128]{1,0:T(8,128)} %bitcast.8, f32[384,128]{1,0:T(8,128)} %bitcast.11, f32[192,128]{1,0:T(8,128)} %copy-done.1, f32[192,128]{1,0:T(8,128)} %copy-done), custom_call_target="tpu_custom_call" | custom-call | tf_op jit(solution)/shard_map/pallas_call | solution.py:214
  30.8 3.3 %collective-permute-start.2 = (f32[672,128]{1,0:T(8,128)}, f32[672,128]{1,0:T(8,128)S(1)}, u32[]{:S(2)}, u32[]{:S(2)}) collective-permute-start(f32[672,128]{1,0:T(8,128)} %get-tuple-element.16), channel_id=1, source_target_pairs={{0,16},{16,32},{32,48},{48,64},{64,80},{80,96},{96,112},{1,17},{17... | collective-permute-start | bytes 1032200 | tf_op jit(solution)/shard_map/ppermute | solution.py:602
  34.1 1.9 %collective-permute-start.3 = (f32[672,128]{1,0:T(8,128)}, f32[672,128]{1,0:T(8,128)S(1)}, u32[]{:S(2)}, u32[]{:S(2)}) collective-permute-start(f32[672,128]{1,0:T(8,128)} %get-tuple-element.17), channel_id=1, source_target_pairs={{16,0},{32,16},{48,32},{64,48},{80,64},{96,80},{112,96},{17,1},{33... | collective-permute-start | bytes 1032200 | tf_op jit(solution)/shard_map/ppermute | solution.py:603
  36.0 31.0 %shard_map.85 = (f32[2048,128]{1,0:T(8,128)}, f32[8,3,8,128]{3,2,1,0:T(8,128)}, f32[16,16,7,8,128]{4,3,2,1,0:T(8,128)}) custom-call(f32[2048,128]{1,0:T(8,128)} %bitcast.9, f32[384,128]{1,0:T(8,128)} %bitcast.12, f32[192,128]{1,0:T(8,128)} %copy-done.1, f32[192,128]{1,0:T(8,128)} %copy-done, s32[384,128]{1,0:T(8,128)} %bitcast.14, s32[384,128]{1,0:T(8,128)} %bitcast.16), custom_call_target="tpu_custom_call" | custom-call | tf_op jit(solution)/shard_map/pallas_call | solution.py:421
  67.1 49.8 %collective-permute-done.2.low_ref = f32[672,128]{1,0:T(8,128)S(1)} collective-permute-done((f32[672,128]{1,0:T(8,128)}, f32[672,128]{1,0:T(8,128)S(1)}, u32[]{:S(2)}, u32[]{:S(2)}) %collective-permute-start.2) | collective-permute-done | bytes 344096 | tf_op jit(solution)/shard_map/ppermute | solution.py:602
  116.8 0.0 copy-start.2
  116.8 12.7 %collective-permute-done.3.high_ref = f32[672,128]{1,0:T(8,128)S(1)} collective-permute-done((f32[672,128]{1,0:T(8,128)}, f32[672,128]{1,0:T(8,128)S(1)}, u32[]{:S(2)}, u32[]{:S(2)}) %collective-permute-start.3) | collective-permute-done | bytes 344096 | tf_op jit(solution)/shard_map/ppermute | solution.py:603
  129.5 0.0 copy-start.3
  129.5 0.0 copy-done.2
  129.5 0.7 copy-done.3
  130.3 18.1 %shard_map.86.moved_hbm = f32[2048,128]{1,0:T(8,128)} custom-call(f32[672,128]{1,0:T(8,128)} %copy-done.2, f32[672,128]{1,0:T(8,128)} %copy-done.3, f32[8,3,8,128]{3,2,1,0:T(8,128)} %get-tuple-element.18.partial_ref, f32[384,128]{1,0:T(8,128)} %bitcast.13, s32[384,128]{1,0:T(8,128)} %bitcast.15, s32[384,128]{1,0:T(8,128)} %bitcast.17, ...), custom_call_target="tpu_custom_call" | custom-call | tf_op jit(solution)/shard_map/pallas_call | solution.py:502
  148.3 0.0 all-to-all-done.arrived_hbm
  148.3 5.9 %shard_map.87 = f32[2048,128]{1,0:T(8,128)} custom-call(bf16[128,264,128]{2,1,0:T(8,128)(2,1)} %all-to-all-done.arrived_hbm, f32[2048,128]{1,0:T(8,128)} %shard_map.86.moved_hbm), custom_call_target="tpu_custom_call" | custom-call | tf_op jit(solution)/shard_map/pallas_call | solution.py:573
Async XLA Ops:
  2.6 13.0 %collective-permute-start.1 = (f32[192,128]{1,0:T(8,128)}, f32[192,128]{1,0:T(8,128)S(1)}, u32[]{:S(2)}, u32[]{:S(2)}) collective-permute-start(f32[192,128]{1,0:T(8,128)} %shard_map.83), channel_id=1, source_target_pairs={{1,0},{2,1},{3,2},{4,3},{5,4},{6,5},{7,6},{8,7},{9,8},{10,9},{11,1... | collective-permute-start | bytes 294920 | tf_op jit(solution)/shard_map/ppermute | solution.py:595
  3.2 12.4 %collective-permute-start = (f32[192,128]{1,0:T(8,128)}, f32[192,128]{1,0:T(8,128)S(1)}, u32[]{:S(2)}, u32[]{:S(2)}) collective-permute-start(f32[192,128]{1,0:T(8,128)} %shard_map.83), channel_id=1, source_target_pairs={{0,1},{1,2},{2,3},{3,4},{4,5},{5,6},{6,7},{7,8},{8,9},{9,10},{10,1... | collective-permute-start | bytes 294920 | tf_op jit(solution)/shard_map/ppermute | solution.py:595
  15.6 0.6 copy-start
  15.6 0.7 copy-start.1
  16.2 132.1 %all-to-all-start = ((bf16[128,264,128]{2,1,0:T(8,128)(2,1)}), bf16[128,264,128]{2,1,0:T(8,128)(2,1)}, u32[]{:S(2)}, u32[]{:S(2)}) async-start(bf16[128,264,128]{2,1,0:T(8,128)(2,1)} %shard_map.82), calls=%async_computation | async-start | bytes 17301504 | tf_op jit(solution)/shard_map/all_to_all | solution.py:619
  30.8 86.0 %collective-permute-start.2 = (f32[672,128]{1,0:T(8,128)}, f32[672,128]{1,0:T(8,128)S(1)}, u32[]{:S(2)}, u32[]{:S(2)}) collective-permute-start(f32[672,128]{1,0:T(8,128)} %get-tuple-element.16), channel_id=1, source_target_pairs={{0,16},{16,32},{32,48},{48,64},{64,80},{80,96},{96,112},{1,17},{17... | collective-permute-start | bytes 1032200 | tf_op jit(solution)/shard_map/ppermute | solution.py:602
  34.1 95.4 %collective-permute-start.3 = (f32[672,128]{1,0:T(8,128)}, f32[672,128]{1,0:T(8,128)S(1)}, u32[]{:S(2)}, u32[]{:S(2)}) collective-permute-start(f32[672,128]{1,0:T(8,128)} %get-tuple-element.17), channel_id=1, source_target_pairs={{16,0},{32,16},{48,32},{64,48},{80,64},{96,80},{112,96},{17,1},{33... | collective-permute-start | bytes 1032200 | tf_op jit(solution)/shard_map/ppermute | solution.py:603
  116.8 12.7 %copy-start.2 = (f32[672,128]{1,0:T(8,128)}, f32[672,128]{1,0:T(8,128)S(1)}, u32[]{:S(2)}) copy-start(f32[672,128]{1,0:T(8,128)S(1)} %collective-permute-done.2.low_ref) | copy-start | bytes 1032196
  129.5 0.7 copy-start.3

commit v6 on v5

--- a/solution.py
+++ b/solution.py
@@ -190,12 +190,10 @@
     return jnp.where(lax.rem(lane, EDGE) < WIDE, left, right)
 
 
-def rows_kernel(tracers_ref, winds_ref, left_ref, right_ref, top_ref, bottom_ref):
+def rows_kernel(odd_ref, tracers_ref, winds_ref, left_ref, right_ref, near_ref, far_ref):
     both = merged_edges(left_ref[...], right_ref[...])
-    for target, wind_from, tracer_from in (
-        (top_ref, 0, 0),
-        (bottom_ref, ROWS - WIDE, ROWS - NEAR),
-    ):
+
+    def fill(target, wind_from, tracer_from):
         for row in range(WIDE):
             for comp in range(3):
                 at = (row * 3 + comp) * LEV
@@ -209,13 +207,25 @@
                     )
         target[MSG : MSG + EDGE_ROWS, :] = both
 
-
-def outer_rows(tracers, winds, left, right):
+    @pl.when(odd_ref[0] == 0)
+    def _():
+        fill(near_ref, ROWS - WIDE, ROWS - NEAR)
+        fill(far_ref, 0, 0)
+
+    @pl.when(odd_ref[0] == 1)
+    def _():
+        fill(near_ref, 0, 0)
+        fill(far_ref, ROWS - WIDE, ROWS - NEAR)
+
+
+def outer_rows(odd, tracers, winds, left, right):
     return pl.pallas_call(
         rows_kernel,
+        in_specs=[pl.BlockSpec(memory_space=pltpu.SMEM)]
+        + [pl.BlockSpec(memory_space=pltpu.VMEM)] * 4,
         out_shape=[jax.ShapeDtypeStruct((MSG + EDGE_ROWS, COLS), jnp.float32)] * 2,
         compiler_params=params(60),
-    )(tracers, winds, left, right)
+    )(odd, tracers, winds, left, right)
 
 
 def cubic_weights(frac):
@@ -439,79 +449,87 @@
 
 
 def outer_kernel(
-    low_ref, high_ref, partial_ref, winds_ref, first_ref, second_ref, taps_hbm, inner_hbm, out_ref,
+    side_ref, halo_ref, partial_ref, winds_ref, first_ref, second_ref, taps_hbm, inner_hbm, out_ref,
     wind_taps, tracer_taps, spread_ref, sems,
 ):
+    side = side_ref[0]
     own = SIDE_TAPS - NEAR
     loads = (
-        pltpu.make_async_copy(taps_hbm.at[pl.ds(0, own)], tracer_taps.at[pl.ds(NEAR, own)], sems.at[0]),
         pltpu.make_async_copy(
-            taps_hbm.at[pl.ds(ROWS - own, own)], tracer_taps.at[pl.ds(SIDE_TAPS, own)], sems.at[1]
+            taps_hbm.at[pl.ds(side * (ROWS - own), own)],
+            tracer_taps.at[pl.ds((1 - side) * NEAR, own)],
+            sems.at[0],
         ),
-        pltpu.make_async_copy(inner_hbm, out_ref, sems.at[2]),
+        pltpu.make_async_copy(inner_hbm, out_ref, sems.at[1]),
     )
     for load in loads:
         load.start()
-    for comp in range(3):
-        for ref, onto, upper in ((low_ref, 0, 1), (high_ref, WIDE, 0)):
+
+    def prepare(late):
+        upper = 1 - late
+        for comp in range(3):
             for row in range(WIDE):
                 at = (row * 3 + comp) * LEV
                 within = row + (8 - WIDE if upper else 0)
-                edge = edge_piece(ref, MSG + NTR * 8 + within, comp * 2 + upper)
-                keep_wind_taps(wind_taps, onto + row, comp, ref[at : at + LEV, :], edge)
-    for place in range(SIDE_ROWS):
-        row = place if place < WIDE else place + ROWS - SIDE_ROWS
-        wind, level_w, row_w, col_w = first_weights(winds_ref, first_ref, row)
-        if place < WIDE:
-            rows = [(across, place + across) for across in range(WIDE - place)]
-        else:
-            rows = [
-                (across, row + across - ROWS) for across in range(WIDE + ROWS - row, W_TAPS)
-            ]
-        total = [partial_ref[place, comp] for comp in range(3)]
-        midwind = wind_sum(wind_taps, rows, total, level_w, row_w, col_w)
-        keep_second_weights(spread_ref, place, wind, midwind, second_ref, row)
-    for ref, onto, upper in ((low_ref, 0, 1), (high_ref, SIDE_TAPS + own, 0)):
-
-        def halo_taps(row, carry, ref=ref, onto=onto, upper=upper):
+                edge = edge_piece(halo_ref, MSG + NTR * 8 + within, comp * 2 + upper)
+                keep_wind_taps(wind_taps, row, comp, halo_ref[at : at + LEV, :], edge)
+        for place in range(WIDE):
+            row = place + late * (ROWS - WIDE)
+            wind, level_w, row_w, col_w = first_weights(winds_ref, first_ref, row)
+            if late:
+                rows = [
+                    (across, row + across - ROWS - WIDE)
+                    for across in range(WIDE + ROWS - row, W_TAPS)
+                ]
+            else:
+                rows = [(across, place + across) for across in range(WIDE - place)]
+            total = [partial_ref[place + late * WIDE, comp] for comp in range(3)]
+            midwind = wind_sum(wind_taps, rows, total, level_w, row_w, col_w)
+            keep_second_weights(spread_ref, place, wind, midwind, second_ref, row)
+
+        def halo_taps(row, carry):
             def main_of(level, half):
                 at = WIND_MSG + row * LEV * NTR + level * NTR + half * 8
-                return ref[pl.ds(pl.multiple_of(at, 8), 8), :]
+                return halo_ref[pl.ds(pl.multiple_of(at, 8), 8), :]
 
             within = row + (8 - NEAR if upper else 0)
-            keep_tracer_taps(tracer_taps, row + onto, main_of, ref, MSG, within, upper)
+            onto = row + late * own
+            keep_tracer_taps(tracer_taps, onto, main_of, halo_ref, MSG, within, upper)
             return carry
 
         lax.fori_loop(0, NEAR, halo_taps, 0)
+
+    for late in range(2):
+        pl.when(side == late)(functools.partial(prepare, late))
     for load in loads:
         load.wait()
 
     def cell(index, carry):
         place, level = index // LEV, lax.rem(index, LEV)
-        late = place >= WIDE
-        row = jnp.where(late, place + ROWS - SIDE_ROWS, place)
-        first_tap = jnp.where(late, place - WIDE + SIDE_TAPS, place)
-        move_cell(tracer_taps, first_tap, spread_ref, place, level, row, out_ref)
+        row = place + side * (ROWS - WIDE)
+        move_cell(tracer_taps, place, spread_ref, place, level, row, out_ref)
         return carry
 
-    lax.fori_loop(0, SIDE_ROWS * LEV, cell, 0)
-
-
-def outer_advect(low, high, partial, winds, first, second, taps, inner):
+    lax.fori_loop(0, WIDE * LEV, cell, 0)
+
+
+def outer_advect(side, halo, partial, winds, first, second, taps, inner):
     vmem = pl.BlockSpec(memory_space=pltpu.VMEM)
     return pl.pallas_call(
         outer_kernel,
-        in_specs=[vmem] * 6 + [pl.BlockSpec(memory_space=pl.ANY)] * 2,
+        in_specs=[pl.BlockSpec(memory_space=pltpu.SMEM)]
+        + [vmem] * 5
+        + [pl.BlockSpec(memory_space=pl.ANY)] * 2,
         out_specs=vmem,
         out_shape=jax.ShapeDtypeStruct((NTR * LEV * ROWS, COLS), jnp.float32),
         scratch_shapes=[
-            pltpu.VMEM((SIDE_ROWS, 3, L_TAPS, W_TAPS, LEV, COLS), jnp.float32),
-            pltpu.VMEM((2 * SIDE_TAPS, PER_GROUP, T_TAPS, 8, COLS), jnp.float32),
-            pltpu.VMEM((SIDE_ROWS, SPREADS, LEV, COLS), jnp.float32),
-            pltpu.SemaphoreType.DMA((3,)),
+            pltpu.VMEM((WIDE, 3, L_TAPS, W_TAPS, LEV, COLS), jnp.float32),
+            pltpu.VMEM((SIDE_TAPS, PER_GROUP, T_TAPS, 8, COLS), jnp.float32),
+            pltpu.VMEM((WIDE, SPREADS, LEV, COLS), jnp.float32),
+            pltpu.SemaphoreType.DMA((2,)),
         ],
         compiler_params=params(60),
-    )(low, high, partial, winds, first, second, taps, inner)
+    )(side, halo, partial, winds, first, second, taps, inner)
 
 
 def combine_kernel(
@@ -597,12 +615,17 @@
 
 def advect(tracers, winds, left, right, first, second):
     lats = lax.axis_size("lat")
-    top, bottom = outer_rows(tracers, winds, left, right)
-    up = [(i, i + 1) for i in range(lats - 1)]
-    low = lax.ppermute(bottom, "lat", up)
-    high = lax.ppermute(top, "lat", [(b, a) for a, b in up])
+    odd = lax.rem(lax.axis_index("lat"), 2).reshape(1).astype(jnp.int32)
+    near_rows, far_rows = outer_rows(odd, tracers, winds, left, right)
+
+    def swapped(value, start):
+        pairs = [(i, i + 1) for i in range(start, lats - 1, 2)]
+        return lax.ppermute(value, "lat", pairs + [(b, a) for a, b in pairs])
+
+    near, far = swapped(near_rows, 0), swapped(far_rows, 1)
     inner, partial, taps = inner_advect(tracers, winds, left, right, first, second)
-    return outer_advect(low, high, partial, winds, first, second, taps, inner)
+    moved = outer_advect(1 - odd, near, partial, winds, first, second, taps, inner)
+    return outer_advect(odd, far, partial, winds, first, second, taps, moved)
 
 
 def body(

time: 154 us -> 146 us (0.948)
  the two profiles are of different devices: /device:TPU:71 before, /device:TPU:36 now
where the time goes in v6:
time: 146 us; the launch traced here: 145 us
  Pallas kernels  71.4 us (49%)
  waiting for transfers between devices  53 us (36%)
  starting transfers between devices  18 us (12%)
  local copies, waits for them, and re-layouts  2.11 us (1%)
    ppermute x2, waiting for transfers between devices, swapped(): return lax.ppermute(value, 'lat', pairs + [(b, a) for a, b in pairs])  43.6 us
    pallas_call x1, Pallas kernels, inner_advect(): pl.pallas_call(inner_kernel, in_specs=[vmem] * 6, out_specs=[vmem, vmem,...  31 us
    pallas_call x2, Pallas kernels, outer_advect(): pl.pallas_call(outer_kernel, in_specs=[pl.BlockSpec(memory_space=pltpu.SM...  20.1 us
    all_to_all x1, starting transfers between devices, body(): lax.all_to_all(chunks, ('lat', 'lon'), split_axis=0, concat_axis=0, tiled...  13.5 us
    all_to_all x1, waiting for transfers between devices, body(): lax.all_to_all(chunks, ('lat', 'lon'), split_axis=0, concat_axis=0, tiled...  9.35 us
    pallas_call x1, Pallas kernels, remap(): pl.pallas_call(remap_kernel, in_specs=[pl.BlockSpec(memory_space=pltpu.SM...  9.32 us
    pallas_call x1, Pallas kernels, combine(): pl.pallas_call(combine_kernel, in_specs=[anywhere] * 2, out_specs=anywher...  5.87 us
  transfers between devices with their start and end apart: 5, of which 2 were waited for; matrix products, arithmetic and copies ran while one was open for 0% of the time, Pallas kernels for 44%

profile of v6, /device:TPU:36, one launch (start us, length us, event | category | flops | bytes accessed | tf_op | source)
XLA Modules:
  0.0 144.6 jit_solution(3638290033230972039)
XLA Ops:
  0.0 2.6 %shard_map.83 = f32[192,128]{1,0:T(8,128)} custom-call(f32[2048,128]{1,0:T(8,128)} %bitcast.8, f32[384,128]{1,0:T(8,128)} %bitcast.11), custom_call_target="tpu_custom_call" | custom-call | tf_op jit(solution)/shard_map/pallas_call | solution.py:174
  2.6 0.6 collective-permute-start.1
  3.2 1.5 %collective-permute-start = (f32[192,128]{1,0:T(8,128)}, f32[192,128]{1,0:T(8,128)S(1)}, u32[]{:S(2)}, u32[]{:S(2)}) collective-permute-start(f32[192,128]{1,0:T(8,128)} %shard_map.83), channel_id=1, source_target_pairs={{0,1},{1,2},{2,3},{3,4},{4,5},{5,6},{6,7},{7,8},{8,9},{9,10},{10,1... | collective-permute-start | bytes 294920 | tf_op jit(solution)/shard_map/ppermute | solution.py:613
  4.7 9.3 %shard_map.82 = bf16[128,264,128]{2,1,0:T(8,128)(2,1)} custom-call(s32[4,48]{1,0:T(4,128)} %bitcast.22, s32[4,48]{1,0:T(4,128)} %bitcast.23, bf16[48,128,256]{2,1,0:T(8,128)(2,1)} %flux_hbm.1, bf16[48,4,256,128]{3,2,1,0:T(8,128)(2,1)} %weight_hbm.1), custom_call_target="tpu_custom_call" | custom-call | tf_op jit(solution)/shard_map/pallas_call | solution.py:104
  14.0 0.0 collective-permute-done.1.right_ref
  14.0 0.0 copy-start
  14.0 0.0 collective-permute-done.left_ref
  14.0 0.0 copy-start.1
  14.0 0.6 copy-done
  14.6 0.1 copy-done.1
  14.7 13.5 %all-to-all-start = ((bf16[128,264,128]{2,1,0:T(8,128)(2,1)}), bf16[128,264,128]{2,1,0:T(8,128)(2,1)}, u32[]{:S(2)}, u32[]{:S(2)}) async-start(bf16[128,264,128]{2,1,0:T(8,128)(2,1)} %shard_map.82), calls=%async_computation | async-start | bytes 17301504 | tf_op jit(solution)/shard_map/all_to_all | solution.py:642
  28.2 2.5 %shard_map.84 = (f32[672,128]{1,0:T(8,128)}, f32[672,128]{1,0:T(8,128)}) custom-call(s32[1]{0:T(128)} %bitcast.4.odd_ref.side_ref, f32[2048,128]{1,0:T(8,128)} %bitcast.9, f32[384,128]{1,0:T(8,128)} %bitcast.12, f32[192,128]{1,0:T(8,128)} %copy-done.1, f32[192,128]{1,0:T(8,128)} %copy-done), custom_call_target="tpu_custom_call" | custom-call | tf_op jit(solution)/shard_map/pallas_call | solution.py:222
  30.7 0.1 collective-permute-start.3
  30.9 2.3 %collective-permute-start.2 = (f32[672,128]{1,0:T(8,128)}, f32[672,128]{1,0:T(8,128)S(1)}, u32[]{:S(2)}, u32[]{:S(2)}) collective-permute-start(f32[672,128]{1,0:T(8,128)} %get-tuple-element.16), channel_id=1, source_target_pairs={{16,32},{48,64},{80,96},{32,16},{64,48},{96,80},{17,33},{49,65},{8... | collective-permute-start | bytes 1032200 | tf_op jit(solution)/shard_map/ppermute | solution.py:623
  33.1 31.0 %shard_map.85 = (f32[2048,128]{1,0:T(8,128)}, f32[8,3,8,128]{3,2,1,0:T(8,128)}, f32[16,16,7,8,128]{4,3,2,1,0:T(8,128)}) custom-call(f32[2048,128]{1,0:T(8,128)} %bitcast.10, f32[384,128]{1,0:T(8,128)} %bitcast.13, f32[192,128]{1,0:T(8,128)} %copy-done.1, f32[192,128]{1,0:T(8,128)} %copy-done, s32[384,128]{1,0:T(8,128)} %bitcast.16, s32[384,128]{1,0:T(8,128)} %bitcast.19), custom_call_target="tpu_custom_call" | custom-call | tf_op jit(solution)/shard_map/pallas_call | solution.py:431
  64.2 0.0 collective-permute-done.3.halo_ref
  64.2 0.0 copy-start.3
  64.2 0.7 copy-done.3
  64.9 10.0 %shard_map.86.inner_hbm = f32[2048,128]{1,0:T(8,128)} custom-call(s32[1]{0:T(128)S(6)} %sub.3.side_ref, f32[672,128]{1,0:T(8,128)} %copy-done.3, f32[8,3,8,128]{3,2,1,0:T(8,128)} %get-tuple-element.17.partial_ref, f32[384,128]{1,0:T(8,128)} %bitcast.14, s32[384,128]{1,0:T(8,128)} %bitcast.17, s32[384,128]{1,0:T(8,128)} %bitcast.20, ...), custom_call_target="tpu_custom_call" | custom-call | tf_op jit(solution)/shard_map/pallas_call | solution.py:518
  75.0 43.6 %collective-permute-done.2.halo_ref = f32[672,128]{1,0:T(8,128)S(1)} collective-permute-done((f32[672,128]{1,0:T(8,128)}, f32[672,128]{1,0:T(8,128)S(1)}, u32[]{:S(2)}, u32[]{:S(2)}) %collective-permute-start.2) | collective-permute-done | bytes 344096 | tf_op jit(solution)/shard_map/ppermute | solution.py:623
  118.6 0.0 copy-start.2
  118.6 0.7 copy-done.2
  119.3 10.0 %shard_map.87.moved_hbm = f32[2048,128]{1,0:T(8,128)} custom-call(s32[1]{0:T(128)} %bitcast.4.odd_ref.side_ref, f32[672,128]{1,0:T(8,128)} %copy-done.2, f32[8,3,8,128]{3,2,1,0:T(8,128)} %get-tuple-element.17.partial_ref, f32[384,128]{1,0:T(8,128)} %bitcast.15, s32[384,128]{1,0:T(8,128)} %bitcast.18, s32[384,128]{1,0:T(8,128)} %bitcast.21, ...), custom_call_target="tpu_custom_call" | custom-call | tf_op jit(solution)/shard_map/pallas_call | solution.py:518
  129.4 9.4 %all-to-all-done.arrived_hbm = bf16[128,264,128]{2,1,0:T(8,128)(2,1)} async-done(((bf16[128,264,128]{2,1,0:T(8,128)(2,1)}), bf16[128,264,128]{2,1,0:T(8,128)(2,1)}, u32[]{:S(2)}, u32[]{:S(2)}) %all-to-all-start) | async-done | bytes 8650784 | tf_op jit(solution)/shard_map/all_to_all | solution.py:642
  138.7 5.9 %shard_map.88 = f32[2048,128]{1,0:T(8,128)} custom-call(bf16[128,264,128]{2,1,0:T(8,128)(2,1)} %all-to-all-done.arrived_hbm, f32[2048,128]{1,0:T(8,128)} %shard_map.87.moved_hbm), custom_call_target="tpu_custom_call" | custom-call | tf_op jit(solution)/shard_map/pallas_call | solution.py:591
Async XLA Ops:
  2.6 11.4 %collective-permute-start.1 = (f32[192,128]{1,0:T(8,128)}, f32[192,128]{1,0:T(8,128)S(1)}, u32[]{:S(2)}, u32[]{:S(2)}) collective-permute-start(f32[192,128]{1,0:T(8,128)} %shard_map.83), channel_id=1, source_target_pairs={{1,0},{2,1},{3,2},{4,3},{5,4},{6,5},{7,6},{8,7},{9,8},{10,9},{11,1... | collective-permute-start | bytes 294920 | tf_op jit(solution)/shard_map/ppermute | solution.py:613
  3.2 10.8 %collective-permute-start = (f32[192,128]{1,0:T(8,128)}, f32[192,128]{1,0:T(8,128)S(1)}, u32[]{:S(2)}, u32[]{:S(2)}) collective-permute-start(f32[192,128]{1,0:T(8,128)} %shard_map.83), channel_id=1, source_target_pairs={{0,1},{1,2},{2,3},{3,4},{4,5},{5,6},{6,7},{7,8},{8,9},{9,10},{10,1... | collective-permute-start | bytes 294920 | tf_op jit(solution)/shard_map/ppermute | solution.py:613
  14.0 0.6 copy-start
  14.0 0.7 copy-start.1
  14.7 124.0 %all-to-all-start = ((bf16[128,264,128]{2,1,0:T(8,128)(2,1)}), bf16[128,264,128]{2,1,0:T(8,128)(2,1)}, u32[]{:S(2)}, u32[]{:S(2)}) async-start(bf16[128,264,128]{2,1,0:T(8,128)(2,1)} %shard_map.82), calls=%async_computation | async-start | bytes 17301504 | tf_op jit(solution)/shard_map/all_to_all | solution.py:642
  30.7 33.5 %collective-permute-start.3 = (f32[672,128]{1,0:T(8,128)}, f32[672,128]{1,0:T(8,128)S(1)}, u32[]{:S(2)}, u32[]{:S(2)}) collective-permute-start(f32[672,128]{1,0:T(8,128)} %get-tuple-element.19), channel_id=1, source_target_pairs={{0,16},{32,48},{64,80},{96,112},{16,0},{48,32},{80,64},{112,96},{1... | collective-permute-start | bytes 1032200 | tf_op jit(solution)/shard_map/ppermute | solution.py:623
  30.9 87.7 %collective-permute-start.2 = (f32[672,128]{1,0:T(8,128)}, f32[672,128]{1,0:T(8,128)S(1)}, u32[]{:S(2)}, u32[]{:S(2)}) collective-permute-start(f32[672,128]{1,0:T(8,128)} %get-tuple-element.16), channel_id=1, source_target_pairs={{16,32},{48,64},{80,96},{32,16},{64,48},{96,80},{17,33},{49,65},{8... | collective-permute-start | bytes 1032200 | tf_op jit(solution)/shard_map/ppermute | solution.py:623
  64.2 0.7 copy-start.3
  118.6 0.7 copy-start.2

commit v7 on v6

--- a/solution.py
+++ b/solution.py
@@ -19,9 +19,9 @@
 TROWS = ROWS + 2 * NEAR
 EDGE = 2 * WIDE
 PER_GROUP = COLS // EDGE
-TILE_STEP = 4
-SOURCE_STEP = 8
-SUMS = 2
+TILE_STEP = 6
+SOURCE_STEP = 16
+SUMS = 1
 MARK_ROWS = 8
 OUT_PARTS = 4
 
@@ -135,7 +135,7 @@
 TRACER_MSG = NEAR * LEV * NTR
 MSG = WIND_MSG + TRACER_MSG
 EDGE_ROWS = (NTR + LEV) * 8
-LOADS = 8
+LOADS = 4
 
 
 def pack_kernel(tracers_hbm, winds_hbm, edge_ref, tracers_ref, winds_ref, sems):
@@ -224,7 +224,7 @@
         in_specs=[pl.BlockSpec(memory_space=pltpu.SMEM)]
         + [pl.BlockSpec(memory_space=pltpu.VMEM)] * 4,
         out_shape=[jax.ShapeDtypeStruct((MSG + EDGE_ROWS, COLS), jnp.float32)] * 2,
-        compiler_params=params(60),
+        compiler_params=params(8),
     )(odd, tracers, winds, left, right)
 
 
@@ -444,7 +444,7 @@
             pltpu.VMEM((ROWS - SIDE_ROWS, SPREADS, LEV, COLS), jnp.float32),
             pltpu.SemaphoreType.DMA,
         ],
-        compiler_params=params(60),
+        compiler_params=params(40),
     )(tracers, winds, left, right, first, second)
 
 

time: 146 us -> 145 us (level)
  Pallas kernels: 71.4 us -> 66.2 us
  local copies, waits for them, and re-layouts: 2.11 us -> 6.02 us
    unnamed x8 -> x18, local copies, waits for them, and re-layouts: 2.11 us -> 6.02 us
    pallas_call x1, Pallas kernels: 2.52 us -> 0.29 us  [outer_rows(): pl.pallas_call(rows_kernel, in_specs=[pl.BlockSpec(memory_space=pltpu.SME...]
    pallas_call x1, Pallas kernels: 31 us -> 29.2 us  [inner_advect(): pl.pallas_call(inner_kernel, in_specs=[vmem] * 6, out_specs=[vmem, vmem,...]
  transfers between devices with their start and end apart: 5 -> 5, of which waited for: 2 -> 2; matrix products, arithmetic and copies ran while one was open for 0% -> 0% of each run, Pallas kernels for 44% -> 41%
where the time goes in v7:
time: 145 us; the launch traced here: 143 us
  Pallas kernels  66.2 us (46%)
  waiting for transfers between devices  52.4 us (36%)
  starting transfers between devices  18.1 us (12%)
  local copies, waits for them, and re-layouts  6.02 us (4%)
    ppermute x2, waiting for transfers between devices, swapped(): return lax.ppermute(value, 'lat', pairs + [(b, a) for a, b in pairs])  43 us
    pallas_call x1, Pallas kernels, inner_advect(): pl.pallas_call(inner_kernel, in_specs=[vmem] * 6, out_specs=[vmem, vmem,...  29.2 us
    pallas_call x2, Pallas kernels, outer_advect(): pl.pallas_call(outer_kernel, in_specs=[pl.BlockSpec(memory_space=pltpu.SM...  20.1 us
    all_to_all x1, starting transfers between devices, body(): lax.all_to_all(chunks, ('lat', 'lon'), split_axis=0, concat_axis=0, tiled...  13.5 us
    all_to_all x1, waiting for transfers between devices, body(): lax.all_to_all(chunks, ('lat', 'lon'), split_axis=0, concat_axis=0, tiled...  9.4 us
    pallas_call x1, Pallas kernels, remap(): pl.pallas_call(remap_kernel, in_specs=[pl.BlockSpec(memory_space=pltpu.SM...  9.22 us
    unnamed x18, local copies, waits for them, and re-layouts  6.02 us
    pallas_call x1, Pallas kernels, combine(): pl.pallas_call(combine_kernel, in_specs=[anywhere] * 2, out_specs=anywher...  5.22 us
  transfers between devices with their start and end apart: 5, of which 2 were waited for; matrix products, arithmetic and copies ran while one was open for 0% of the time, Pallas kernels for 41%

profile of v7, /device:TPU:36, one launch (start us, length us, event | category | flops | bytes accessed | tf_op | source)
XLA Modules:
  0.0 142.9 jit_solution(2943254081046370786)
XLA Ops:
  0.0 2.3 %shard_map.83 = f32[192,128]{1,0:T(8,128)} custom-call(f32[2048,128]{1,0:T(8,128)} %bitcast.8, f32[384,128]{1,0:T(8,128)} %bitcast.11), custom_call_target="tpu_custom_call" | custom-call | tf_op jit(solution)/shard_map/pallas_call | solution.py:174
  2.3 0.6 collective-permute-start.1
  2.9 1.5 %collective-permute-start = (f32[192,128]{1,0:T(8,128)}, f32[192,128]{1,0:T(8,128)S(1)}, u32[]{:S(2)}, u32[]{:S(2)}) collective-permute-start(f32[192,128]{1,0:T(8,128)} %shard_map.83), channel_id=1, source_target_pairs={{0,1},{1,2},{2,3},{3,4},{4,5},{5,6},{6,7},{7,8},{8,9},{9,10},{10,1... | collective-permute-start | bytes 294920 | tf_op jit(solution)/shard_map/ppermute | solution.py:613
  4.4 9.2 %shard_map.82 = bf16[128,264,128]{2,1,0:T(8,128)(2,1)} custom-call(s32[4,48]{1,0:T(4,128)} %bitcast.22, s32[4,48]{1,0:T(4,128)} %bitcast.23, bf16[48,128,256]{2,1,0:T(8,128)(2,1)} %flux_hbm.1, bf16[48,4,256,128]{3,2,1,0:T(8,128)(2,1)} %weight_hbm.1), custom_call_target="tpu_custom_call" | custom-call | tf_op jit(solution)/shard_map/pallas_call | solution.py:104
  13.6 0.0 copy-start.1
  13.6 0.0 copy-start.2
  13.6 0.0 copy-start.3
  13.6 0.0 copy-start.4
  13.7 0.0 collective-permute-done.1.right_ref
  13.7 0.0 collective-permute-done.left_ref
  13.7 13.5 %all-to-all-start = ((bf16[128,264,128]{2,1,0:T(8,128)(2,1)}), bf16[128,264,128]{2,1,0:T(8,128)(2,1)}, u32[]{:S(2)}, u32[]{:S(2)}) async-start(bf16[128,264,128]{2,1,0:T(8,128)(2,1)} %shard_map.82), calls=%async_computation | async-start | bytes 17301504 | tf_op jit(solution)/shard_map/all_to_all | solution.py:642
  27.2 0.0 copy-done.1
  27.2 0.0 copy-done.2
  27.2 0.3 shard_map.84
  27.5 0.2 collective-permute-start.3
  27.7 2.3 %collective-permute-start.2 = (f32[672,128]{1,0:T(8,128)S(1)}, f32[672,128]{1,0:T(8,128)S(1)}, u32[]{:S(2)}, u32[]{:S(2)}) collective-permute-start(f32[672,128]{1,0:T(8,128)S(1)} %get-tuple-element.16), channel_id=1, source_target_pairs={{16,32},{48,64},{80,96},{32,16},{64,48},{96,80},{17,33},{49,65},{8... | collective-permute-start | bytes 1032200 | tf_op jit(solution)/shard_map/ppermute | solution.py:623
  30.0 0.0 copy-done.3
  30.0 0.0 copy-done.4
  30.0 29.2 %shard_map.85 = (f32[2048,128]{1,0:T(8,128)S(1)}, f32[8,3,8,128]{3,2,1,0:T(8,128)S(1)}, f32[16,16,7,8,128]{4,3,2,1,0:T(8,128)S(1)}) custom-call(f32[2048,128]{1,0:T(8,128)S(1)} %bitcast.10, f32[384,128]{1,0:T(8,128)S(1)} %bitcast.15, f32[192,128]{1,0:T(8,128)S(1)} %collective-permute-done.left_ref, f32[192,128]{1,0:T(8,128)S(1)} %collective-permute-done.1.right_ref, ...), custom_call_target="tpu_custom_call" | custom-call | tf_op jit(solution)/shard_map/pallas_call | solution.py:431
  59.2 0.0 copy-start
  59.2 2.9 %copy-done = f32[16,16,7,8,128]{4,3,2,1,0:T(8,128)} copy-done((f32[16,16,7,8,128]{4,3,2,1,0:T(8,128)}, f32[16,16,7,8,128]{4,3,2,1,0:T(8,128)S(1)}, u32[]{:S(2)}) %copy-start) | copy-done | bytes 7340056
  62.1 0.0 copy-start.5
  62.1 1.0 copy-done.5
  63.0 0.0 copy-start.6
  63.0 0.6 copy-done.6
  63.7 0.0 collective-permute-done.3.halo_ref
  63.7 0.0 copy-start.8
  63.7 0.8 copy-done.8
  64.5 10.0 %shard_map.86.inner_hbm = f32[2048,128]{1,0:T(8,128)} custom-call(s32[1]{0:T(128)S(6)} %sub.3.side_ref, f32[672,128]{1,0:T(8,128)} %copy-done.8, f32[8,3,8,128]{3,2,1,0:T(8,128)} %copy-done.6, f32[384,128]{1,0:T(8,128)} %bitcast.12, s32[384,128]{1,0:T(8,128)} %bitcast.16, s32[384,128]{1,0:T(8,128)} %bitcast.19, f32[16,16,7,8,128]{4,3,2,1,0:T(8,128)} %copy-done, ...), custom_call_target="tpu_custom_call" | custom-call | tf_op jit(solution)/shard_map/pallas_call | solution.py:518
  74.4 43.0 %collective-permute-done.2.halo_ref = f32[672,128]{1,0:T(8,128)S(1)} collective-permute-done((f32[672,128]{1,0:T(8,128)S(1)}, f32[672,128]{1,0:T(8,128)S(1)}, u32[]{:S(2)}, u32[]{:S(2)}) %collective-permute-start.2) | collective-permute-done | bytes 344096 | tf_op jit(solution)/shard_map/ppermute | solution.py:623
  117.5 0.0 copy-start.7
  117.5 0.7 copy-done.7
  118.2 10.1 %shard_map.87.moved_hbm = f32[2048,128]{1,0:T(8,128)} custom-call(s32[1]{0:T(128)} %bitcast.4.odd_ref.side_ref, f32[672,128]{1,0:T(8,128)} %copy-done.7, f32[8,3,8,128]{3,2,1,0:T(8,128)} %copy-done.6, f32[384,128]{1,0:T(8,128)} %bitcast.13, s32[384,128]{1,0:T(8,128)} %bitcast.17, s32[384,128]{1,0:T(8,128)} %bitcast.20, f32[16,16,7,8,128]{4,3,2,1,0:T(8,128)} %copy-done, ...), custom_call_target="tpu_custom_call" | custom-call | tf_op jit(solution)/shard_map/pallas_call | solution.py:518
  128.3 9.4 %all-to-all-done.arrived_hbm = bf16[128,264,128]{2,1,0:T(8,128)(2,1)} async-done(((bf16[128,264,128]{2,1,0:T(8,128)(2,1)}), bf16[128,264,128]{2,1,0:T(8,128)(2,1)}, u32[]{:S(2)}, u32[]{:S(2)}) %all-to-all-start) | async-done | bytes 8650784 | tf_op jit(solution)/shard_map/all_to_all | solution.py:642
  137.7 5.2 %shard_map.88 = f32[2048,128]{1,0:T(8,128)} custom-call(bf16[128,264,128]{2,1,0:T(8,128)(2,1)} %all-to-all-done.arrived_hbm, f32[2048,128]{1,0:T(8,128)} %shard_map.87.moved_hbm), custom_call_target="tpu_custom_call" | custom-call | tf_op jit(solution)/shard_map/pallas_call | solution.py:591
Async XLA Ops:
  2.3 11.4 %collective-permute-start.1 = (f32[192,128]{1,0:T(8,128)}, f32[192,128]{1,0:T(8,128)S(1)}, u32[]{:S(2)}, u32[]{:S(2)}) collective-permute-start(f32[192,128]{1,0:T(8,128)} %shard_map.83), channel_id=1, source_target_pairs={{1,0},{2,1},{3,2},{4,3},{5,4},{6,5},{7,6},{8,7},{9,8},{10,9},{11,1... | collective-permute-start | bytes 294920 | tf_op jit(solution)/shard_map/ppermute | solution.py:613
  2.9 10.8 %collective-permute-start = (f32[192,128]{1,0:T(8,128)}, f32[192,128]{1,0:T(8,128)S(1)}, u32[]{:S(2)}, u32[]{:S(2)}) collective-permute-start(f32[192,128]{1,0:T(8,128)} %shard_map.83), channel_id=1, source_target_pairs={{0,1},{1,2},{2,3},{3,4},{4,5},{5,6},{6,7},{7,8},{8,9},{9,10},{10,1... | collective-permute-start | bytes 294920 | tf_op jit(solution)/shard_map/ppermute | solution.py:613
  13.6 13.6 %copy-start.1 = (f32[16,8,16,128]{3,2,1,0:T(8,128)S(1)}, f32[16,8,16,128]{3,2,1,0:T(8,128)}, u32[]{:S(2)}) copy-start(f32[16,8,16,128]{3,2,1,0:T(8,128)} %param.8) | copy-start | bytes 3145732
  13.6 13.6 %copy-start.2 = (f32[3,8,16,128]{3,2,1,0:T(8,128)S(1)}, f32[3,8,16,128]{3,2,1,0:T(8,128)}, u32[]{:S(2)}) copy-start(f32[3,8,16,128]{3,2,1,0:T(8,128)} %param.9) | copy-start | bytes 589828
  13.6 16.4 %copy-start.3 = (s32[3,8,16,128]{3,2,1,0:T(8,128)S(1)}, s32[3,8,16,128]{3,2,1,0:T(8,128)}, u32[]{:S(2)}) copy-start(s32[3,8,16,128]{3,2,1,0:T(8,128)} %param.10) | copy-start | bytes 589828
  13.6 16.4 %copy-start.4 = (s32[3,8,16,128]{3,2,1,0:T(8,128)S(1)}, s32[3,8,16,128]{3,2,1,0:T(8,128)}, u32[]{:S(2)}) copy-start(s32[3,8,16,128]{3,2,1,0:T(8,128)} %param.11) | copy-start | bytes 589828
  13.7 124.0 %all-to-all-start = ((bf16[128,264,128]{2,1,0:T(8,128)(2,1)}), bf16[128,264,128]{2,1,0:T(8,128)(2,1)}, u32[]{:S(2)}, u32[]{:S(2)}) async-start(bf16[128,264,128]{2,1,0:T(8,128)(2,1)} %shard_map.82), calls=%async_computation | async-start | bytes 17301504 | tf_op jit(solution)/shard_map/all_to_all | solution.py:642
  27.5 36.2 %collective-permute-start.3 = (f32[672,128]{1,0:T(8,128)S(1)}, f32[672,128]{1,0:T(8,128)S(1)}, u32[]{:S(2)}, u32[]{:S(2)}) collective-permute-start(f32[672,128]{1,0:T(8,128)S(1)} %get-tuple-element.19), channel_id=1, source_target_pairs={{0,16},{32,48},{64,80},{96,112},{16,0},{48,32},{80,64},{112,96},{1... | collective-permute-start | bytes 1032200 | tf_op jit(solution)/shard_map/ppermute | solution.py:623
  27.7 89.8 %collective-permute-start.2 = (f32[672,128]{1,0:T(8,128)S(1)}, f32[672,128]{1,0:T(8,128)S(1)}, u32[]{:S(2)}, u32[]{:S(2)}) collective-permute-start(f32[672,128]{1,0:T(8,128)S(1)} %get-tuple-element.16), channel_id=1, source_target_pairs={{16,32},{48,64},{80,96},{32,16},{64,48},{96,80},{17,33},{49,65},{8... | collective-permute-start | bytes 1032200 | tf_op jit(solution)/shard_map/ppermute | solution.py:623
  59.2 2.9 %copy-start = (f32[16,16,7,8,128]{4,3,2,1,0:T(8,128)}, f32[16,16,7,8,128]{4,3,2,1,0:T(8,128)S(1)}, u32[]{:S(2)}) copy-start(f32[16,16,7,8,128]{4,3,2,1,0:T(8,128)S(1)} %get-tuple-element.18.taps_hbm) | copy-start | bytes 22020100
  62.1 1.0 copy-start.5
  63.0 0.6 copy-start.6
  63.7 0.8 copy-start.8
  117.5 0.7 copy-start.7

commit v8 on v7

--- a/solution.py
+++ b/solution.py
@@ -528,7 +528,7 @@
             pltpu.VMEM((WIDE, SPREADS, LEV, COLS), jnp.float32),
             pltpu.SemaphoreType.DMA((2,)),
         ],
-        compiler_params=params(60),
+        compiler_params=params(24),
     )(side, halo, partial, winds, first, second, taps, inner)
 
 

time: 145 us -> 145 us (level)
  waiting for transfers between devices: 52.4 us -> 61.2 us
  local copies, waits for them, and re-layouts: 6.02 us -> 1 us
  Pallas kernels: 66.2 us -> 62.5 us
    ppermute x2, waiting for transfers between devices: 43 us -> 50.1 us  [swapped(): return lax.ppermute(value, 'lat', pairs + [(b, a) for a, b in pairs])]
    unnamed x18 -> x10, local copies, waits for them, and re-layouts: 6.02 us -> 1 us
    pallas_call x2, Pallas kernels: 20.1 us -> 16.3 us  [outer_advect(): pl.pallas_call(outer_kernel, in_specs=[pl.BlockSpec(memory_space=pltpu.SM...]
    all_to_all x1, waiting for transfers between devices: 9.4 us -> 11 us  [body(): lax.all_to_all(chunks, ('lat', 'lon'), split_axis=0, concat_axis=0, tiled...]
  transfers between devices with their start and end apart: 5 -> 5, of which waited for: 2 -> 2; matrix products, arithmetic and copies ran while one was open for 0% -> 0% of each run, Pallas kernels for 41% -> 38%
where the time goes in v8:
time: 145 us; the launch traced here: 143 us
  Pallas kernels  62.5 us (43%)
  waiting for transfers between devices  61.2 us (42%)
  starting transfers between devices  18 us (12%)
    ppermute x2, waiting for transfers between devices, swapped(): return lax.ppermute(value, 'lat', pairs + [(b, a) for a, b in pairs])  50.1 us
    pallas_call x1, Pallas kernels, inner_advect(): pl.pallas_call(inner_kernel, in_specs=[vmem] * 6, out_specs=[vmem, vmem,...  29.2 us
    pallas_call x2, Pallas kernels, outer_advect(): pl.pallas_call(outer_kernel, in_specs=[pl.BlockSpec(memory_space=pltpu.SM...  16.3 us
    all_to_all x1, starting transfers between devices, body(): lax.all_to_all(chunks, ('lat', 'lon'), split_axis=0, concat_axis=0, tiled...  13.4 us
    all_to_all x1, waiting for transfers between devices, body(): lax.all_to_all(chunks, ('lat', 'lon'), split_axis=0, concat_axis=0, tiled...  11 us
    pallas_call x1, Pallas kernels, remap(): pl.pallas_call(remap_kernel, in_specs=[pl.BlockSpec(memory_space=pltpu.SM...  9.24 us
    pallas_call x1, Pallas kernels, combine(): pl.pallas_call(combine_kernel, in_specs=[anywhere] * 2, out_specs=anywher...  5.22 us
  transfers between devices with their start and end apart: 5, of which 2 were waited for; matrix products, arithmetic and copies ran while one was open for 0% of the time, Pallas kernels for 38%

profile of v8, /device:TPU:36, one launch (start us, length us, event | category | flops | bytes accessed | tf_op | source)
XLA Modules:
  0.0 142.9 jit_solution(13990337392763461411)
XLA Ops:
  0.0 2.3 %shard_map.83 = f32[192,128]{1,0:T(8,128)} custom-call(f32[2048,128]{1,0:T(8,128)} %bitcast.8, f32[384,128]{1,0:T(8,128)} %bitcast.11), custom_call_target="tpu_custom_call" | custom-call | tf_op jit(solution)/shard_map/pallas_call | solution.py:174
  2.3 0.6 collective-permute-start.1
  2.9 1.5 %collective-permute-start = (f32[192,128]{1,0:T(8,128)}, f32[192,128]{1,0:T(8,128)S(1)}, u32[]{:S(2)}, u32[]{:S(2)}) collective-permute-start(f32[192,128]{1,0:T(8,128)} %shard_map.83), channel_id=1, source_target_pairs={{0,1},{1,2},{2,3},{3,4},{4,5},{5,6},{6,7},{7,8},{8,9},{9,10},{10,1... | collective-permute-start | bytes 294920 | tf_op jit(solution)/shard_map/ppermute | solution.py:613
  4.4 9.2 %shard_map.82 = bf16[128,264,128]{2,1,0:T(8,128)(2,1)} custom-call(s32[4,48]{1,0:T(4,128)} %bitcast.22, s32[4,48]{1,0:T(4,128)} %bitcast.23, bf16[48,128,256]{2,1,0:T(8,128)(2,1)} %flux_hbm.1, bf16[48,4,256,128]{3,2,1,0:T(8,128)(2,1)} %weight_hbm.1), custom_call_target="tpu_custom_call" | custom-call | tf_op jit(solution)/shard_map/pallas_call | solution.py:104
  13.6 0.0 copy-start
  13.6 0.0 copy-start.1
  13.7 0.0 copy-start.3
  13.7 0.0 copy-start.4
  13.7 0.0 collective-permute-done.1.right_ref
  13.7 0.0 collective-permute-done.left_ref
  13.7 13.4 %all-to-all-start = ((bf16[128,264,128]{2,1,0:T(8,128)(2,1)}), bf16[128,264,128]{2,1,0:T(8,128)(2,1)}, u32[]{:S(2)}, u32[]{:S(2)}) async-start(bf16[128,264,128]{2,1,0:T(8,128)(2,1)} %shard_map.82), calls=%async_computation | async-start | bytes 17301504 | tf_op jit(solution)/shard_map/all_to_all | solution.py:642
  27.2 0.0 copy-done
  27.2 0.0 copy-done.1
  27.2 0.3 shard_map.84
  27.5 0.2 collective-permute-start.3
  27.7 2.3 %collective-permute-start.2 = (f32[672,128]{1,0:T(8,128)S(1)}, f32[672,128]{1,0:T(8,128)S(1)}, u32[]{:S(2)}, u32[]{:S(2)}) collective-permute-start(f32[672,128]{1,0:T(8,128)S(1)} %get-tuple-element.16), channel_id=1, source_target_pairs={{16,32},{48,64},{80,96},{32,16},{64,48},{96,80},{17,33},{49,65},{8... | collective-permute-start | bytes 1032200 | tf_op jit(solution)/shard_map/ppermute | solution.py:623
  30.0 0.0 copy-done.3
  30.0 0.0 copy-done.4
  30.0 29.2 %shard_map.85 = (f32[2048,128]{1,0:T(8,128)S(1)}, f32[8,3,8,128]{3,2,1,0:T(8,128)S(1)}, f32[16,16,7,8,128]{4,3,2,1,0:T(8,128)S(1)}) custom-call(f32[2048,128]{1,0:T(8,128)S(1)} %bitcast.10, f32[384,128]{1,0:T(8,128)S(1)} %bitcast.13, f32[192,128]{1,0:T(8,128)S(1)} %collective-permute-done.left_ref, f32[192,128]{1,0:T(8,128)S(1)} %collective-permute-done.1.right_ref, ...), custom_call_target="tpu_custom_call" | custom-call | tf_op jit(solution)/shard_map/pallas_call | solution.py:431
  59.2 0.0 collective-permute-done.3.halo_ref
  59.2 8.1 %shard_map.86.inner_hbm = f32[2048,128]{1,0:T(8,128)S(1)} custom-call(s32[1]{0:T(128)S(6)} %sub.3.side_ref, f32[672,128]{1,0:T(8,128)S(1)} %collective-permute-done.3.halo_ref, f32[8,3,8,128]{3,2,1,0:T(8,128)S(1)} %get-tuple-element.17.partial_ref, f32[384,128]{1,0:T(8,128)S(1)} %bitcast.14, s32[384,128]{1,0:T(8,128)S(1)} %bitcast.17, ...), custom_call_target="tpu_custom_call" | custom-call | tf_op jit(solution)/shard_map/pallas_call | solution.py:518
  67.3 50.1 %collective-permute-done.2.halo_ref = f32[672,128]{1,0:T(8,128)S(1)} collective-permute-done((f32[672,128]{1,0:T(8,128)S(1)}, f32[672,128]{1,0:T(8,128)S(1)}, u32[]{:S(2)}, u32[]{:S(2)}) %collective-permute-start.2) | collective-permute-done | bytes 344096 | tf_op jit(solution)/shard_map/ppermute | solution.py:623
  117.4 8.2 %shard_map.87.moved_hbm = f32[2048,128]{1,0:T(8,128)S(1)} custom-call(s32[1]{0:T(128)} %bitcast.4.odd_ref.side_ref, f32[672,128]{1,0:T(8,128)S(1)} %collective-permute-done.2.halo_ref, f32[8,3,8,128]{3,2,1,0:T(8,128)S(1)} %get-tuple-element.17.partial_ref, f32[384,128]{1,0:T(8,128)S(1)} %bitcast.15, s32[384,128]{1,0:T(8,128)S(1)} %bitcast.18, ...), custom_call_target="tpu_custom_call" | custom-call | tf_op jit(solution)/shard_map/pallas_call | solution.py:518
  125.6 0.0 copy-start.2
  125.7 1.0 copy-done.2
  126.6 11.0 %all-to-all-done.arrived_hbm = bf16[128,264,128]{2,1,0:T(8,128)(2,1)} async-done(((bf16[128,264,128]{2,1,0:T(8,128)(2,1)}), bf16[128,264,128]{2,1,0:T(8,128)(2,1)}, u32[]{:S(2)}, u32[]{:S(2)}) %all-to-all-start) | async-done | bytes 8650784 | tf_op jit(solution)/shard_map/all_to_all | solution.py:642
  137.7 5.2 %shard_map.88 = f32[2048,128]{1,0:T(8,128)} custom-call(bf16[128,264,128]{2,1,0:T(8,128)(2,1)} %all-to-all-done.arrived_hbm, f32[2048,128]{1,0:T(8,128)} %copy-done.2), custom_call_target="tpu_custom_call" | custom-call | tf_op jit(solution)/shard_map/pallas_call | solution.py:591
Async XLA Ops:
  2.3 11.4 %collective-permute-start.1 = (f32[192,128]{1,0:T(8,128)}, f32[192,128]{1,0:T(8,128)S(1)}, u32[]{:S(2)}, u32[]{:S(2)}) collective-permute-start(f32[192,128]{1,0:T(8,128)} %shard_map.83), channel_id=1, source_target_pairs={{1,0},{2,1},{3,2},{4,3},{5,4},{6,5},{7,6},{8,7},{9,8},{10,9},{11,1... | collective-permute-start | bytes 294920 | tf_op jit(solution)/shard_map/ppermute | solution.py:613
  2.9 10.8 %collective-permute-start = (f32[192,128]{1,0:T(8,128)}, f32[192,128]{1,0:T(8,128)S(1)}, u32[]{:S(2)}, u32[]{:S(2)}) collective-permute-start(f32[192,128]{1,0:T(8,128)} %shard_map.83), channel_id=1, source_target_pairs={{0,1},{1,2},{2,3},{3,4},{4,5},{5,6},{6,7},{7,8},{8,9},{9,10},{10,1... | collective-permute-start | bytes 294920 | tf_op jit(solution)/shard_map/ppermute | solution.py:613
  13.6 13.5 %copy-start = (f32[16,8,16,128]{3,2,1,0:T(8,128)S(1)}, f32[16,8,16,128]{3,2,1,0:T(8,128)}, u32[]{:S(2)}) copy-start(f32[16,8,16,128]{3,2,1,0:T(8,128)} %param.8) | copy-start | bytes 3145732
  13.6 13.5 %copy-start.1 = (f32[3,8,16,128]{3,2,1,0:T(8,128)S(1)}, f32[3,8,16,128]{3,2,1,0:T(8,128)}, u32[]{:S(2)}) copy-start(f32[3,8,16,128]{3,2,1,0:T(8,128)} %param.9) | copy-start | bytes 589828
  13.7 16.3 %copy-start.3 = (s32[3,8,16,128]{3,2,1,0:T(8,128)S(1)}, s32[3,8,16,128]{3,2,1,0:T(8,128)}, u32[]{:S(2)}) copy-start(s32[3,8,16,128]{3,2,1,0:T(8,128)} %param.10) | copy-start | bytes 589828
  13.7 16.3 %copy-start.4 = (s32[3,8,16,128]{3,2,1,0:T(8,128)S(1)}, s32[3,8,16,128]{3,2,1,0:T(8,128)}, u32[]{:S(2)}) copy-start(s32[3,8,16,128]{3,2,1,0:T(8,128)} %param.11) | copy-start | bytes 589828
  13.7 124.0 %all-to-all-start = ((bf16[128,264,128]{2,1,0:T(8,128)(2,1)}), bf16[128,264,128]{2,1,0:T(8,128)(2,1)}, u32[]{:S(2)}, u32[]{:S(2)}) async-start(bf16[128,264,128]{2,1,0:T(8,128)(2,1)} %shard_map.82), calls=%async_computation | async-start | bytes 17301504 | tf_op jit(solution)/shard_map/all_to_all | solution.py:642
  27.5 31.7 %collective-permute-start.3 = (f32[672,128]{1,0:T(8,128)S(1)}, f32[672,128]{1,0:T(8,128)S(1)}, u32[]{:S(2)}, u32[]{:S(2)}) collective-permute-start(f32[672,128]{1,0:T(8,128)S(1)} %get-tuple-element.19), channel_id=1, source_target_pairs={{0,16},{32,48},{64,80},{96,112},{16,0},{48,32},{80,64},{112,96},{1... | collective-permute-start | bytes 1032200 | tf_op jit(solution)/shard_map/ppermute | solution.py:623
  27.7 89.8 %collective-permute-start.2 = (f32[672,128]{1,0:T(8,128)S(1)}, f32[672,128]{1,0:T(8,128)S(1)}, u32[]{:S(2)}, u32[]{:S(2)}) collective-permute-start(f32[672,128]{1,0:T(8,128)S(1)} %get-tuple-element.16), channel_id=1, source_target_pairs={{16,32},{48,64},{80,96},{32,16},{64,48},{96,80},{17,33},{49,65},{8... | collective-permute-start | bytes 1032200 | tf_op jit(solution)/shard_map/ppermute | solution.py:623
  125.6 1.0 copy-start.2
